TPU v7x, 8 devices: a whole 2x2x1 slice. The times are simulated.
8 devices in a mesh: batch: 1 (over z), row: 2 (over y), col: 4 (over x, core).
Axes of the slice: x: 2, y: 2, z: 1, core: 2. Of those that a mesh axis runs over, the one named last changes fastest.
Arguments:
- tri_mat: bfloat16 [3072, 3072], P(('batch', 'row'), 'col')
- rhs_mat: bfloat16 [3072, 32768], P(('batch', 'row'), 'col')
Outputs:
- output: bfloat16 [3072, 32768], P(('batch', 'row'), 'col')
All inputs are finite; a program needn't handle non-finite values.
Results may differ from a plain program's by a relative error of at most 0.001.
Values are sent between devices in bfloat16 or wider.
A program may use at most 1 GiB of HBM per device.

v0:
```python
import functools

import jax
import jax.numpy as jnp
from jax import lax
from jax.experimental import pallas as pl
from jax.experimental.pallas import tpu as pltpu
from jax.sharding import PartitionSpec as P


BLOCK = 256


def block_kernel(count, *refs):
    lo_ref, lr_ref, bo_ref = refs[:3]
    rem_refs = refs[3:3 + count]
    out_ref = refs[-1]
    acc = jnp.dot(lo_ref[...], bo_ref[...], preferred_element_type=jnp.float32)
    for j in range(count):
        acc += jnp.dot(lr_ref[:, j * BLOCK:(j + 1) * BLOCK], rem_refs[j][...], preferred_element_type=jnp.float32)
    out_ref[...] = acc.astype(out_ref.dtype)


def row_block(step, count, start, tile, l_own, l_rem, b_own, pieces, x, partial=False):
    depth = (step + 1) * BLOCK
    rows, cols = b_own.shape
    width = pieces[0].shape[1]
    base = start // tile
    in_specs = [
        pl.BlockSpec((BLOCK, depth), lambda n: (step, 0)),
        pl.BlockSpec((BLOCK, count * BLOCK), lambda n: (step, 0)),
        pl.BlockSpec((depth, tile), lambda n: (0, base + n)),
    ]
    in_specs += [pl.BlockSpec((BLOCK, tile), lambda n: (0, n))] * count
    args = [l_own, l_rem, b_own, *pieces[:count]]
    aliases = {}
    if partial:
        out_spec = pl.BlockSpec((BLOCK, tile), lambda n: (0, n))
        out_shape = jax.ShapeDtypeStruct((BLOCK, width), jnp.float32)
    else:
        out_spec = pl.BlockSpec((BLOCK, tile), lambda n: (step, base + n))
        out_shape = jax.ShapeDtypeStruct((rows, cols), jnp.bfloat16)
        if x is not None:
            aliases = {len(args): 0}
            args.append(x)
            in_specs.append(pl.BlockSpec(memory_space=pl.ANY))
    return pl.pallas_call(
        functools.partial(block_kernel, count),
        grid=(width // tile,),
        in_specs=in_specs,
        out_specs=out_spec,
        out_shape=out_shape,
        input_output_aliases=aliases,
        compiler_params=pltpu.CompilerParams(vmem_limit_bytes=40 << 20),
        cost_estimate=pl.CostEstimate(
            flops=2 * BLOCK * (depth + count * BLOCK) * width,
            bytes_accessed=(depth + count * BLOCK + BLOCK) * width * 2, transcendentals=0),
    )(*args)


def finish_kernel(l_ref, b_ref, acc_ref, x_in, x_ref):
    del x_in
    acc = acc_ref[...] + jnp.dot(l_ref[...], b_ref[...], preferred_element_type=jnp.float32)
    x_ref[...] = acc.astype(x_ref.dtype)


def finish(step, start, tile, l_rem, piece, acc, acc_start, x):
    width = piece.shape[1]
    base, acc_base = start // tile, acc_start // tile
    return pl.pallas_call(
        finish_kernel,
        grid=(width // tile,),
        in_specs=[
            pl.BlockSpec((BLOCK, BLOCK), lambda n: (step, step)),
            pl.BlockSpec((BLOCK, tile), lambda n: (0, n)),
            pl.BlockSpec((BLOCK, tile), lambda n: (0, acc_base + n)),
            pl.BlockSpec(memory_space=pl.ANY),
        ],
        out_specs=pl.BlockSpec((BLOCK, tile), lambda n: (step, base + n)),
        out_shape=jax.ShapeDtypeStruct(x.shape, x.dtype),
        input_output_aliases={3: 0},
        compiler_params=pltpu.CompilerParams(vmem_limit_bytes=16 << 20),
        cost_estimate=pl.CostEstimate(
            flops=2 * BLOCK * BLOCK * width, bytes_accessed=BLOCK * width * 8, transcendentals=0),
    )(l_rem, piece, acc, x)


def weave(even, odd):
    count = even.shape[1] // BLOCK
    parts = []
    for j in range(count):
        parts += [even[:, j * BLOCK:(j + 1) * BLOCK], odd[:, j * BLOCK:(j + 1) * BLOCK]]
    return jnp.concatenate(parts, axis=1)


def solution(mesh):
    grid_rows = mesh.shape["row"]
    grid_cols = mesh.shape["col"]
    swap_row = [(r, r ^ 1) for r in range(grid_rows)]

    def local_trmm(tri_loc, rhs_loc):
        rows, cols = rhs_loc.shape
        steps = rows // BLOCK
        final = steps - 1
        half = cols // 2
        first = cols // 16

        order = [(final, cols - first, first)]
        order += [(j, h * half, half) for j in range(final) for h in range(2)]
        tail = [(0, half), (half, cols // 4), (half + cols // 4, cols // 8), (cols - 2 * first, first)]
        order += [(final, off, w) for off, w in tail]

        got = {}
        source = rhs_loc
        for j, off, w in order:
            piece = source[j * BLOCK:(j + 1) * BLOCK, off:off + w]
            source, piece = lax.optimization_barrier((source, piece))
            got[j, off] = lax.ppermute(piece, "row", swap_row)
        l_core, l_chip, l_both = (
            lax.ppermute(tri_loc, "col", [(c, c ^ d) for c in range(grid_cols)]) for d in (1, 2, 3))
        p = lax.axis_index("row")
        q = lax.axis_index("col")
        on_first = q < 2
        same = weave(jnp.where(on_first, tri_loc, l_chip), jnp.where(on_first, l_chip, tri_loc))
        other = weave(jnp.where(on_first, l_core, l_both), jnp.where(on_first, l_both, l_core))
        matches = (q % 2) == p
        l_own = jnp.where(matches, same, other)
        l_rem = jnp.where(matches, other, same)

        x = None
        for j in range(final):
            for h in range(2):
                x = row_block(j, j + 1, h * half, 1024, l_own, l_rem, rhs_loc, [got[k, h * half] for k in range(j + 1)], x)
        acc = [row_block(final, final, h * half, 1024, l_own, l_rem, rhs_loc, [got[k, h * half] for k in range(final)], None,
                         partial=True) for h in range(2)]
        for off, w in [(cols - first, first), *tail]:
            h = off // half
            x = finish(final, off, min(w, 1024), l_rem, got[final, off], acc[h], off - h * half, x)
        return x

    part_spec = P(("batch", "row"), "col")
    return jax.shard_map(local_trmm, mesh=mesh, in_specs=(part_spec, part_spec), out_specs=part_spec, check_vma=False)
```

profile of v0, /device:TPU:0, one launch (start us, length us, event | category | flops | bytes accessed | tf_op | source)
XLA Modules:
  0.0 551.4 jit_solution(6407289229376852846)
XLA Ops:
  10.3 3.2 slice.95
  13.5 3.2 slice.96
  26.0 3.2 slice.100
  38.6 3.2 slice.104
  49.6 5.8 %collective-permute-done.1 = bf16[1536,768]{1,0:T(8,128)(2,1)} collective-permute-done((bf16[1536,768]{1,0:T(8,128)(2,1)}, bf16[1536,768]{1,0:T(8,128)(2,1)}, u32[]{:S(2)}, u32[]{:S(2)}) %collective-permute-start.1) | collective-permute-done | bytes 2359328 | tf_op jit(solution)/shard_map/ppermute | solution.py:120
  59.9 46.2 %collective-permute-done.2 = bf16[1536,768]{1,0:T(8,128)(2,1)} collective-permute-done((bf16[1536,768]{1,0:T(8,128)(2,1)}, bf16[1536,768]{1,0:T(8,128)(2,1)}, u32[]{:S(2)}, u32[]{:S(2)}) %collective-permute-start.2) | collective-permute-done | bytes 2359328 | tf_op jit(solution)/shard_map/ppermute | solution.py:120
  114.3 32.6 %collective-permute-done.13.refs_4_ = bf16[256,4096]{1,0:T(8,128)(2,1)S(1)} collective-permute-done((bf16[256,4096]{1,0:T(8,128)(2,1)}, bf16[256,4096]{1,0:T(8,128)(2,1)S(1)}, u32[]{:S(2)}, u32[]{:S(2)}) %collective-permute-start.13) | collective-permute-done | bytes 2097184 | tf_op jit(solution)/shard_map/ppermute | solution.py:118
  150.2 41.6 %collective-permute-done.5.refs_4_ = bf16[256,4096]{1,0:T(8,128)(2,1)S(1)} collective-permute-done((bf16[256,4096]{1,0:T(8,128)(2,1)}, bf16[256,4096]{1,0:T(8,128)(2,1)S(1)}, u32[]{:S(2)}, u32[]{:S(2)}) %collective-permute-start.5) | collective-permute-done | bytes 2097184 | tf_op jit(solution)/shard_map/ppermute | solution.py:118
  195.1 4.4 broadcast_select_fusion
  199.6 7.9 %shard_map.30.refs_4_ = bf16[1536,8192]{1,0:T(8,128)(2,1)} custom-call(bf16[1536,1536]{1,0:T(8,128)(2,1)S(1)} %get-tuple-element.63.refs_0_, bf16[1536,1536]{1,0:T(8,128)(2,1)S(1)} %get-tuple-element.64.refs_1_.l_ref, bf16[1536,8192]{1,0:T(8,128)(2,1)} %refs_2_.23, bf16[256,4096]{1,0:T(8,128)(2,1)} %collective-permute-done.12.refs_3_), custom_call_target="tpu_custom_call" | custom-call | flops 1073741824 | bytes 6291456 | tf_op jit(solution)/shard_map/pallas_call | solution.py:47
  207.4 4.8 shard_map.31.refs_5_
  212.2 6.2 %shard_map.32.refs_5_ = bf16[1536,8192]{1,0:T(8,128)(2,1)} custom-call(bf16[1536,1536]{1,0:T(8,128)(2,1)S(1)} %get-tuple-element.63.refs_0_, bf16[1536,1536]{1,0:T(8,128)(2,1)S(1)} %get-tuple-element.64.refs_1_.l_ref, bf16[1536,8192]{1,0:T(8,128)(2,1)} %refs_2_.23, ...), custom_call_target="tpu_custom_call", output_to_operand_aliasing={{}: (5, {})} | custom-call | flops 2147483648 | bytes 10485760 | tf_op jit(solution)/shard_map/pallas_call | solution.py:47
  218.4 18.5 %collective-permute-done.14.refs_5_ = bf16[256,4096]{1,0:T(8,128)(2,1)} collective-permute-done((bf16[256,4096]{1,0:T(8,128)(2,1)}, bf16[256,4096]{1,0:T(8,128)(2,1)}, u32[]{:S(2)}, u32[]{:S(2)}) %collective-permute-start.14) | collective-permute-done | bytes 2097184 | tf_op jit(solution)/shard_map/ppermute | solution.py:118
  238.9 5.8 %shard_map.33.refs_6_ = bf16[1536,8192]{1,0:T(8,128)(2,1)} custom-call(bf16[1536,1536]{1,0:T(8,128)(2,1)S(1)} %get-tuple-element.63.refs_0_, bf16[1536,1536]{1,0:T(8,128)(2,1)S(1)} %get-tuple-element.64.refs_1_.l_ref, bf16[1536,8192]{1,0:T(8,128)(2,1)} %refs_2_.23, bf16[256,4096]{1,0:T(8,128)(2,1)S(1)} %copy-done.4, ...), custom_call_target="tpu_custom_call", output_to_operand_aliasing={{}: (5, {})} | custom-call | flops 2147483648 | bytes 10485760 | tf_op jit(solution)/shard_map/pallas_call | solution.py:47
  244.7 7.7 %shard_map.34.refs_6_ = bf16[1536,8192]{1,0:T(8,128)(2,1)} custom-call(bf16[1536,1536]{1,0:T(8,128)(2,1)S(1)} %get-tuple-element.63.refs_0_, bf16[1536,1536]{1,0:T(8,128)(2,1)} %copy-done, bf16[1536,8192]{1,0:T(8,128)(2,1)} %refs_2_.23, bf16[256,4096]{1,0:T(8,128)(2,1)} %collective-permute-done.12.refs_3_, ...), custom_call_target="tpu_custom_call", output_to_operand_aliasing={{}: (6, {})} | custom-call | flops 3221225472 | bytes 14680064 | tf_op jit(solution)/shard_map/pallas_call | solution.py:47
  252.3 29.4 %collective-permute-done.6.refs_5_ = bf16[256,4096]{1,0:T(8,128)(2,1)} collective-permute-done((bf16[256,4096]{1,0:T(8,128)(2,1)}, bf16[256,4096]{1,0:T(8,128)(2,1)}, u32[]{:S(2)}, u32[]{:S(2)}) %collective-permute-start.6) | collective-permute-done | bytes 2097184 | tf_op jit(solution)/shard_map/ppermute | solution.py:118
  283.8 7.4 %shard_map.35.refs_7_ = bf16[1536,8192]{1,0:T(8,128)(2,1)} custom-call(bf16[1536,1536]{1,0:T(8,128)(2,1)S(1)} %get-tuple-element.63.refs_0_, bf16[1536,1536]{1,0:T(8,128)(2,1)} %copy-done, bf16[1536,8192]{1,0:T(8,128)(2,1)} %refs_2_.23, bf16[256,4096]{1,0:T(8,128)(2,1)S(1)} %copy-done.4, ...), custom_call_target="tpu_custom_call", output_to_operand_aliasing={{}: (6, {})} | custom-call | flops 3221225472 | bytes 14680064 | tf_op jit(solution)/shard_map/pallas_call | solution.py:47
  291.2 35.5 %collective-permute-done.15.refs_6_ = bf16[256,4096]{1,0:T(8,128)(2,1)} collective-permute-done((bf16[256,4096]{1,0:T(8,128)(2,1)}, bf16[256,4096]{1,0:T(8,128)(2,1)}, u32[]{:S(2)}, u32[]{:S(2)}) %collective-permute-start.15) | collective-permute-done | bytes 2097184 | tf_op jit(solution)/shard_map/ppermute | solution.py:118
  328.8 9.2 %shard_map.36.refs_7_ = bf16[1536,8192]{1,0:T(8,128)(2,1)} custom-call(bf16[1536,1536]{1,0:T(8,128)(2,1)S(1)} %get-tuple-element.63.refs_0_, bf16[1536,1536]{1,0:T(8,128)(2,1)} %copy-done, bf16[1536,8192]{1,0:T(8,128)(2,1)} %refs_2_.23, bf16[256,4096]{1,0:T(8,128)(2,1)} %collective-permute-done.12.refs_3_, ...), custom_call_target="tpu_custom_call", output_to_operand_aliasing={{}: (7, {})} | custom-call | flops 4294967296 | bytes 18874368 | tf_op jit(solution)/shard_map/pallas_call | solution.py:47
  338.0 33.7 %collective-permute-done.7.refs_6_ = bf16[256,4096]{1,0:T(8,128)(2,1)} collective-permute-done((bf16[256,4096]{1,0:T(8,128)(2,1)}, bf16[256,4096]{1,0:T(8,128)(2,1)}, u32[]{:S(2)}, u32[]{:S(2)}) %collective-permute-start.7) | collective-permute-done | bytes 2097184 | tf_op jit(solution)/shard_map/ppermute | solution.py:118
  373.7 8.9 %shard_map.37.refs_8_ = bf16[1536,8192]{1,0:T(8,128)(2,1)} custom-call(bf16[1536,1536]{1,0:T(8,128)(2,1)S(1)} %get-tuple-element.63.refs_0_, bf16[1536,1536]{1,0:T(8,128)(2,1)} %copy-done, bf16[1536,8192]{1,0:T(8,128)(2,1)} %refs_2_.23, bf16[256,4096]{1,0:T(8,128)(2,1)S(1)} %copy-done.4, ...), custom_call_target="tpu_custom_call", output_to_operand_aliasing={{}: (7, {})} | custom-call | flops 4294967296 | bytes 18874368 | tf_op jit(solution)/shard_map/pallas_call | solution.py:47
  382.6 34.0 %collective-permute-done.8.refs_7_ = bf16[256,4096]{1,0:T(8,128)(2,1)} collective-permute-done((bf16[256,4096]{1,0:T(8,128)(2,1)}, bf16[256,4096]{1,0:T(8,128)(2,1)}, u32[]{:S(2)}, u32[]{:S(2)}) %collective-permute-start.8) | collective-permute-done | bytes 2097184 | tf_op jit(solution)/shard_map/ppermute | solution.py:118
  418.7 11.7 %shard_map.28.acc_ref = f32[256,4096]{1,0:T(8,128)} custom-call(bf16[1536,1536]{1,0:T(8,128)(2,1)} %copy-done.1, bf16[1536,1536]{1,0:T(8,128)(2,1)} %copy-done, bf16[1536,8192]{1,0:T(8,128)(2,1)} %refs_2_.23, bf16[256,4096]{1,0:T(8,128)(2,1)S(1)} %copy-done.4, bf16[256,4096]{1,0:T(8,128)(2,1)S(1)} %copy-done.11, ...), custom_call_target="tpu_custom_call" | custom-call | flops 5905580032 | bytes 25165824 | tf_op jit(solution)/shard_map/pallas_call | solution.py:47
  430.4 31.2 %collective-permute-done.16.refs_7_ = bf16[256,4096]{1,0:T(8,128)(2,1)} collective-permute-done((bf16[256,4096]{1,0:T(8,128)(2,1)}, bf16[256,4096]{1,0:T(8,128)(2,1)}, u32[]{:S(2)}, u32[]{:S(2)}) %collective-permute-start.16) | collective-permute-done | bytes 2097184 | tf_op jit(solution)/shard_map/ppermute | solution.py:118
  463.6 12.2 %shard_map.29.acc_ref = f32[256,4096]{1,0:T(8,128)} custom-call(bf16[1536,1536]{1,0:T(8,128)(2,1)} %copy-done.1, bf16[1536,1536]{1,0:T(8,128)(2,1)} %copy-done, bf16[1536,8192]{1,0:T(8,128)(2,1)} %refs_2_.23, bf16[256,4096]{1,0:T(8,128)(2,1)} %collective-permute-done.12.refs_3_, bf16[256,4096]{1,0:T(8,128)(2,1)S(1)} %copy-done.8, ...), custom_call_target="tpu_custom_call" | custom-call | flops 5905580032 | bytes 25165824 | tf_op jit(solution)/shard_map/pallas_call | solution.py:47
  475.8 11.7 %shard_map.38.refs_8_ = bf16[1536,8192]{1,0:T(8,128)(2,1)} custom-call(bf16[1536,1536]{1,0:T(8,128)(2,1)} %copy-done.1, bf16[1536,1536]{1,0:T(8,128)(2,1)} %copy-done, bf16[1536,8192]{1,0:T(8,128)(2,1)} %refs_2_.23, bf16[256,4096]{1,0:T(8,128)(2,1)} %collective-permute-done.12.refs_3_, ...), custom_call_target="tpu_custom_call", output_to_operand_aliasing={{}: (8, {})} | custom-call | flops 5368709120 | bytes 23068672 | tf_op jit(solution)/shard_map/pallas_call | solution.py:47
  487.6 10.7 %shard_map.39.x_in = bf16[1536,8192]{1,0:T(8,128)(2,1)} custom-call(bf16[1536,1536]{1,0:T(8,128)(2,1)} %copy-done.1, bf16[1536,1536]{1,0:T(8,128)(2,1)} %copy-done, bf16[1536,8192]{1,0:T(8,128)(2,1)} %refs_2_.23, bf16[256,4096]{1,0:T(8,128)(2,1)S(1)} %copy-done.5, bf16[256,4096]{1,0:T(8,128)(2,1)S(1)} %copy-done.12, ...), custom_call_target="tpu_custom_call", output_to_operand_aliasing={{}: (8, {})} | custom-call | flops 5368709120 | bytes 23068672 | tf_op jit(solution)/shard_map/pallas_call | solution.py:47
  500.4 11.7 %collective-permute-done.11.b_ref = bf16[256,4096]{1,0:T(8,128)(2,1)} collective-permute-done((bf16[256,4096]{1,0:T(8,128)(2,1)S(1)}, bf16[256,4096]{1,0:T(8,128)(2,1)}, u32[]{:S(2)}, u32[]{:S(2)}) %collective-permute-start.11) | collective-permute-done | bytes 2097184 | tf_op jit(solution)/shard_map/ppermute | solution.py:118
  512.1 4.3 shard_map.41.x_in
  516.4 18.1 %collective-permute-done.10.b_ref = bf16[256,2048]{1,0:T(8,128)(2,1)} collective-permute-done((bf16[256,2048]{1,0:T(8,128)(2,1)}, bf16[256,2048]{1,0:T(8,128)(2,1)}, u32[]{:S(2)}, u32[]{:S(2)}) %collective-permute-start.10) | collective-permute-done | bytes 1048608 | tf_op jit(solution)/shard_map/ppermute | solution.py:118
  537.1 8.7 %collective-permute-done.9.b_ref = bf16[256,1024]{1,0:T(8,128)(2,1)S(1)} collective-permute-done((bf16[256,1024]{1,0:T(8,128)(2,1)S(1)}, bf16[256,1024]{1,0:T(8,128)(2,1)S(1)}, u32[]{:S(2)}, u32[]{:S(2)}) %collective-permute-start.9) | collective-permute-done | bytes 524320 | tf_op jit(solution)/shard_map/ppermute | solution.py:118
  546.8 3.6 collective-permute-done.3.b_ref
  (95 shorter events, 75.0 us)
Async XLA Ops:
  0.0 47.6 %collective-permute-start = (bf16[1536,768]{1,0:T(8,128)(2,1)}, bf16[1536,768]{1,0:T(8,128)(2,1)}, u32[]{:S(2)}, u32[]{:S(2)}) collective-permute-start(bf16[1536,768]{1,0:T(8,128)(2,1)} %param.2), channel_id=1, source_target_pairs={{0,1},{1,0},{2,3},{3,2},{4,5},{5,4},{6,7},{7,6}} | collective-permute-start | bytes 7077896 | tf_op jit(solution)/shard_map/ppermute | solution.py:120
  0.8 54.5 %collective-permute-start.1 = (bf16[1536,768]{1,0:T(8,128)(2,1)}, bf16[1536,768]{1,0:T(8,128)(2,1)}, u32[]{:S(2)}, u32[]{:S(2)}) collective-permute-start(bf16[1536,768]{1,0:T(8,128)(2,1)} %param.2), channel_id=1, source_target_pairs={{0,3},{1,2},{2,1},{3,0},{4,7},{5,6},{6,5},{7,4}} | collective-permute-start | bytes 7077896 | tf_op jit(solution)/shard_map/ppermute | solution.py:120
  3.4 102.7 %collective-permute-start.2 = (bf16[1536,768]{1,0:T(8,128)(2,1)}, bf16[1536,768]{1,0:T(8,128)(2,1)}, u32[]{:S(2)}, u32[]{:S(2)}) collective-permute-start(bf16[1536,768]{1,0:T(8,128)(2,1)} %param.2), channel_id=1, source_target_pairs={{0,2},{1,3},{2,0},{3,1},{4,6},{5,7},{6,4},{7,5}} | collective-permute-start | bytes 7077896 | tf_op jit(solution)/shard_map/ppermute | solution.py:120
  8.2 102.0 %collective-permute-start.12 = (bf16[256,4096]{1,0:T(8,128)(2,1)}, bf16[256,4096]{1,0:T(8,128)(2,1)}, u32[]{:S(2)}, u32[]{:S(2)}) collective-permute-start(bf16[256,4096]{1,0:T(8,128)(2,1)} %slice.94), channel_id=1, source_target_pairs={{0,4},{4,0},{1,5},{5,1},{2,6},{6,2},{3,7},{7,3}} | collective-permute-start | bytes 6291464 | tf_op jit(solution)/shard_map/ppermute | solution.py:118
  13.5 97.1 %collective-permute-start.4 = (bf16[256,4096]{1,0:T(8,128)(2,1)}, bf16[256,4096]{1,0:T(8,128)(2,1)S(1)}, u32[]{:S(2)}, u32[]{:S(2)}) collective-permute-start(bf16[256,4096]{1,0:T(8,128)(2,1)} %slice.95), channel_id=1, source_target_pairs={{0,4},{4,0},{1,5},{5,1},{2,6},{6,2},{3,7},{7,3}} | collective-permute-start | bytes 6291464 | tf_op jit(solution)/shard_map/ppermute | solution.py:118
  47.6 99.3 %collective-permute-start.13 = (bf16[256,4096]{1,0:T(8,128)(2,1)}, bf16[256,4096]{1,0:T(8,128)(2,1)S(1)}, u32[]{:S(2)}, u32[]{:S(2)}) collective-permute-start(bf16[256,4096]{1,0:T(8,128)(2,1)} %slice.96), channel_id=1, source_target_pairs={{0,4},{4,0},{1,5},{5,1},{2,6},{6,2},{3,7},{7,3}} | collective-permute-start | bytes 6291464 | tf_op jit(solution)/shard_map/ppermute | solution.py:118
  55.4 136.4 %collective-permute-start.5 = (bf16[256,4096]{1,0:T(8,128)(2,1)}, bf16[256,4096]{1,0:T(8,128)(2,1)S(1)}, u32[]{:S(2)}, u32[]{:S(2)}) collective-permute-start(bf16[256,4096]{1,0:T(8,128)(2,1)} %slice.97), channel_id=1, source_target_pairs={{0,4},{4,0},{1,5},{5,1},{2,6},{6,2},{3,7},{7,3}} | collective-permute-start | bytes 6291464 | tf_op jit(solution)/shard_map/ppermute | solution.py:118
  59.6 48.2 %copy-start.16 = (bf16[1536,768]{1,0:T(8,128)(2,1)S(1)}, bf16[1536,768]{1,0:T(8,128)(2,1)}, u32[]{:S(2)}) copy-start(bf16[1536,768]{1,0:T(8,128)(2,1)} %param.2) | copy-start | bytes 7077892
  106.1 130.8 %collective-permute-start.14 = (bf16[256,4096]{1,0:T(8,128)(2,1)}, bf16[256,4096]{1,0:T(8,128)(2,1)}, u32[]{:S(2)}, u32[]{:S(2)}) collective-permute-start(bf16[256,4096]{1,0:T(8,128)(2,1)} %slice.98), channel_id=1, source_target_pairs={{0,4},{4,0},{1,5},{5,1},{2,6},{6,2},{3,7},{7,3}} | collective-permute-start | bytes 6291464 | tf_op jit(solution)/shard_map/ppermute | solution.py:118
  110.2 85.0 %copy-start.14 = (bf16[1536,1536]{1,0:T(8,128)(2,1)}, bf16[1536,1536]{1,0:T(8,128)(2,1)S(1)}, u32[]{:S(2)}) copy-start(bf16[1536,1536]{1,0:T(8,128)(2,1)S(1)} %get-tuple-element.70) | copy-start | bytes 14155780
  110.2 84.9 %copy-start.15 = (bf16[1536,1536]{1,0:T(8,128)(2,1)}, bf16[1536,1536]{1,0:T(8,128)(2,1)S(1)}, u32[]{:S(2)}) copy-start(bf16[1536,1536]{1,0:T(8,128)(2,1)S(1)} %get-tuple-element.69) | copy-start | bytes 14155780
  110.2 171.6 %collective-permute-start.6 = (bf16[256,4096]{1,0:T(8,128)(2,1)}, bf16[256,4096]{1,0:T(8,128)(2,1)}, u32[]{:S(2)}, u32[]{:S(2)}) collective-permute-start(bf16[256,4096]{1,0:T(8,128)(2,1)} %slice.99), channel_id=1, source_target_pairs={{0,4},{4,0},{1,5},{5,1},{2,6},{6,2},{3,7},{7,3}} | collective-permute-start | bytes 6291464 | tf_op jit(solution)/shard_map/ppermute | solution.py:118
  112.2 214.5 %collective-permute-start.15 = (bf16[256,4096]{1,0:T(8,128)(2,1)}, bf16[256,4096]{1,0:T(8,128)(2,1)}, u32[]{:S(2)}, u32[]{:S(2)}) collective-permute-start(bf16[256,4096]{1,0:T(8,128)(2,1)} %slice.100), channel_id=1, source_target_pairs={{0,4},{4,0},{1,5},{5,1},{2,6},{6,2},{3,7},{7,3}} | collective-permute-start | bytes 6291464 | tf_op jit(solution)/shard_map/ppermute | solution.py:118
  148.2 223.5 %collective-permute-start.7 = (bf16[256,4096]{1,0:T(8,128)(2,1)}, bf16[256,4096]{1,0:T(8,128)(2,1)}, u32[]{:S(2)}, u32[]{:S(2)}) collective-permute-start(bf16[256,4096]{1,0:T(8,128)(2,1)} %slice.101), channel_id=1, source_target_pairs={{0,4},{4,0},{1,5},{5,1},{2,6},{6,2},{3,7},{7,3}} | collective-permute-start | bytes 6291464 | tf_op jit(solution)/shard_map/ppermute | solution.py:118
  193.1 223.5 %collective-permute-start.8 = (bf16[256,4096]{1,0:T(8,128)(2,1)}, bf16[256,4096]{1,0:T(8,128)(2,1)}, u32[]{:S(2)}, u32[]{:S(2)}) collective-permute-start(bf16[256,4096]{1,0:T(8,128)(2,1)} %slice.103), channel_id=1, source_target_pairs={{0,4},{4,0},{1,5},{5,1},{2,6},{6,2},{3,7},{7,3}} | collective-permute-start | bytes 6291464 | tf_op jit(solution)/shard_map/ppermute | solution.py:118
  199.5 39.4 %copy-start = (bf16[1536,1536]{1,0:T(8,128)(2,1)}, bf16[1536,1536]{1,0:T(8,128)(2,1)S(1)}, u32[]{:S(2)}) copy-start(bf16[1536,1536]{1,0:T(8,128)(2,1)S(1)} %get-tuple-element.64.refs_1_.l_ref) | copy-start | bytes 14155780
  199.5 174.2 %copy-start.1 = (bf16[1536,1536]{1,0:T(8,128)(2,1)}, bf16[1536,1536]{1,0:T(8,128)(2,1)S(1)}, u32[]{:S(2)}) copy-start(bf16[1536,1536]{1,0:T(8,128)(2,1)S(1)} %get-tuple-element.63.refs_0_) | copy-start | bytes 14155780
  212.2 26.7 %copy-start.10 = (bf16[256,4096]{1,0:T(8,128)(2,1)S(1)}, bf16[256,4096]{1,0:T(8,128)(2,1)}, u32[]{:S(2)}) copy-start(bf16[256,4096]{1,0:T(8,128)(2,1)} %copy-done.9) | copy-start | bytes 6291460
  236.9 224.7 %collective-permute-start.16 = (bf16[256,4096]{1,0:T(8,128)(2,1)}, bf16[256,4096]{1,0:T(8,128)(2,1)}, u32[]{:S(2)}, u32[]{:S(2)}) collective-permute-start(bf16[256,4096]{1,0:T(8,128)(2,1)} %slice.102), channel_id=1, source_target_pairs={{0,4},{4,0},{1,5},{5,1},{2,6},{6,2},{3,7},{7,3}} | collective-permute-start | bytes 6291464 | tf_op jit(solution)/shard_map/ppermute | solution.py:118
  252.3 74.4 %copy-start.17 = (bf16[256,4096]{1,0:T(8,128)(2,1)S(1)}, bf16[256,4096]{1,0:T(8,128)(2,1)}, u32[]{:S(2)}) copy-start(bf16[256,4096]{1,0:T(8,128)(2,1)} %slice.104) | copy-start | bytes 6291460
  281.8 216.5 %collective-permute-start.17 = (bf16[256,512]{1,0:T(8,128)(2,1)}, bf16[256,512]{1,0:T(8,128)(2,1)}, u32[]{:S(2)}, u32[]{:S(2)}) collective-permute-start(bf16[256,512]{1,0:T(8,128)(2,1)} %slice.93), channel_id=1, source_target_pairs={{0,4},{4,0},{1,5},{5,1},{2,6},{6,2},{3,7},{7,3}} | collective-permute-start | bytes 786440 | tf_op jit(solution)/shard_map/ppermute | solution.py:118
  291.2 82.5 %copy-start.11 = (bf16[256,4096]{1,0:T(8,128)(2,1)S(1)}, bf16[256,4096]{1,0:T(8,128)(2,1)}, u32[]{:S(2)}) copy-start(bf16[256,4096]{1,0:T(8,128)(2,1)} %copy-done.9) | copy-start | bytes 6291460
  326.7 185.4 %collective-permute-start.11 = (bf16[256,4096]{1,0:T(8,128)(2,1)S(1)}, bf16[256,4096]{1,0:T(8,128)(2,1)}, u32[]{:S(2)}, u32[]{:S(2)}) collective-permute-start(bf16[256,4096]{1,0:T(8,128)(2,1)S(1)} %copy-done.17), channel_id=1, source_target_pairs={{0,4},{4,0},{1,5},{5,1},{2,6},{6,2},{3,7},{7,3}} | collective-permute-start | bytes 6291464 | tf_op jit(solution)/shard_map/ppermute | solution.py:118
  338.0 78.7 %copy-start.18 = (bf16[256,1024]{1,0:T(8,128)(2,1)S(1)}, bf16[256,1024]{1,0:T(8,128)(2,1)}, u32[]{:S(2)}) copy-start(bf16[256,1024]{1,0:T(8,128)(2,1)} %slice.106) | copy-start | bytes 1572868
  371.7 162.9 %collective-permute-start.10 = (bf16[256,2048]{1,0:T(8,128)(2,1)}, bf16[256,2048]{1,0:T(8,128)(2,1)}, u32[]{:S(2)}, u32[]{:S(2)}) collective-permute-start(bf16[256,2048]{1,0:T(8,128)(2,1)} %slice.105), channel_id=1, source_target_pairs={{0,4},{4,0},{1,5},{5,1},{2,6},{6,2},{3,7},{7,3}} | collective-permute-start | bytes 3145736 | tf_op jit(solution)/shard_map/ppermute | solution.py:118
  382.6 79.0 %copy-start.19 = (bf16[256,512]{1,0:T(8,128)(2,1)S(1)}, bf16[256,512]{1,0:T(8,128)(2,1)}, u32[]{:S(2)}) copy-start(bf16[256,512]{1,0:T(8,128)(2,1)} %slice.107) | copy-start | bytes 786436
  382.6 81.0 %copy-start.8 = (bf16[256,4096]{1,0:T(8,128)(2,1)S(1)}, bf16[256,4096]{1,0:T(8,128)(2,1)}, u32[]{:S(2)}) copy-start(bf16[256,4096]{1,0:T(8,128)(2,1)} %copy-done.6) | copy-start | bytes 6291460
  416.6 129.1 %collective-permute-start.9 = (bf16[256,1024]{1,0:T(8,128)(2,1)S(1)}, bf16[256,1024]{1,0:T(8,128)(2,1)S(1)}, u32[]{:S(2)}, u32[]{:S(2)}) collective-permute-start(bf16[256,1024]{1,0:T(8,128)(2,1)S(1)} %copy-done.18), channel_id=1, source_target_pairs={{0,4},{4,0},{1,5},{5,1},{2,6},{6,2},{3,7},{7,3}} | collective-permute-start | bytes 1572872 | tf_op jit(solution)/shard_map/ppermute | solution.py:118
  461.6 88.9 %collective-permute-start.3 = (bf16[256,512]{1,0:T(8,128)(2,1)S(1)}, bf16[256,512]{1,0:T(8,128)(2,1)S(1)}, u32[]{:S(2)}, u32[]{:S(2)}) collective-permute-start(bf16[256,512]{1,0:T(8,128)(2,1)S(1)} %copy-done.19), channel_id=1, source_target_pairs={{0,4},{4,0},{1,5},{5,1},{2,6},{6,2},{3,7},{7,3}} | collective-permute-start | bytes 786440 | tf_op jit(solution)/shard_map/ppermute | solution.py:118
  475.8 11.8 %copy-start.12 = (bf16[256,4096]{1,0:T(8,128)(2,1)S(1)}, bf16[256,4096]{1,0:T(8,128)(2,1)}, u32[]{:S(2)}) copy-start(bf16[256,4096]{1,0:T(8,128)(2,1)} %copy-done.9) | copy-start | bytes 6291460
  475.8 22.5 %slice-start = ((s8[4718592]{0:T(1024)(128)(4,1)}), s8[4194304]{0:T(1024)(128)(4,1)S(1)}, s32[]{:S(2)}) async-start(s8[4718592]{0:T(1024)(128)(4,1)} %bitcast), calls=%async_computation | async-start | bytes 8388608
  498.3 13.8 %copy-start.13 = (f32[256,4096]{1,0:T(8,128)S(1)}, f32[256,4096]{1,0:T(8,128)}, u32[]{:S(2)}) copy-start(f32[256,4096]{1,0:T(8,128)} %shard_map.29.acc_ref) | copy-start | bytes 12582916
  (8 other events, 50.2 us)
where the time goes:
time: 552 us; the launch traced here: 551 us
  waiting for transfers between devices  351 us (64%)
  Pallas kernels  115 us (21%)
  local copies, waits for them, and re-layouts  47.1 us (9%)
  starting transfers between devices  29.3 us (5%)
  other arithmetic  9.05 us (2%)
    ppermute x15, waiting for transfers between devices, local_trmm(): got[j, off] = lax.ppermute(piece, 'row', swap_row)  299 us
    pallas_call x12, Pallas kernels, row_block(): pl.pallas_call(functools.partial(block_kernel, count), grid=(width // til...  104 us
    ppermute x3, waiting for transfers between devices, local_trmm(): lax.ppermute(tri_loc, 'col', [(c, c ^ d) for c in range(grid_cols)])  52 us
    slice x15, local copies, waits for them, and re-layouts, local_trmm(): piece = source[j * BLOCK:(j + 1) * BLOCK, off:off + w]  42.1 us
    ppermute x15, starting transfers between devices, local_trmm(): got[j, off] = lax.ppermute(piece, 'row', swap_row)  25.9 us
  transfers between devices with their start and end apart: 18, of which 14 were waited for; matrix products, arithmetic and copies ran while one was open for 9% of the time, Pallas kernels for 21%

commit v1 on v0

--- a/solution.py
+++ b/solution.py
@@ -11,14 +11,15 @@
 BLOCK = 256
 
 
-def block_kernel(count, *refs):
+def block_kernel(count, aliased, *refs):
     lo_ref, lr_ref, bo_ref = refs[:3]
     rem_refs = refs[3:3 + count]
-    out_ref = refs[-1]
+    out_refs = refs[3 + count + aliased:]
     acc = jnp.dot(lo_ref[...], bo_ref[...], preferred_element_type=jnp.float32)
     for j in range(count):
         acc += jnp.dot(lr_ref[:, j * BLOCK:(j + 1) * BLOCK], rem_refs[j][...], preferred_element_type=jnp.float32)
-    out_ref[...] = acc.astype(out_ref.dtype)
+    for out_ref in out_refs:
+        out_ref[...] = acc.astype(out_ref.dtype)
 
 
 def row_block(step, count, start, tile, l_own, l_rem, b_own, pieces, x, partial=False):
@@ -33,22 +34,21 @@
     ]
     in_specs += [pl.BlockSpec((BLOCK, tile), lambda n: (0, n))] * count
     args = [l_own, l_rem, b_own, *pieces[:count]]
+    out_specs = [pl.BlockSpec((BLOCK, tile), lambda n: (step, base + n))]
+    out_shape = [jax.ShapeDtypeStruct((rows, cols), jnp.bfloat16)]
     aliases = {}
+    if x is not None:
+        aliases = {len(args): 0}
+        args.append(x)
+        in_specs.append(pl.BlockSpec(memory_space=pltpu.HBM))
     if partial:
-        out_spec = pl.BlockSpec((BLOCK, tile), lambda n: (0, n))
-        out_shape = jax.ShapeDtypeStruct((BLOCK, width), jnp.float32)
-    else:
-        out_spec = pl.BlockSpec((BLOCK, tile), lambda n: (step, base + n))
-        out_shape = jax.ShapeDtypeStruct((rows, cols), jnp.bfloat16)
-        if x is not None:
-            aliases = {len(args): 0}
-            args.append(x)
-            in_specs.append(pl.BlockSpec(memory_space=pl.ANY))
+        out_specs.append(pl.BlockSpec((BLOCK, tile), lambda n: (0, n)))
+        out_shape.append(jax.ShapeDtypeStruct((BLOCK, width), jnp.float32))
     return pl.pallas_call(
-        functools.partial(block_kernel, count),
+        functools.partial(block_kernel, count, len(aliases)),
         grid=(width // tile,),
         in_specs=in_specs,
-        out_specs=out_spec,
+        out_specs=out_specs,
         out_shape=out_shape,
         input_output_aliases=aliases,
         compiler_params=pltpu.CompilerParams(vmem_limit_bytes=40 << 20),
@@ -58,26 +58,47 @@
     )(*args)
 
 
-def finish_kernel(l_ref, b_ref, acc_ref, x_in, x_ref):
+def finish_kernel(step, start, row, tile, acc_start, l_ref, b_ref, acc_ref, x_in, x_ref, l_buf, b_buf, acc_buf, out_buf, sems):
     del x_in
-    acc = acc_ref[...] + jnp.dot(l_ref[...], b_ref[...], preferred_element_type=jnp.float32)
-    x_ref[...] = acc.astype(x_ref.dtype)
+    rows = pl.ds(step * BLOCK, BLOCK)
+
+    @pl.when(lax.axis_index("row") == row)
+    def _():
+        l_copy = pltpu.make_async_copy(l_ref.at[rows, rows], l_buf, sems.at[0])
+        b_copy = pltpu.make_async_copy(b_ref, b_buf, sems.at[1])
+        acc_copy = pltpu.make_async_copy(acc_ref.at[:, pl.ds(acc_start, b_ref.shape[1])], acc_buf, sems.at[2])
+        l_copy.start()
+        b_copy.start()
+        acc_copy.start()
+        l_copy.wait()
+        b_copy.wait()
+        acc_copy.wait()
+
+        @pl.loop(0, b_ref.shape[1] // tile)
+        def _(n):
+            columns = pl.ds(pl.multiple_of(n * tile, tile), tile)
+            acc = acc_buf[:, columns] + jnp.dot(l_buf[...], b_buf[:, columns], preferred_element_type=jnp.float32)
+            out_buf[:, columns] = acc.astype(out_buf.dtype)
+
+        out_copy = pltpu.make_async_copy(out_buf, x_ref.at[rows, pl.ds(start, b_ref.shape[1])], sems.at[3])
+        out_copy.start()
+        out_copy.wait()
 
 
-def finish(step, start, tile, l_rem, piece, acc, acc_start, x):
+def finish(step, start, row, l_rem, piece, acc, acc_start, x):
     width = piece.shape[1]
-    base, acc_base = start // tile, acc_start // tile
     return pl.pallas_call(
-        finish_kernel,
-        grid=(width // tile,),
-        in_specs=[
-            pl.BlockSpec((BLOCK, BLOCK), lambda n: (step, step)),
-            pl.BlockSpec((BLOCK, tile), lambda n: (0, n)),
-            pl.BlockSpec((BLOCK, tile), lambda n: (0, acc_base + n)),
-            pl.BlockSpec(memory_space=pl.ANY),
+        functools.partial(finish_kernel, step, start, row, min(width, 512), acc_start),
+        in_specs=[pl.BlockSpec(memory_space=pltpu.HBM)] * 4,
+        out_specs=pl.BlockSpec(memory_space=pltpu.HBM),
+        out_shape=jax.ShapeDtypeStruct(x.shape, x.dtype),
+        scratch_shapes=[
+            pltpu.VMEM((BLOCK, BLOCK), l_rem.dtype),
+            pltpu.VMEM((BLOCK, width), piece.dtype),
+            pltpu.VMEM((BLOCK, width), acc.dtype),
+            pltpu.VMEM((BLOCK, width), x.dtype),
+            pltpu.SemaphoreType.DMA((4,)),
         ],
-        out_specs=pl.BlockSpec((BLOCK, tile), lambda n: (step, base + n)),
-        out_shape=jax.ShapeDtypeStruct(x.shape, x.dtype),
         input_output_aliases={3: 0},
         compiler_params=pltpu.CompilerParams(vmem_limit_bytes=16 << 20),
         cost_estimate=pl.CostEstimate(
@@ -130,12 +151,14 @@
         x = None
         for j in range(final):
             for h in range(2):
-                x = row_block(j, j + 1, h * half, 1024, l_own, l_rem, rhs_loc, [got[k, h * half] for k in range(j + 1)], x)
-        acc = [row_block(final, final, h * half, 1024, l_own, l_rem, rhs_loc, [got[k, h * half] for k in range(final)], None,
-                         partial=True) for h in range(2)]
+                x, = row_block(j, j + 1, h * half, 1024, l_own, l_rem, rhs_loc, [got[k, h * half] for k in range(j + 1)], x)
+        acc = [None, None]
+        for h in range(2):
+            x, acc[h] = row_block(
+                final, final, h * half, 1024, l_own, l_rem, rhs_loc, [got[k, h * half] for k in range(final)], x, partial=True)
         for off, w in [(cols - first, first), *tail]:
             h = off // half
-            x = finish(final, off, min(w, 1024), l_rem, got[final, off], acc[h], off - h * half, x)
+            x = finish(final, off, grid_rows - 1, l_rem, got[final, off], acc[h], off - h * half, x)
         return x
 
     part_spec = P(("batch", "row"), "col")

time: 552 us -> 552 us (level)
  Pallas kernels: 115 us -> 105 us
  waiting for transfers between devices: 351 us -> 358 us
    pallas_call x17, Pallas kernels: 115 us -> 105 us  [the longest x12 104 us: row_block(): pl.pallas_call(functools.partial(block_kernel, count, len(aliases)), grid...]
    ppermute x15, waiting for transfers between devices: 299 us -> 306 us  [local_trmm(): got[j, off] = lax.ppermute(piece, 'row', swap_row)]
  transfers between devices with their start and end apart: 18 -> 18, of which waited for: 14 -> 14; matrix products, arithmetic and copies ran while one was open for 9% -> 9% of each run, Pallas kernels for 21% -> 19%
where the time goes in v1:
time: 552 us; the launch traced here: 551 us
  waiting for transfers between devices  358 us (65%)
  Pallas kernels  105 us (19%)
  local copies, waits for them, and re-layouts  49.4 us (9%)
  starting transfers between devices  29.3 us (5%)
  other arithmetic  9.05 us (2%)
    ppermute x15, waiting for transfers between devices, local_trmm(): got[j, off] = lax.ppermute(piece, 'row', swap_row)  306 us
    pallas_call x12, Pallas kernels, row_block(): pl.pallas_call(functools.partial(block_kernel, count, len(aliases)), grid...  104 us
    ppermute x3, waiting for transfers between devices, local_trmm(): lax.ppermute(tri_loc, 'col', [(c, c ^ d) for c in range(grid_cols)])  51.7 us
    slice x15, local copies, waits for them, and re-layouts, local_trmm(): piece = source[j * BLOCK:(j + 1) * BLOCK, off:off + w]  42.3 us
    ppermute x15, starting transfers between devices, local_trmm(): got[j, off] = lax.ppermute(piece, 'row', swap_row)  25.9 us
  transfers between devices with their start and end apart: 18, of which 14 were waited for; matrix products, arithmetic and copies ran while one was open for 9% of the time, Pallas kernels for 19%

profile of v1, /device:TPU:0, one launch (start us, length us, event | category | flops | bytes accessed | tf_op | source)
XLA Modules:
  0.0 550.7 jit_solution(7493730440664847362)
XLA Ops:
  13.4 3.2 slice.96
  19.8 3.2 slice.98
  26.1 3.2 slice.100
  32.4 3.2 slice.102
  35.6 3.2 slice.103
  49.8 5.5 %collective-permute-done.1 = bf16[1536,768]{1,0:T(8,128)(2,1)} collective-permute-done((bf16[1536,768]{1,0:T(8,128)(2,1)}, bf16[1536,768]{1,0:T(8,128)(2,1)}, u32[]{:S(2)}, u32[]{:S(2)}) %collective-permute-start.1) | collective-permute-done | bytes 2359328 | tf_op jit(solution)/shard_map/ppermute | solution.py:141
  59.9 46.2 %collective-permute-done.2 = bf16[1536,768]{1,0:T(8,128)(2,1)} collective-permute-done((bf16[1536,768]{1,0:T(8,128)(2,1)}, bf16[1536,768]{1,0:T(8,128)(2,1)}, u32[]{:S(2)}, u32[]{:S(2)}) %collective-permute-start.2) | collective-permute-done | bytes 2359328 | tf_op jit(solution)/shard_map/ppermute | solution.py:141
  114.2 32.7 %collective-permute-done.10.refs_4_ = bf16[256,4096]{1,0:T(8,128)(2,1)S(1)} collective-permute-done((bf16[256,4096]{1,0:T(8,128)(2,1)}, bf16[256,4096]{1,0:T(8,128)(2,1)S(1)}, u32[]{:S(2)}, u32[]{:S(2)}) %collective-permute-start.10) | collective-permute-done | bytes 2097184 | tf_op jit(solution)/shard_map/ppermute | solution.py:139
  150.2 41.6 %collective-permute-done.5.refs_4_ = bf16[256,4096]{1,0:T(8,128)(2,1)S(1)} collective-permute-done((bf16[256,4096]{1,0:T(8,128)(2,1)}, bf16[256,4096]{1,0:T(8,128)(2,1)S(1)}, u32[]{:S(2)}, u32[]{:S(2)}) %collective-permute-start.5) | collective-permute-done | bytes 2097184 | tf_op jit(solution)/shard_map/ppermute | solution.py:139
  195.2 4.4 broadcast_select_fusion
  199.6 7.9 %shard_map.28.refs_4_ = bf16[1536,8192]{1,0:T(8,128)(2,1)} custom-call(bf16[1536,1536]{1,0:T(8,128)(2,1)S(1)} %get-tuple-element.71.refs_0_, bf16[1536,1536]{1,0:T(8,128)(2,1)S(1)} %get-tuple-element.72.refs_1_.l_ref, bf16[1536,8192]{1,0:T(8,128)(2,1)} %refs_2_.23, bf16[256,4096]{1,0:T(8,128)(2,1)} %collective-permute-done.9.refs_3_), custom_call_target="tpu_custom_call" | custom-call | flops 1073741824 | bytes 6291456 | tf_op jit(solution)/shard_map/pallas_call | solution.py:47
  207.4 4.8 shard_map.29.refs_5_
  212.2 6.2 %shard_map.30.refs_5_ = bf16[1536,8192]{1,0:T(8,128)(2,1)} custom-call(bf16[1536,1536]{1,0:T(8,128)(2,1)S(1)} %get-tuple-element.71.refs_0_, bf16[1536,1536]{1,0:T(8,128)(2,1)S(1)} %get-tuple-element.72.refs_1_.l_ref, bf16[1536,8192]{1,0:T(8,128)(2,1)} %refs_2_.23, bf16[256,4096]{1,0:T(8,128)(2,1)} %collective-permute-done.9.refs_3_, ...), custom_call_target="tpu_custom_call", output_to_operand_aliasing={{}: (5, {})} | custom-call | flops 2147483648 | bytes 10485760 | tf_op jit(solution)/shard_map/pallas_call | solution.py:47
  218.4 18.5 %collective-permute-done.11.refs_5_ = bf16[256,4096]{1,0:T(8,128)(2,1)} collective-permute-done((bf16[256,4096]{1,0:T(8,128)(2,1)}, bf16[256,4096]{1,0:T(8,128)(2,1)}, u32[]{:S(2)}, u32[]{:S(2)}) %collective-permute-start.11) | collective-permute-done | bytes 2097184 | tf_op jit(solution)/shard_map/ppermute | solution.py:139
  238.9 5.8 %shard_map.31.refs_6_ = bf16[1536,8192]{1,0:T(8,128)(2,1)} custom-call(bf16[1536,1536]{1,0:T(8,128)(2,1)S(1)} %get-tuple-element.71.refs_0_, bf16[1536,1536]{1,0:T(8,128)(2,1)S(1)} %get-tuple-element.72.refs_1_.l_ref, bf16[1536,8192]{1,0:T(8,128)(2,1)} %refs_2_.23, bf16[256,4096]{1,0:T(8,128)(2,1)S(1)} %copy-done.3, ...), custom_call_target="tpu_custom_call", output_to_operand_aliasing={{}: (5, {})} | custom-call | flops 2147483648 | bytes 10485760 | tf_op jit(solution)/shard_map/pallas_call | solution.py:47
  244.7 7.7 %shard_map.32.refs_6_ = bf16[1536,8192]{1,0:T(8,128)(2,1)} custom-call(bf16[1536,1536]{1,0:T(8,128)(2,1)S(1)} %get-tuple-element.71.refs_0_, bf16[1536,1536]{1,0:T(8,128)(2,1)} %copy-done, bf16[1536,8192]{1,0:T(8,128)(2,1)} %refs_2_.23, bf16[256,4096]{1,0:T(8,128)(2,1)} %collective-permute-done.9.refs_3_, ...), custom_call_target="tpu_custom_call", output_to_operand_aliasing={{}: (6, {})} | custom-call | flops 3221225472 | bytes 14680064 | tf_op jit(solution)/shard_map/pallas_call | solution.py:47
  252.4 29.4 %collective-permute-done.6.refs_5_ = bf16[256,4096]{1,0:T(8,128)(2,1)} collective-permute-done((bf16[256,4096]{1,0:T(8,128)(2,1)}, bf16[256,4096]{1,0:T(8,128)(2,1)}, u32[]{:S(2)}, u32[]{:S(2)}) %collective-permute-start.6) | collective-permute-done | bytes 2097184 | tf_op jit(solution)/shard_map/ppermute | solution.py:139
  283.8 7.4 %shard_map.33.refs_7_ = bf16[1536,8192]{1,0:T(8,128)(2,1)} custom-call(bf16[1536,1536]{1,0:T(8,128)(2,1)S(1)} %get-tuple-element.71.refs_0_, bf16[1536,1536]{1,0:T(8,128)(2,1)} %copy-done, bf16[1536,8192]{1,0:T(8,128)(2,1)} %refs_2_.23, bf16[256,4096]{1,0:T(8,128)(2,1)S(1)} %copy-done.3, ...), custom_call_target="tpu_custom_call", output_to_operand_aliasing={{}: (6, {})} | custom-call | flops 3221225472 | bytes 14680064 | tf_op jit(solution)/shard_map/pallas_call | solution.py:47
  291.2 35.5 %collective-permute-done.12.refs_6_ = bf16[256,4096]{1,0:T(8,128)(2,1)} collective-permute-done((bf16[256,4096]{1,0:T(8,128)(2,1)}, bf16[256,4096]{1,0:T(8,128)(2,1)}, u32[]{:S(2)}, u32[]{:S(2)}) %collective-permute-start.12) | collective-permute-done | bytes 2097184 | tf_op jit(solution)/shard_map/ppermute | solution.py:139
  328.8 9.2 %shard_map.34.refs_7_ = bf16[1536,8192]{1,0:T(8,128)(2,1)} custom-call(bf16[1536,1536]{1,0:T(8,128)(2,1)S(1)} %get-tuple-element.71.refs_0_, bf16[1536,1536]{1,0:T(8,128)(2,1)} %copy-done, bf16[1536,8192]{1,0:T(8,128)(2,1)} %refs_2_.23, bf16[256,4096]{1,0:T(8,128)(2,1)} %collective-permute-done.9.refs_3_, ...), custom_call_target="tpu_custom_call", output_to_operand_aliasing={{}: (7, {})} | custom-call | flops 4294967296 | bytes 18874368 | tf_op jit(solution)/shard_map/pallas_call | solution.py:47
  338.0 33.7 %collective-permute-done.7.refs_6_ = bf16[256,4096]{1,0:T(8,128)(2,1)} collective-permute-done((bf16[256,4096]{1,0:T(8,128)(2,1)}, bf16[256,4096]{1,0:T(8,128)(2,1)}, u32[]{:S(2)}, u32[]{:S(2)}) %collective-permute-start.7) | collective-permute-done | bytes 2097184 | tf_op jit(solution)/shard_map/ppermute | solution.py:139
  373.7 8.9 %shard_map.35.refs_8_ = bf16[1536,8192]{1,0:T(8,128)(2,1)} custom-call(bf16[1536,1536]{1,0:T(8,128)(2,1)S(1)} %get-tuple-element.71.refs_0_, bf16[1536,1536]{1,0:T(8,128)(2,1)} %copy-done, bf16[1536,8192]{1,0:T(8,128)(2,1)} %refs_2_.23, bf16[256,4096]{1,0:T(8,128)(2,1)S(1)} %copy-done.3, ...), custom_call_target="tpu_custom_call", output_to_operand_aliasing={{}: (7, {})} | custom-call | flops 4294967296 | bytes 18874368 | tf_op jit(solution)/shard_map/pallas_call | solution.py:47
  382.6 34.0 %collective-permute-done.13.refs_7_ = bf16[256,4096]{1,0:T(8,128)(2,1)} collective-permute-done((bf16[256,4096]{1,0:T(8,128)(2,1)}, bf16[256,4096]{1,0:T(8,128)(2,1)}, u32[]{:S(2)}, u32[]{:S(2)}) %collective-permute-start.13) | collective-permute-done | bytes 2097184 | tf_op jit(solution)/shard_map/ppermute | solution.py:139
  418.7 10.9 %shard_map.36.refs_8_ = bf16[1536,8192]{1,0:T(8,128)(2,1)} custom-call(bf16[1536,1536]{1,0:T(8,128)(2,1)} %copy-done.1, bf16[1536,1536]{1,0:T(8,128)(2,1)} %copy-done, bf16[1536,8192]{1,0:T(8,128)(2,1)} %refs_2_.23, bf16[256,4096]{1,0:T(8,128)(2,1)} %collective-permute-done.9.refs_3_, ...), custom_call_target="tpu_custom_call", output_to_operand_aliasing={{}: (8, {})} | custom-call | flops 5368709120 | bytes 23068672 | tf_op jit(solution)/shard_map/pallas_call | solution.py:47
  429.5 32.1 %collective-permute-done.8.refs_7_ = bf16[256,4096]{1,0:T(8,128)(2,1)} collective-permute-done((bf16[256,4096]{1,0:T(8,128)(2,1)}, bf16[256,4096]{1,0:T(8,128)(2,1)}, u32[]{:S(2)}, u32[]{:S(2)}) %collective-permute-start.8) | collective-permute-done | bytes 2097184 | tf_op jit(solution)/shard_map/ppermute | solution.py:139
  463.6 10.5 %shard_map.37.refs_8_ = bf16[1536,8192]{1,0:T(8,128)(2,1)} custom-call(bf16[1536,1536]{1,0:T(8,128)(2,1)} %copy-done.1, bf16[1536,1536]{1,0:T(8,128)(2,1)} %copy-done, bf16[1536,8192]{1,0:T(8,128)(2,1)} %refs_2_.23, bf16[256,4096]{1,0:T(8,128)(2,1)S(1)} %copy-done.4, bf16[256,4096]{1,0:T(8,128)(2,1)S(1)} %copy-done.8, ...), custom_call_target="tpu_custom_call", output_to_operand_aliasing={{}: (8, {})} | custom-call | flops 5368709120 | bytes 23068672 | tf_op jit(solution)/shard_map/pallas_call | solution.py:47
  474.2 12.9 %shard_map.38 = (bf16[1536,8192]{1,0:T(8,128)(2,1)}, f32[256,4096]{1,0:T(8,128)}) custom-call(bf16[1536,1536]{1,0:T(8,128)(2,1)} %copy-done.1, bf16[1536,1536]{1,0:T(8,128)(2,1)} %copy-done, bf16[1536,8192]{1,0:T(8,128)(2,1)} %refs_2_.23, bf16[256,4096]{1,0:T(8,128)(2,1)} %collective-permute-done.9.refs_3_, ...), custom_call_target="tpu_custom_call", output_to_operand_aliasing={{0}: (8, {})} | custom-call | flops 5905580032 | bytes 25165824 | tf_op jit(solution)/shard_map/pallas_call | solution.py:47
  487.1 12.5 %shard_map.39 = (bf16[1536,8192]{1,0:T(8,128)(2,1)}, f32[256,4096]{1,0:T(8,128)}) custom-call(bf16[1536,1536]{1,0:T(8,128)(2,1)} %copy-done.1, bf16[1536,1536]{1,0:T(8,128)(2,1)} %copy-done, bf16[1536,8192]{1,0:T(8,128)(2,1)} %refs_2_.23, bf16[256,4096]{1,0:T(8,128)(2,1)S(1)} %copy-done.4, ...), custom_call_target="tpu_custom_call", output_to_operand_aliasing={{0}: (8, {})} | custom-call | flops 5905580032 | bytes 25165824 | tf_op jit(solution)/shard_map/pallas_call | solution.py:47
  501.8 10.3 %collective-permute-done.16.b_ref = bf16[256,4096]{1,0:T(8,128)(2,1)} collective-permute-done((bf16[256,4096]{1,0:T(8,128)(2,1)}, bf16[256,4096]{1,0:T(8,128)(2,1)}, u32[]{:S(2)}, u32[]{:S(2)}) %collective-permute-start.16) | collective-permute-done | bytes 2097184 | tf_op jit(solution)/shard_map/ppermute | solution.py:139
  512.2 22.4 %collective-permute-done.15.b_ref = bf16[256,2048]{1,0:T(8,128)(2,1)} collective-permute-done((bf16[256,2048]{1,0:T(8,128)(2,1)}, bf16[256,2048]{1,0:T(8,128)(2,1)}, u32[]{:S(2)}, u32[]{:S(2)}) %collective-permute-start.15) | collective-permute-done | bytes 1048608 | tf_op jit(solution)/shard_map/ppermute | solution.py:139
  534.7 11.1 %collective-permute-done.14.b_ref = bf16[256,1024]{1,0:T(8,128)(2,1)S(1)} collective-permute-done((bf16[256,1024]{1,0:T(8,128)(2,1)S(1)}, bf16[256,1024]{1,0:T(8,128)(2,1)S(1)}, u32[]{:S(2)}, u32[]{:S(2)}) %collective-permute-start.14) | collective-permute-done | bytes 524320 | tf_op jit(solution)/shard_map/ppermute | solution.py:139
  545.8 4.7 collective-permute-done.3.b_ref
  (93 shorter events, 67.6 us)
Async XLA Ops:
  0.0 47.8 %collective-permute-start = (bf16[1536,768]{1,0:T(8,128)(2,1)}, bf16[1536,768]{1,0:T(8,128)(2,1)}, u32[]{:S(2)}, u32[]{:S(2)}) collective-permute-start(bf16[1536,768]{1,0:T(8,128)(2,1)} %param.2), channel_id=1, source_target_pairs={{0,1},{1,0},{2,3},{3,2},{4,5},{5,4},{6,7},{7,6}} | collective-permute-start | bytes 7077896 | tf_op jit(solution)/shard_map/ppermute | solution.py:141
  0.8 54.5 %collective-permute-start.1 = (bf16[1536,768]{1,0:T(8,128)(2,1)}, bf16[1536,768]{1,0:T(8,128)(2,1)}, u32[]{:S(2)}, u32[]{:S(2)}) collective-permute-start(bf16[1536,768]{1,0:T(8,128)(2,1)} %param.2), channel_id=1, source_target_pairs={{0,3},{1,2},{2,1},{3,0},{4,7},{5,6},{6,5},{7,4}} | collective-permute-start | bytes 7077896 | tf_op jit(solution)/shard_map/ppermute | solution.py:141
  3.4 102.7 %collective-permute-start.2 = (bf16[1536,768]{1,0:T(8,128)(2,1)}, bf16[1536,768]{1,0:T(8,128)(2,1)}, u32[]{:S(2)}, u32[]{:S(2)}) collective-permute-start(bf16[1536,768]{1,0:T(8,128)(2,1)} %param.2), channel_id=1, source_target_pairs={{0,2},{1,3},{2,0},{3,1},{4,6},{5,7},{6,4},{7,5}} | collective-permute-start | bytes 7077896 | tf_op jit(solution)/shard_map/ppermute | solution.py:141
  8.3 101.9 %collective-permute-start.9 = (bf16[256,4096]{1,0:T(8,128)(2,1)}, bf16[256,4096]{1,0:T(8,128)(2,1)}, u32[]{:S(2)}, u32[]{:S(2)}) collective-permute-start(bf16[256,4096]{1,0:T(8,128)(2,1)} %slice.94), channel_id=1, source_target_pairs={{0,4},{4,0},{1,5},{5,1},{2,6},{6,2},{3,7},{7,3}} | collective-permute-start | bytes 6291464 | tf_op jit(solution)/shard_map/ppermute | solution.py:139
  13.4 97.2 %collective-permute-start.4 = (bf16[256,4096]{1,0:T(8,128)(2,1)}, bf16[256,4096]{1,0:T(8,128)(2,1)S(1)}, u32[]{:S(2)}, u32[]{:S(2)}) collective-permute-start(bf16[256,4096]{1,0:T(8,128)(2,1)} %slice.95), channel_id=1, source_target_pairs={{0,4},{4,0},{1,5},{5,1},{2,6},{6,2},{3,7},{7,3}} | collective-permute-start | bytes 6291464 | tf_op jit(solution)/shard_map/ppermute | solution.py:139
  47.8 99.1 %collective-permute-start.10 = (bf16[256,4096]{1,0:T(8,128)(2,1)}, bf16[256,4096]{1,0:T(8,128)(2,1)S(1)}, u32[]{:S(2)}, u32[]{:S(2)}) collective-permute-start(bf16[256,4096]{1,0:T(8,128)(2,1)} %slice.96), channel_id=1, source_target_pairs={{0,4},{4,0},{1,5},{5,1},{2,6},{6,2},{3,7},{7,3}} | collective-permute-start | bytes 6291464 | tf_op jit(solution)/shard_map/ppermute | solution.py:139
  55.4 136.5 %collective-permute-start.5 = (bf16[256,4096]{1,0:T(8,128)(2,1)}, bf16[256,4096]{1,0:T(8,128)(2,1)S(1)}, u32[]{:S(2)}, u32[]{:S(2)}) collective-permute-start(bf16[256,4096]{1,0:T(8,128)(2,1)} %slice.97), channel_id=1, source_target_pairs={{0,4},{4,0},{1,5},{5,1},{2,6},{6,2},{3,7},{7,3}} | collective-permute-start | bytes 6291464 | tf_op jit(solution)/shard_map/ppermute | solution.py:139
  59.6 48.2 %copy-start.16 = (bf16[1536,768]{1,0:T(8,128)(2,1)S(1)}, bf16[1536,768]{1,0:T(8,128)(2,1)}, u32[]{:S(2)}) copy-start(bf16[1536,768]{1,0:T(8,128)(2,1)} %param.2) | copy-start | bytes 7077892
  106.1 130.8 %collective-permute-start.11 = (bf16[256,4096]{1,0:T(8,128)(2,1)}, bf16[256,4096]{1,0:T(8,128)(2,1)}, u32[]{:S(2)}, u32[]{:S(2)}) collective-permute-start(bf16[256,4096]{1,0:T(8,128)(2,1)} %slice.98), channel_id=1, source_target_pairs={{0,4},{4,0},{1,5},{5,1},{2,6},{6,2},{3,7},{7,3}} | collective-permute-start | bytes 6291464 | tf_op jit(solution)/shard_map/ppermute | solution.py:139
  110.2 85.0 %copy-start.14 = (bf16[1536,1536]{1,0:T(8,128)(2,1)}, bf16[1536,1536]{1,0:T(8,128)(2,1)S(1)}, u32[]{:S(2)}) copy-start(bf16[1536,1536]{1,0:T(8,128)(2,1)S(1)} %get-tuple-element.78) | copy-start | bytes 14155780
  110.2 85.0 %copy-start.15 = (bf16[1536,1536]{1,0:T(8,128)(2,1)}, bf16[1536,1536]{1,0:T(8,128)(2,1)S(1)}, u32[]{:S(2)}) copy-start(bf16[1536,1536]{1,0:T(8,128)(2,1)S(1)} %get-tuple-element.77) | copy-start | bytes 14155780
  110.2 171.6 %collective-permute-start.6 = (bf16[256,4096]{1,0:T(8,128)(2,1)}, bf16[256,4096]{1,0:T(8,128)(2,1)}, u32[]{:S(2)}, u32[]{:S(2)}) collective-permute-start(bf16[256,4096]{1,0:T(8,128)(2,1)} %slice.99), channel_id=1, source_target_pairs={{0,4},{4,0},{1,5},{5,1},{2,6},{6,2},{3,7},{7,3}} | collective-permute-start | bytes 6291464 | tf_op jit(solution)/shard_map/ppermute | solution.py:139
  112.2 214.6 %collective-permute-start.12 = (bf16[256,4096]{1,0:T(8,128)(2,1)}, bf16[256,4096]{1,0:T(8,128)(2,1)}, u32[]{:S(2)}, u32[]{:S(2)}) collective-permute-start(bf16[256,4096]{1,0:T(8,128)(2,1)} %slice.100), channel_id=1, source_target_pairs={{0,4},{4,0},{1,5},{5,1},{2,6},{6,2},{3,7},{7,3}} | collective-permute-start | bytes 6291464 | tf_op jit(solution)/shard_map/ppermute | solution.py:139
  148.2 223.5 %collective-permute-start.7 = (bf16[256,4096]{1,0:T(8,128)(2,1)}, bf16[256,4096]{1,0:T(8,128)(2,1)}, u32[]{:S(2)}, u32[]{:S(2)}) collective-permute-start(bf16[256,4096]{1,0:T(8,128)(2,1)} %slice.101), channel_id=1, source_target_pairs={{0,4},{4,0},{1,5},{5,1},{2,6},{6,2},{3,7},{7,3}} | collective-permute-start | bytes 6291464 | tf_op jit(solution)/shard_map/ppermute | solution.py:139
  193.1 223.5 %collective-permute-start.13 = (bf16[256,4096]{1,0:T(8,128)(2,1)}, bf16[256,4096]{1,0:T(8,128)(2,1)}, u32[]{:S(2)}, u32[]{:S(2)}) collective-permute-start(bf16[256,4096]{1,0:T(8,128)(2,1)} %slice.102), channel_id=1, source_target_pairs={{0,4},{4,0},{1,5},{5,1},{2,6},{6,2},{3,7},{7,3}} | collective-permute-start | bytes 6291464 | tf_op jit(solution)/shard_map/ppermute | solution.py:139
  199.6 39.4 %copy-start = (bf16[1536,1536]{1,0:T(8,128)(2,1)}, bf16[1536,1536]{1,0:T(8,128)(2,1)S(1)}, u32[]{:S(2)}) copy-start(bf16[1536,1536]{1,0:T(8,128)(2,1)S(1)} %get-tuple-element.72.refs_1_.l_ref) | copy-start | bytes 14155780
  199.6 174.2 %copy-start.1 = (bf16[1536,1536]{1,0:T(8,128)(2,1)}, bf16[1536,1536]{1,0:T(8,128)(2,1)S(1)}, u32[]{:S(2)}) copy-start(bf16[1536,1536]{1,0:T(8,128)(2,1)S(1)} %get-tuple-element.71.refs_0_) | copy-start | bytes 14155780
  212.2 26.7 %copy-start.7 = (bf16[256,4096]{1,0:T(8,128)(2,1)S(1)}, bf16[256,4096]{1,0:T(8,128)(2,1)}, u32[]{:S(2)}) copy-start(bf16[256,4096]{1,0:T(8,128)(2,1)} %copy-done.6) | copy-start | bytes 6291460
  236.9 224.7 %collective-permute-start.8 = (bf16[256,4096]{1,0:T(8,128)(2,1)}, bf16[256,4096]{1,0:T(8,128)(2,1)}, u32[]{:S(2)}, u32[]{:S(2)}) collective-permute-start(bf16[256,4096]{1,0:T(8,128)(2,1)} %slice.103), channel_id=1, source_target_pairs={{0,4},{4,0},{1,5},{5,1},{2,6},{6,2},{3,7},{7,3}} | collective-permute-start | bytes 6291464 | tf_op jit(solution)/shard_map/ppermute | solution.py:139
  252.4 76.4 %copy-start.11 = (bf16[256,4096]{1,0:T(8,128)(2,1)S(1)}, bf16[256,4096]{1,0:T(8,128)(2,1)}, u32[]{:S(2)}) copy-start(bf16[256,4096]{1,0:T(8,128)(2,1)} %copy-done.9) | copy-start | bytes 6291460
  281.8 217.8 %collective-permute-start.17 = (bf16[256,512]{1,0:T(8,128)(2,1)}, bf16[256,512]{1,0:T(8,128)(2,1)}, u32[]{:S(2)}, u32[]{:S(2)}) collective-permute-start(bf16[256,512]{1,0:T(8,128)(2,1)} %slice.93), channel_id=1, source_target_pairs={{0,4},{4,0},{1,5},{5,1},{2,6},{6,2},{3,7},{7,3}} | collective-permute-start | bytes 786440 | tf_op jit(solution)/shard_map/ppermute | solution.py:139
  326.8 185.4 %collective-permute-start.16 = (bf16[256,4096]{1,0:T(8,128)(2,1)}, bf16[256,4096]{1,0:T(8,128)(2,1)}, u32[]{:S(2)}, u32[]{:S(2)}) collective-permute-start(bf16[256,4096]{1,0:T(8,128)(2,1)} %slice.104), channel_id=1, source_target_pairs={{0,4},{4,0},{1,5},{5,1},{2,6},{6,2},{3,7},{7,3}} | collective-permute-start | bytes 6291464 | tf_op jit(solution)/shard_map/ppermute | solution.py:139
  338.0 78.7 %copy-start.17 = (bf16[256,1024]{1,0:T(8,128)(2,1)S(1)}, bf16[256,1024]{1,0:T(8,128)(2,1)}, u32[]{:S(2)}) copy-start(bf16[256,1024]{1,0:T(8,128)(2,1)} %slice.106) | copy-start | bytes 1572868
  371.7 162.9 %collective-permute-start.15 = (bf16[256,2048]{1,0:T(8,128)(2,1)}, bf16[256,2048]{1,0:T(8,128)(2,1)}, u32[]{:S(2)}, u32[]{:S(2)}) collective-permute-start(bf16[256,2048]{1,0:T(8,128)(2,1)} %slice.105), channel_id=1, source_target_pairs={{0,4},{4,0},{1,5},{5,1},{2,6},{6,2},{3,7},{7,3}} | collective-permute-start | bytes 3145736 | tf_op jit(solution)/shard_map/ppermute | solution.py:139
  382.6 79.0 %copy-start.18 = (bf16[256,512]{1,0:T(8,128)(2,1)S(1)}, bf16[256,512]{1,0:T(8,128)(2,1)}, u32[]{:S(2)}) copy-start(bf16[256,512]{1,0:T(8,128)(2,1)} %slice.107) | copy-start | bytes 786436
  382.6 81.0 %copy-start.4 = (bf16[256,4096]{1,0:T(8,128)(2,1)S(1)}, bf16[256,4096]{1,0:T(8,128)(2,1)}, u32[]{:S(2)}) copy-start(bf16[256,4096]{1,0:T(8,128)(2,1)} %copy-done.2) | copy-start | bytes 6291460
  382.6 81.0 %copy-start.8 = (bf16[256,4096]{1,0:T(8,128)(2,1)S(1)}, bf16[256,4096]{1,0:T(8,128)(2,1)}, u32[]{:S(2)}) copy-start(bf16[256,4096]{1,0:T(8,128)(2,1)} %copy-done.6) | copy-start | bytes 6291460
  416.6 129.1 %collective-permute-start.14 = (bf16[256,1024]{1,0:T(8,128)(2,1)S(1)}, bf16[256,1024]{1,0:T(8,128)(2,1)S(1)}, u32[]{:S(2)}, u32[]{:S(2)}) collective-permute-start(bf16[256,1024]{1,0:T(8,128)(2,1)S(1)} %copy-done.17), channel_id=1, source_target_pairs={{0,4},{4,0},{1,5},{5,1},{2,6},{6,2},{3,7},{7,3}} | collective-permute-start | bytes 1572872 | tf_op jit(solution)/shard_map/ppermute | solution.py:139
  429.5 44.6 %copy-start.12 = (bf16[256,4096]{1,0:T(8,128)(2,1)S(1)}, bf16[256,4096]{1,0:T(8,128)(2,1)}, u32[]{:S(2)}) copy-start(bf16[256,4096]{1,0:T(8,128)(2,1)} %copy-done.9) | copy-start | bytes 6291460
  461.6 88.9 %collective-permute-start.3 = (bf16[256,512]{1,0:T(8,128)(2,1)S(1)}, bf16[256,512]{1,0:T(8,128)(2,1)S(1)}, u32[]{:S(2)}, u32[]{:S(2)}) collective-permute-start(bf16[256,512]{1,0:T(8,128)(2,1)S(1)} %copy-done.18), channel_id=1, source_target_pairs={{0,4},{4,0},{1,5},{5,1},{2,6},{6,2},{3,7},{7,3}} | collective-permute-start | bytes 786440 | tf_op jit(solution)/shard_map/ppermute | solution.py:139
  474.2 25.4 %slice-start = ((s8[4718592]{0:T(1024)(128)(4,1)}), s8[4194304]{0:T(1024)(128)(4,1)S(1)}, s32[]{:S(2)}) async-start(s8[4718592]{0:T(1024)(128)(4,1)} %bitcast), calls=%async_computation | async-start | bytes 8388608
  487.1 12.5 %slice-start.1 = ((s8[4718592]{0:T(1024)(128)(4,1)}), s8[524288]{0:T(1024)(128)(4,1)S(1)}, s32[]{:S(2)}) async-start(s8[4718592]{0:T(1024)(128)(4,1)} %bitcast), calls=%async_computation.1 | async-start | bytes 1048576
  (7 other events, 29.3 us)

commit v2 on v1

--- a/solution.py
+++ b/solution.py
@@ -106,6 +106,29 @@
     )(l_rem, piece, acc, x)
 
 
+def cut_kernel(row, start, b_ref, out_ref, buf, sems):
+    @pl.when(lax.axis_index("row") == 0)
+    def _():
+        fetch = pltpu.make_async_copy(b_ref.at[pl.ds(row, BLOCK), pl.ds(start, buf.shape[1])], buf, sems.at[0])
+        fetch.start()
+        fetch.wait()
+        store = pltpu.make_async_copy(buf, out_ref, sems.at[1])
+        store.start()
+        store.wait()
+
+
+def cut(b, row, start, width):
+    return pl.pallas_call(
+        functools.partial(cut_kernel, row, start),
+        in_specs=[pl.BlockSpec(memory_space=pltpu.HBM)],
+        out_specs=pl.BlockSpec(memory_space=pltpu.HBM),
+        out_shape=jax.ShapeDtypeStruct((BLOCK, width), b.dtype),
+        scratch_shapes=[pltpu.VMEM((BLOCK, width), b.dtype), pltpu.SemaphoreType.DMA((2,))],
+        compiler_params=pltpu.CompilerParams(vmem_limit_bytes=60 << 20),
+        cost_estimate=pl.CostEstimate(flops=2 * BLOCK * width, bytes_accessed=BLOCK * width * 4, transcendentals=0),
+    )(b)
+
+
 def weave(even, odd):
     count = even.shape[1] // BLOCK
     parts = []
@@ -118,6 +141,7 @@
     grid_rows = mesh.shape["row"]
     grid_cols = mesh.shape["col"]
     swap_row = [(r, r ^ 1) for r in range(grid_rows)]
+    down_row = [(r, r + 1) for r in range(grid_rows - 1)]
 
     def local_trmm(tri_loc, rhs_loc):
         rows, cols = rhs_loc.shape
@@ -133,10 +157,10 @@
 
         got = {}
         source = rhs_loc
-        for j, off, w in order:
-            piece = source[j * BLOCK:(j + 1) * BLOCK, off:off + w]
+        for i, (j, off, w) in enumerate(order):
+            piece = source[j * BLOCK:(j + 1) * BLOCK, off:off + w] if i else cut(source, j * BLOCK, off, w)
             source, piece = lax.optimization_barrier((source, piece))
-            got[j, off] = lax.ppermute(piece, "row", swap_row)
+            got[j, off] = lax.ppermute(piece, "row", down_row if i and j == final else swap_row)
         l_core, l_chip, l_both = (
             lax.ppermute(tri_loc, "col", [(c, c ^ d) for c in range(grid_cols)]) for d in (1, 2, 3))
         p = lax.axis_index("row")

time: 552 us -> 550 us (level)
    slice x15 -> x14, local copies, waits for them, and re-layouts: 42.3 us -> 40.6 us  [local_trmm(): source[j * BLOCK:(j + 1) * BLOCK, off:off + w]]
where the time goes in v2:
time: 550 us; the launch traced here: 548 us
  waiting for transfers between devices  361 us (66%)
  Pallas kernels  106 us (19%)
  local copies, waits for them, and re-layouts  47.7 us (9%)
  starting transfers between devices  24.7 us (4%)
  other arithmetic  9.05 us (2%)
    ppermute x15, waiting for transfers between devices, local_trmm(): lax.ppermute(piece, 'row', down_row if i and j == final else swap_row)  307 us
    pallas_call x12, Pallas kernels, row_block(): pl.pallas_call(functools.partial(block_kernel, count, len(aliases)), grid...  104 us
    ppermute x3, waiting for transfers between devices, local_trmm(): lax.ppermute(tri_loc, 'col', [(c, c ^ d) for c in range(grid_cols)])  53.4 us
    slice x14, local copies, waits for them, and re-layouts, local_trmm(): source[j * BLOCK:(j + 1) * BLOCK, off:off + w]  40.6 us
    ppermute x15, starting transfers between devices, local_trmm(): lax.ppermute(piece, 'row', down_row if i and j == final else swap_row)  21.3 us
  transfers between devices with their start and end apart: 18, of which 14 were waited for; matrix products, arithmetic and copies ran while one was open for 9% of the time, Pallas kernels for 19%

profile of v2, /device:TPU:0, one launch (start us, length us, event | category | flops | bytes accessed | tf_op | source)
XLA Modules:
  0.0 548.5 jit_solution(8046020906636239205)
XLA Ops:
  13.4 3.2 slice.92
  19.7 3.2 slice.94
  35.5 3.2 slice.99
  48.2 7.2 %collective-permute-done.1 = bf16[1536,768]{1,0:T(8,128)(2,1)} collective-permute-done((bf16[1536,768]{1,0:T(8,128)(2,1)}, bf16[1536,768]{1,0:T(8,128)(2,1)}, u32[]{:S(2)}, u32[]{:S(2)}) %collective-permute-start.1) | collective-permute-done | bytes 2359328 | tf_op jit(solution)/shard_map/ppermute | solution.py:165
  59.9 46.2 %collective-permute-done.2 = bf16[1536,768]{1,0:T(8,128)(2,1)} collective-permute-done((bf16[1536,768]{1,0:T(8,128)(2,1)}, bf16[1536,768]{1,0:T(8,128)(2,1)}, u32[]{:S(2)}, u32[]{:S(2)}) %collective-permute-start.2) | collective-permute-done | bytes 2359328 | tf_op jit(solution)/shard_map/ppermute | solution.py:165
  114.2 32.7 %collective-permute-done.10.refs_4_ = bf16[256,4096]{1,0:T(8,128)(2,1)S(1)} collective-permute-done((bf16[256,4096]{1,0:T(8,128)(2,1)}, bf16[256,4096]{1,0:T(8,128)(2,1)S(1)}, u32[]{:S(2)}, u32[]{:S(2)}) %collective-permute-start.10) | collective-permute-done | bytes 2097184 | tf_op jit(solution)/shard_map/ppermute | solution.py:163
  148.6 43.2 %collective-permute-done.5.refs_4_ = bf16[256,4096]{1,0:T(8,128)(2,1)S(1)} collective-permute-done((bf16[256,4096]{1,0:T(8,128)(2,1)}, bf16[256,4096]{1,0:T(8,128)(2,1)S(1)}, u32[]{:S(2)}, u32[]{:S(2)}) %collective-permute-start.5) | collective-permute-done | bytes 2097184 | tf_op jit(solution)/shard_map/ppermute | solution.py:163
  193.5 4.4 broadcast_select_fusion
  197.9 7.4 %shard_map.29.refs_4_ = bf16[1536,8192]{1,0:T(8,128)(2,1)} custom-call(bf16[1536,1536]{1,0:T(8,128)(2,1)S(1)} %get-tuple-element.71.refs_0_, bf16[1536,1536]{1,0:T(8,128)(2,1)S(1)} %get-tuple-element.72.refs_1_.l_ref, bf16[1536,8192]{1,0:T(8,128)(2,1)} %refs_2_.23, bf16[256,4096]{1,0:T(8,128)(2,1)} %collective-permute-done.9.refs_3_), custom_call_target="tpu_custom_call" | custom-call | flops 1073741824 | bytes 6291456 | tf_op jit(solution)/shard_map/pallas_call | solution.py:47
  205.3 4.8 shard_map.30.refs_5_
  210.1 6.2 %shard_map.31.refs_5_ = bf16[1536,8192]{1,0:T(8,128)(2,1)} custom-call(bf16[1536,1536]{1,0:T(8,128)(2,1)S(1)} %get-tuple-element.71.refs_0_, bf16[1536,1536]{1,0:T(8,128)(2,1)S(1)} %get-tuple-element.72.refs_1_.l_ref, bf16[1536,8192]{1,0:T(8,128)(2,1)} %refs_2_.23, bf16[256,4096]{1,0:T(8,128)(2,1)} %collective-permute-done.9.refs_3_, ...), custom_call_target="tpu_custom_call", output_to_operand_aliasing={{}: (5, {})} | custom-call | flops 2147483648 | bytes 10485760 | tf_op jit(solution)/shard_map/pallas_call | solution.py:47
  216.3 20.6 %collective-permute-done.11.refs_5_ = bf16[256,4096]{1,0:T(8,128)(2,1)} collective-permute-done((bf16[256,4096]{1,0:T(8,128)(2,1)}, bf16[256,4096]{1,0:T(8,128)(2,1)}, u32[]{:S(2)}, u32[]{:S(2)}) %collective-permute-start.11) | collective-permute-done | bytes 2097184 | tf_op jit(solution)/shard_map/ppermute | solution.py:163
  237.3 5.8 %shard_map.32.refs_6_ = bf16[1536,8192]{1,0:T(8,128)(2,1)} custom-call(bf16[1536,1536]{1,0:T(8,128)(2,1)S(1)} %get-tuple-element.71.refs_0_, bf16[1536,1536]{1,0:T(8,128)(2,1)S(1)} %get-tuple-element.72.refs_1_.l_ref, bf16[1536,8192]{1,0:T(8,128)(2,1)} %refs_2_.23, bf16[256,4096]{1,0:T(8,128)(2,1)S(1)} %copy-done.3, ...), custom_call_target="tpu_custom_call", output_to_operand_aliasing={{}: (5, {})} | custom-call | flops 2147483648 | bytes 10485760 | tf_op jit(solution)/shard_map/pallas_call | solution.py:47
  243.0 7.7 %shard_map.33.refs_6_ = bf16[1536,8192]{1,0:T(8,128)(2,1)} custom-call(bf16[1536,1536]{1,0:T(8,128)(2,1)S(1)} %get-tuple-element.71.refs_0_, bf16[1536,1536]{1,0:T(8,128)(2,1)} %copy-done, bf16[1536,8192]{1,0:T(8,128)(2,1)} %refs_2_.23, bf16[256,4096]{1,0:T(8,128)(2,1)} %collective-permute-done.9.refs_3_, ...), custom_call_target="tpu_custom_call", output_to_operand_aliasing={{}: (6, {})} | custom-call | flops 3221225472 | bytes 14680064 | tf_op jit(solution)/shard_map/pallas_call | solution.py:47
  250.7 31.1 %collective-permute-done.6.refs_5_ = bf16[256,4096]{1,0:T(8,128)(2,1)} collective-permute-done((bf16[256,4096]{1,0:T(8,128)(2,1)}, bf16[256,4096]{1,0:T(8,128)(2,1)}, u32[]{:S(2)}, u32[]{:S(2)}) %collective-permute-start.6) | collective-permute-done | bytes 2097184 | tf_op jit(solution)/shard_map/ppermute | solution.py:163
  282.2 7.4 %shard_map.34.refs_7_ = bf16[1536,8192]{1,0:T(8,128)(2,1)} custom-call(bf16[1536,1536]{1,0:T(8,128)(2,1)S(1)} %get-tuple-element.71.refs_0_, bf16[1536,1536]{1,0:T(8,128)(2,1)} %copy-done, bf16[1536,8192]{1,0:T(8,128)(2,1)} %refs_2_.23, bf16[256,4096]{1,0:T(8,128)(2,1)S(1)} %copy-done.3, ...), custom_call_target="tpu_custom_call", output_to_operand_aliasing={{}: (6, {})} | custom-call | flops 3221225472 | bytes 14680064 | tf_op jit(solution)/shard_map/pallas_call | solution.py:47
  289.6 37.2 %collective-permute-done.12.refs_6_ = bf16[256,4096]{1,0:T(8,128)(2,1)} collective-permute-done((bf16[256,4096]{1,0:T(8,128)(2,1)}, bf16[256,4096]{1,0:T(8,128)(2,1)}, u32[]{:S(2)}, u32[]{:S(2)}) %collective-permute-start.12) | collective-permute-done | bytes 2097184 | tf_op jit(solution)/shard_map/ppermute | solution.py:163
  326.7 3.6 collective-permute-start.16
  330.4 9.2 %shard_map.35.refs_7_ = bf16[1536,8192]{1,0:T(8,128)(2,1)} custom-call(bf16[1536,1536]{1,0:T(8,128)(2,1)S(1)} %get-tuple-element.71.refs_0_, bf16[1536,1536]{1,0:T(8,128)(2,1)} %copy-done, bf16[1536,8192]{1,0:T(8,128)(2,1)} %refs_2_.23, bf16[256,4096]{1,0:T(8,128)(2,1)} %collective-permute-done.9.refs_3_, ...), custom_call_target="tpu_custom_call", output_to_operand_aliasing={{}: (7, {})} | custom-call | flops 4294967296 | bytes 18874368 | tf_op jit(solution)/shard_map/pallas_call | solution.py:47
  339.6 32.1 %collective-permute-done.7.refs_6_ = bf16[256,4096]{1,0:T(8,128)(2,1)} collective-permute-done((bf16[256,4096]{1,0:T(8,128)(2,1)}, bf16[256,4096]{1,0:T(8,128)(2,1)}, u32[]{:S(2)}, u32[]{:S(2)}) %collective-permute-start.7) | collective-permute-done | bytes 2097184 | tf_op jit(solution)/shard_map/ppermute | solution.py:163
  371.7 3.3 collective-permute-start.15
  375.0 8.9 %shard_map.36.refs_8_ = bf16[1536,8192]{1,0:T(8,128)(2,1)} custom-call(bf16[1536,1536]{1,0:T(8,128)(2,1)S(1)} %get-tuple-element.71.refs_0_, bf16[1536,1536]{1,0:T(8,128)(2,1)} %copy-done, bf16[1536,8192]{1,0:T(8,128)(2,1)} %refs_2_.23, bf16[256,4096]{1,0:T(8,128)(2,1)S(1)} %copy-done.3, ...), custom_call_target="tpu_custom_call", output_to_operand_aliasing={{}: (7, {})} | custom-call | flops 4294967296 | bytes 18874368 | tf_op jit(solution)/shard_map/pallas_call | solution.py:47
  383.9 32.8 %collective-permute-done.13.refs_7_ = bf16[256,4096]{1,0:T(8,128)(2,1)} collective-permute-done((bf16[256,4096]{1,0:T(8,128)(2,1)}, bf16[256,4096]{1,0:T(8,128)(2,1)}, u32[]{:S(2)}, u32[]{:S(2)}) %collective-permute-start.13) | collective-permute-done | bytes 2097184 | tf_op jit(solution)/shard_map/ppermute | solution.py:163
  419.0 10.9 %shard_map.37.refs_8_ = bf16[1536,8192]{1,0:T(8,128)(2,1)} custom-call(bf16[1536,1536]{1,0:T(8,128)(2,1)} %copy-done.1, bf16[1536,1536]{1,0:T(8,128)(2,1)} %copy-done, bf16[1536,8192]{1,0:T(8,128)(2,1)} %refs_2_.23, bf16[256,4096]{1,0:T(8,128)(2,1)} %collective-permute-done.9.refs_3_, ...), custom_call_target="tpu_custom_call", output_to_operand_aliasing={{}: (8, {})} | custom-call | flops 5368709120 | bytes 23068672 | tf_op jit(solution)/shard_map/pallas_call | solution.py:47
  429.8 31.7 %collective-permute-done.8.refs_7_ = bf16[256,4096]{1,0:T(8,128)(2,1)} collective-permute-done((bf16[256,4096]{1,0:T(8,128)(2,1)}, bf16[256,4096]{1,0:T(8,128)(2,1)}, u32[]{:S(2)}, u32[]{:S(2)}) %collective-permute-start.8) | collective-permute-done | bytes 2097184 | tf_op jit(solution)/shard_map/ppermute | solution.py:163
  464.1 10.6 %shard_map.38.refs_8_ = bf16[1536,8192]{1,0:T(8,128)(2,1)} custom-call(bf16[1536,1536]{1,0:T(8,128)(2,1)} %copy-done.1, bf16[1536,1536]{1,0:T(8,128)(2,1)} %copy-done, bf16[1536,8192]{1,0:T(8,128)(2,1)} %refs_2_.23, bf16[256,4096]{1,0:T(8,128)(2,1)S(1)} %copy-done.4, bf16[256,4096]{1,0:T(8,128)(2,1)S(1)} %copy-done.8, ...), custom_call_target="tpu_custom_call", output_to_operand_aliasing={{}: (8, {})} | custom-call | flops 5368709120 | bytes 23068672 | tf_op jit(solution)/shard_map/pallas_call | solution.py:47
  474.7 12.9 %shard_map.39 = (bf16[1536,8192]{1,0:T(8,128)(2,1)}, f32[256,4096]{1,0:T(8,128)}) custom-call(bf16[1536,1536]{1,0:T(8,128)(2,1)} %copy-done.1, bf16[1536,1536]{1,0:T(8,128)(2,1)} %copy-done, bf16[1536,8192]{1,0:T(8,128)(2,1)} %refs_2_.23, bf16[256,4096]{1,0:T(8,128)(2,1)} %collective-permute-done.9.refs_3_, ...), custom_call_target="tpu_custom_call", output_to_operand_aliasing={{0}: (8, {})} | custom-call | flops 5905580032 | bytes 25165824 | tf_op jit(solution)/shard_map/pallas_call | solution.py:47
  487.6 12.5 %shard_map.40 = (bf16[1536,8192]{1,0:T(8,128)(2,1)}, f32[256,4096]{1,0:T(8,128)}) custom-call(bf16[1536,1536]{1,0:T(8,128)(2,1)} %copy-done.1, bf16[1536,1536]{1,0:T(8,128)(2,1)} %copy-done, bf16[1536,8192]{1,0:T(8,128)(2,1)} %refs_2_.23, bf16[256,4096]{1,0:T(8,128)(2,1)S(1)} %copy-done.4, ...), custom_call_target="tpu_custom_call", output_to_operand_aliasing={{0}: (8, {})} | custom-call | flops 5905580032 | bytes 25165824 | tf_op jit(solution)/shard_map/pallas_call | solution.py:47
  502.3 7.7 %collective-permute-done.16.b_ref = bf16[256,4096]{1,0:T(8,128)(2,1)} collective-permute-done((bf16[256,4096]{1,0:T(8,128)(2,1)}, bf16[256,4096]{1,0:T(8,128)(2,1)}, u32[]{:S(2)}, u32[]{:S(2)}) %collective-permute-start.16) | collective-permute-done | bytes 2097184 | tf_op jit(solution)/shard_map/ppermute | solution.py:163
  510.1 22.4 %collective-permute-done.15.b_ref = bf16[256,2048]{1,0:T(8,128)(2,1)} collective-permute-done((bf16[256,2048]{1,0:T(8,128)(2,1)}, bf16[256,2048]{1,0:T(8,128)(2,1)}, u32[]{:S(2)}, u32[]{:S(2)}) %collective-permute-start.15) | collective-permute-done | bytes 1048608 | tf_op jit(solution)/shard_map/ppermute | solution.py:163
  532.6 11.1 %collective-permute-done.14.b_ref = bf16[256,1024]{1,0:T(8,128)(2,1)S(1)} collective-permute-done((bf16[256,1024]{1,0:T(8,128)(2,1)S(1)}, bf16[256,1024]{1,0:T(8,128)(2,1)S(1)}, u32[]{:S(2)}, u32[]{:S(2)}) %collective-permute-start.14) | collective-permute-done | bytes 524320 | tf_op jit(solution)/shard_map/ppermute | solution.py:163
  543.7 4.6 collective-permute-done.3.b_ref
  (93 shorter events, 62.5 us)
Async XLA Ops:
  0.0 47.8 %collective-permute-start = (bf16[1536,768]{1,0:T(8,128)(2,1)}, bf16[1536,768]{1,0:T(8,128)(2,1)}, u32[]{:S(2)}, u32[]{:S(2)}) collective-permute-start(bf16[1536,768]{1,0:T(8,128)(2,1)} %param.2), channel_id=1, source_target_pairs={{0,1},{1,0},{2,3},{3,2},{4,5},{5,4},{6,7},{7,6}} | collective-permute-start | bytes 7077896 | tf_op jit(solution)/shard_map/ppermute | solution.py:165
  0.8 54.5 %collective-permute-start.1 = (bf16[1536,768]{1,0:T(8,128)(2,1)}, bf16[1536,768]{1,0:T(8,128)(2,1)}, u32[]{:S(2)}, u32[]{:S(2)}) collective-permute-start(bf16[1536,768]{1,0:T(8,128)(2,1)} %param.2), channel_id=1, source_target_pairs={{0,3},{1,2},{2,1},{3,0},{4,7},{5,6},{6,5},{7,4}} | collective-permute-start | bytes 7077896 | tf_op jit(solution)/shard_map/ppermute | solution.py:165
  3.4 102.7 %collective-permute-start.2 = (bf16[1536,768]{1,0:T(8,128)(2,1)}, bf16[1536,768]{1,0:T(8,128)(2,1)}, u32[]{:S(2)}, u32[]{:S(2)}) collective-permute-start(bf16[1536,768]{1,0:T(8,128)(2,1)} %param.2), channel_id=1, source_target_pairs={{0,2},{1,3},{2,0},{3,1},{4,6},{5,7},{6,4},{7,5}} | collective-permute-start | bytes 7077896 | tf_op jit(solution)/shard_map/ppermute | solution.py:165
  8.3 101.9 %collective-permute-start.9 = (bf16[256,4096]{1,0:T(8,128)(2,1)}, bf16[256,4096]{1,0:T(8,128)(2,1)}, u32[]{:S(2)}, u32[]{:S(2)}) collective-permute-start(bf16[256,4096]{1,0:T(8,128)(2,1)} %slice.90), channel_id=1, source_target_pairs={{0,4},{4,0},{1,5},{5,1},{2,6},{6,2},{3,7},{7,3}} | collective-permute-start | bytes 6291464 | tf_op jit(solution)/shard_map/ppermute | solution.py:163
  11.8 98.8 %collective-permute-start.4 = (bf16[256,4096]{1,0:T(8,128)(2,1)}, bf16[256,4096]{1,0:T(8,128)(2,1)S(1)}, u32[]{:S(2)}, u32[]{:S(2)}) collective-permute-start(bf16[256,4096]{1,0:T(8,128)(2,1)} %slice.91), channel_id=1, source_target_pairs={{0,4},{4,0},{1,5},{5,1},{2,6},{6,2},{3,7},{7,3}} | collective-permute-start | bytes 6291464 | tf_op jit(solution)/shard_map/ppermute | solution.py:163
  47.8 99.1 %collective-permute-start.10 = (bf16[256,4096]{1,0:T(8,128)(2,1)}, bf16[256,4096]{1,0:T(8,128)(2,1)S(1)}, u32[]{:S(2)}, u32[]{:S(2)}) collective-permute-start(bf16[256,4096]{1,0:T(8,128)(2,1)} %slice.92), channel_id=1, source_target_pairs={{0,4},{4,0},{1,5},{5,1},{2,6},{6,2},{3,7},{7,3}} | collective-permute-start | bytes 6291464 | tf_op jit(solution)/shard_map/ppermute | solution.py:163
  55.4 136.4 %collective-permute-start.5 = (bf16[256,4096]{1,0:T(8,128)(2,1)}, bf16[256,4096]{1,0:T(8,128)(2,1)S(1)}, u32[]{:S(2)}, u32[]{:S(2)}) collective-permute-start(bf16[256,4096]{1,0:T(8,128)(2,1)} %slice.93), channel_id=1, source_target_pairs={{0,4},{4,0},{1,5},{5,1},{2,6},{6,2},{3,7},{7,3}} | collective-permute-start | bytes 6291464 | tf_op jit(solution)/shard_map/ppermute | solution.py:163
  59.6 48.2 %copy-start.16 = (bf16[1536,768]{1,0:T(8,128)(2,1)S(1)}, bf16[1536,768]{1,0:T(8,128)(2,1)}, u32[]{:S(2)}) copy-start(bf16[1536,768]{1,0:T(8,128)(2,1)} %param.2) | copy-start | bytes 7077892
  106.1 130.8 %collective-permute-start.11 = (bf16[256,4096]{1,0:T(8,128)(2,1)}, bf16[256,4096]{1,0:T(8,128)(2,1)}, u32[]{:S(2)}, u32[]{:S(2)}) collective-permute-start(bf16[256,4096]{1,0:T(8,128)(2,1)} %slice.94), channel_id=1, source_target_pairs={{0,4},{4,0},{1,5},{5,1},{2,6},{6,2},{3,7},{7,3}} | collective-permute-start | bytes 6291464 | tf_op jit(solution)/shard_map/ppermute | solution.py:163
  110.2 83.3 %copy-start.14 = (bf16[1536,1536]{1,0:T(8,128)(2,1)}, bf16[1536,1536]{1,0:T(8,128)(2,1)S(1)}, u32[]{:S(2)}) copy-start(bf16[1536,1536]{1,0:T(8,128)(2,1)S(1)} %get-tuple-element.78) | copy-start | bytes 14155780
  110.2 83.3 %copy-start.15 = (bf16[1536,1536]{1,0:T(8,128)(2,1)}, bf16[1536,1536]{1,0:T(8,128)(2,1)S(1)}, u32[]{:S(2)}) copy-start(bf16[1536,1536]{1,0:T(8,128)(2,1)S(1)} %get-tuple-element.77) | copy-start | bytes 14155780
  110.2 171.6 %collective-permute-start.6 = (bf16[256,4096]{1,0:T(8,128)(2,1)}, bf16[256,4096]{1,0:T(8,128)(2,1)}, u32[]{:S(2)}, u32[]{:S(2)}) collective-permute-start(bf16[256,4096]{1,0:T(8,128)(2,1)} %slice.95), channel_id=1, source_target_pairs={{0,4},{4,0},{1,5},{5,1},{2,6},{6,2},{3,7},{7,3}} | collective-permute-start | bytes 6291464 | tf_op jit(solution)/shard_map/ppermute | solution.py:163
  112.2 214.6 %collective-permute-start.12 = (bf16[256,4096]{1,0:T(8,128)(2,1)}, bf16[256,4096]{1,0:T(8,128)(2,1)}, u32[]{:S(2)}, u32[]{:S(2)}) collective-permute-start(bf16[256,4096]{1,0:T(8,128)(2,1)} %slice.96), channel_id=1, source_target_pairs={{0,4},{4,0},{1,5},{5,1},{2,6},{6,2},{3,7},{7,3}} | collective-permute-start | bytes 6291464 | tf_op jit(solution)/shard_map/ppermute | solution.py:163
  148.2 223.5 %collective-permute-start.7 = (bf16[256,4096]{1,0:T(8,128)(2,1)}, bf16[256,4096]{1,0:T(8,128)(2,1)}, u32[]{:S(2)}, u32[]{:S(2)}) collective-permute-start(bf16[256,4096]{1,0:T(8,128)(2,1)} %slice.97), channel_id=1, source_target_pairs={{0,4},{4,0},{1,5},{5,1},{2,6},{6,2},{3,7},{7,3}} | collective-permute-start | bytes 6291464 | tf_op jit(solution)/shard_map/ppermute | solution.py:163
  193.1 223.5 %collective-permute-start.13 = (bf16[256,4096]{1,0:T(8,128)(2,1)}, bf16[256,4096]{1,0:T(8,128)(2,1)}, u32[]{:S(2)}, u32[]{:S(2)}) collective-permute-start(bf16[256,4096]{1,0:T(8,128)(2,1)} %slice.98), channel_id=1, source_target_pairs={{0,4},{4,0},{1,5},{5,1},{2,6},{6,2},{3,7},{7,3}} | collective-permute-start | bytes 6291464 | tf_op jit(solution)/shard_map/ppermute | solution.py:163
  197.9 39.4 %copy-start = (bf16[1536,1536]{1,0:T(8,128)(2,1)}, bf16[1536,1536]{1,0:T(8,128)(2,1)S(1)}, u32[]{:S(2)}) copy-start(bf16[1536,1536]{1,0:T(8,128)(2,1)S(1)} %get-tuple-element.72.refs_1_.l_ref) | copy-start | bytes 14155780
  197.9 177.1 %copy-start.1 = (bf16[1536,1536]{1,0:T(8,128)(2,1)}, bf16[1536,1536]{1,0:T(8,128)(2,1)S(1)}, u32[]{:S(2)}) copy-start(bf16[1536,1536]{1,0:T(8,128)(2,1)S(1)} %get-tuple-element.71.refs_0_) | copy-start | bytes 14155780
  210.1 27.2 %copy-start.7 = (bf16[256,4096]{1,0:T(8,128)(2,1)S(1)}, bf16[256,4096]{1,0:T(8,128)(2,1)}, u32[]{:S(2)}) copy-start(bf16[256,4096]{1,0:T(8,128)(2,1)} %copy-done.6) | copy-start | bytes 6291460
  236.9 224.7 %collective-permute-start.8 = (bf16[256,4096]{1,0:T(8,128)(2,1)}, bf16[256,4096]{1,0:T(8,128)(2,1)}, u32[]{:S(2)}, u32[]{:S(2)}) collective-permute-start(bf16[256,4096]{1,0:T(8,128)(2,1)} %slice.99), channel_id=1, source_target_pairs={{0,4},{4,0},{1,5},{5,1},{2,6},{6,2},{3,7},{7,3}} | collective-permute-start | bytes 6291464 | tf_op jit(solution)/shard_map/ppermute | solution.py:163
  250.7 79.7 %copy-start.11 = (bf16[256,4096]{1,0:T(8,128)(2,1)S(1)}, bf16[256,4096]{1,0:T(8,128)(2,1)}, u32[]{:S(2)}) copy-start(bf16[256,4096]{1,0:T(8,128)(2,1)} %copy-done.9) | copy-start | bytes 6291460
  281.8 218.2 %collective-permute-start.17 = (bf16[256,512]{1,0:T(8,128)(2,1)}, bf16[256,512]{1,0:T(8,128)(2,1)}, u32[]{:S(2)}, u32[]{:S(2)}) collective-permute-start(bf16[256,512]{1,0:T(8,128)(2,1)} %shard_map.28), channel_id=1, source_target_pairs={{0,4},{4,0},{1,5},{5,1},{2,6},{6,2},{3,7},{7,3}} | collective-permute-start | bytes 786440 | tf_op jit(solution)/shard_map/ppermute | solution.py:163
  326.7 183.3 %collective-permute-start.16 = (bf16[256,4096]{1,0:T(8,128)(2,1)}, bf16[256,4096]{1,0:T(8,128)(2,1)}, u32[]{:S(2)}, u32[]{:S(2)}) collective-permute-start(bf16[256,4096]{1,0:T(8,128)(2,1)} %slice.100), channel_id=1, source_target_pairs={{0,4},{1,5},{2,6},{3,7}} | collective-permute-start | bytes 6291464 | tf_op jit(solution)/shard_map/ppermute | solution.py:163
  339.6 77.0 %copy-start.17 = (bf16[256,1024]{1,0:T(8,128)(2,1)S(1)}, bf16[256,1024]{1,0:T(8,128)(2,1)}, u32[]{:S(2)}) copy-start(bf16[256,1024]{1,0:T(8,128)(2,1)} %slice.102) | copy-start | bytes 1572868
  371.7 160.8 %collective-permute-start.15 = (bf16[256,2048]{1,0:T(8,128)(2,1)}, bf16[256,2048]{1,0:T(8,128)(2,1)}, u32[]{:S(2)}, u32[]{:S(2)}) collective-permute-start(bf16[256,2048]{1,0:T(8,128)(2,1)} %slice.101), channel_id=1, source_target_pairs={{0,4},{1,5},{2,6},{3,7}} | collective-permute-start | bytes 3145736 | tf_op jit(solution)/shard_map/ppermute | solution.py:163
  383.8 77.7 %copy-start.18 = (bf16[256,512]{1,0:T(8,128)(2,1)S(1)}, bf16[256,512]{1,0:T(8,128)(2,1)}, u32[]{:S(2)}) copy-start(bf16[256,512]{1,0:T(8,128)(2,1)} %slice.103) | copy-start | bytes 786436
  383.8 80.2 %copy-start.4 = (bf16[256,4096]{1,0:T(8,128)(2,1)S(1)}, bf16[256,4096]{1,0:T(8,128)(2,1)}, u32[]{:S(2)}) copy-start(bf16[256,4096]{1,0:T(8,128)(2,1)} %copy-done.2) | copy-start | bytes 6291460
  383.8 80.2 %copy-start.8 = (bf16[256,4096]{1,0:T(8,128)(2,1)S(1)}, bf16[256,4096]{1,0:T(8,128)(2,1)}, u32[]{:S(2)}) copy-start(bf16[256,4096]{1,0:T(8,128)(2,1)} %copy-done.6) | copy-start | bytes 6291460
  416.6 127.0 %collective-permute-start.14 = (bf16[256,1024]{1,0:T(8,128)(2,1)S(1)}, bf16[256,1024]{1,0:T(8,128)(2,1)S(1)}, u32[]{:S(2)}, u32[]{:S(2)}) collective-permute-start(bf16[256,1024]{1,0:T(8,128)(2,1)S(1)} %copy-done.17), channel_id=1, source_target_pairs={{0,4},{1,5},{2,6},{3,7}} | collective-permute-start | bytes 1572872 | tf_op jit(solution)/shard_map/ppermute | solution.py:163
  429.8 44.8 %copy-start.12 = (bf16[256,4096]{1,0:T(8,128)(2,1)S(1)}, bf16[256,4096]{1,0:T(8,128)(2,1)}, u32[]{:S(2)}) copy-start(bf16[256,4096]{1,0:T(8,128)(2,1)} %copy-done.9) | copy-start | bytes 6291460
  461.6 86.7 %collective-permute-start.3 = (bf16[256,512]{1,0:T(8,128)(2,1)S(1)}, bf16[256,512]{1,0:T(8,128)(2,1)S(1)}, u32[]{:S(2)}, u32[]{:S(2)}) collective-permute-start(bf16[256,512]{1,0:T(8,128)(2,1)S(1)} %copy-done.18), channel_id=1, source_target_pairs={{0,4},{1,5},{2,6},{3,7}} | collective-permute-start | bytes 786440 | tf_op jit(solution)/shard_map/ppermute | solution.py:163
  474.6 25.4 %slice-start = ((s8[4718592]{0:T(1024)(128)(4,1)}), s8[4194304]{0:T(1024)(128)(4,1)S(1)}, s32[]{:S(2)}) async-start(s8[4718592]{0:T(1024)(128)(4,1)} %bitcast), calls=%async_computation | async-start | bytes 8388608
  487.6 12.5 %slice-start.1 = ((s8[4718592]{0:T(1024)(128)(4,1)}), s8[524288]{0:T(1024)(128)(4,1)S(1)}, s32[]{:S(2)}) async-start(s8[4718592]{0:T(1024)(128)(4,1)} %bitcast), calls=%async_computation.1 | async-start | bytes 1048576
  (7 other events, 26.3 us)

commit v3 on v2

--- a/solution.py
+++ b/solution.py
@@ -51,7 +51,7 @@
         out_specs=out_specs,
         out_shape=out_shape,
         input_output_aliases=aliases,
-        compiler_params=pltpu.CompilerParams(vmem_limit_bytes=40 << 20),
+        compiler_params=pltpu.CompilerParams(vmem_limit_bytes=24 << 20),
         cost_estimate=pl.CostEstimate(
             flops=2 * BLOCK * (depth + count * BLOCK) * width,
             bytes_accessed=(depth + count * BLOCK + BLOCK) * width * 2, transcendentals=0),
@@ -100,10 +100,38 @@
             pltpu.SemaphoreType.DMA((4,)),
         ],
         input_output_aliases={3: 0},
-        compiler_params=pltpu.CompilerParams(vmem_limit_bytes=16 << 20),
+        compiler_params=pltpu.CompilerParams(vmem_limit_bytes=12 << 20),
         cost_estimate=pl.CostEstimate(
             flops=2 * BLOCK * BLOCK * width, bytes_accessed=BLOCK * width * 8, transcendentals=0),
     )(l_rem, piece, acc, x)
+
+
+def last_kernel(step, start, row, l_ref, b_ref, acc_ref, x_in, x_ref, out_buf, sem):
+    del x_in
+
+    @pl.when(lax.axis_index("row") == row)
+    def _():
+        acc = acc_ref[...] + jnp.dot(l_ref[...], b_ref[...], preferred_element_type=jnp.float32)
+        out_buf[...] = acc.astype(out_buf.dtype)
+        copy = pltpu.make_async_copy(
+            out_buf, x_ref.at[pl.ds(step * BLOCK, BLOCK), pl.ds(start, b_ref.shape[1])], sem)
+        copy.start()
+        copy.wait()
+
+
+def finish_last(step, start, row, l_last, piece, acc, x):
+    width = piece.shape[1]
+    return pl.pallas_call(
+        functools.partial(last_kernel, step, start, row),
+        in_specs=[pl.BlockSpec(memory_space=pltpu.VMEM)] * 3 + [pl.BlockSpec(memory_space=pltpu.HBM)],
+        out_specs=pl.BlockSpec(memory_space=pltpu.HBM),
+        out_shape=jax.ShapeDtypeStruct(x.shape, x.dtype),
+        scratch_shapes=[pltpu.VMEM((BLOCK, width), x.dtype), pltpu.SemaphoreType.DMA],
+        input_output_aliases={3: 0},
+        compiler_params=pltpu.CompilerParams(vmem_limit_bytes=8 << 20),
+        cost_estimate=pl.CostEstimate(
+            flops=2 * BLOCK * BLOCK * width, bytes_accessed=BLOCK * width * 8, transcendentals=0),
+    )(l_last, piece, acc, x)
 
 
 def cut_kernel(row, start, b_ref, out_ref, buf, sems):
@@ -156,11 +184,17 @@
         order += [(final, off, w) for off, w in tail]
 
         got = {}
-        source = rhs_loc
-        for i, (j, off, w) in enumerate(order):
+
+        def send(i, source):
+            j, off, w = order[i]
             piece = source[j * BLOCK:(j + 1) * BLOCK, off:off + w] if i else cut(source, j * BLOCK, off, w)
             source, piece = lax.optimization_barrier((source, piece))
             got[j, off] = lax.ppermute(piece, "row", down_row if i and j == final else swap_row)
+            return source
+
+        source = rhs_loc
+        for i in range(len(order) - 1):
+            source = send(i, source)
         l_core, l_chip, l_both = (
             lax.ppermute(tri_loc, "col", [(c, c ^ d) for c in range(grid_cols)]) for d in (1, 2, 3))
         p = lax.axis_index("row")
@@ -180,10 +214,16 @@
         for h in range(2):
             x, acc[h] = row_block(
                 final, final, h * half, 1024, l_own, l_rem, rhs_loc, [got[k, h * half] for k in range(final)], x, partial=True)
-        for off, w in [(cols - first, first), *tail]:
+        l_last = l_rem[final * BLOCK:, final * BLOCK:]
+        off, w = tail[-1]
+        acc_last = acc[1][:, off - half:off - half + w]
+        source, acc[1] = lax.optimization_barrier((source, acc[1]))
+        send(len(order) - 1, source)
+        for off, w in [(cols - first, first), *tail[:-1]]:
             h = off // half
             x = finish(final, off, grid_rows - 1, l_rem, got[final, off], acc[h], off - h * half, x)
-        return x
+        off, w = tail[-1]
+        return finish_last(final, off, grid_rows - 1, l_last, got[final, off], acc_last, x)
 
     part_spec = P(("batch", "row"), "col")
     return jax.shard_map(local_trmm, mesh=mesh, in_specs=(part_spec, part_spec), out_specs=part_spec, check_vma=False)

time: 550 us -> 550 us (level)
  waiting for transfers between devices: 361 us -> 370 us
  Pallas kernels: 106 us -> 99.1 us
    ppermute x15, waiting for transfers between devices: 307 us -> 315 us  [send(): lax.ppermute(piece, 'row', down_row if i and j == final else swap_row)]
    pallas_call x12, Pallas kernels: 104 us -> 97.2 us  [row_block(): pl.pallas_call(functools.partial(block_kernel, count, len(aliases)), grid...]
    slice x14 -> x16, local copies, waits for them, and re-layouts: 40.6 us -> 39.9 us  [the longest x14 39.9 us: send(): source[j * BLOCK:(j + 1) * BLOCK, off:off + w]]
  transfers between devices with their start and end apart: 18 -> 18, of which waited for: 14 -> 14; matrix products, arithmetic and copies ran while one was open for 9% -> 9% of each run, Pallas kernels for 19% -> 18%
where the time goes in v3:
time: 550 us; the launch traced here: 548 us
  waiting for transfers between devices  370 us (67%)
  Pallas kernels  99.1 us (18%)
  local copies, waits for them, and re-layouts  44.9 us (8%)
  starting transfers between devices  24.9 us (5%)
  other arithmetic  9.04 us (2%)
    ppermute x15, waiting for transfers between devices, send(): lax.ppermute(piece, 'row', down_row if i and j == final else swap_row)  315 us
    pallas_call x12, Pallas kernels, row_block(): pl.pallas_call(functools.partial(block_kernel, count, len(aliases)), grid...  97.2 us
    ppermute x3, waiting for transfers between devices, local_trmm(): lax.ppermute(tri_loc, 'col', [(c, c ^ d) for c in range(grid_cols)])  55.1 us
    slice x14, local copies, waits for them, and re-layouts, send(): source[j * BLOCK:(j + 1) * BLOCK, off:off + w]  39.9 us
    ppermute x15, starting transfers between devices, send(): lax.ppermute(piece, 'row', down_row if i and j == final else swap_row)  21.5 us
  transfers between devices with their start and end apart: 18, of which 14 were waited for; matrix products, arithmetic and copies ran while one was open for 9% of the time, Pallas kernels for 18%

profile of v3, /device:TPU:0, one launch (start us, length us, event | category | flops | bytes accessed | tf_op | source)
XLA Modules:
  0.0 548.4 jit_solution(13338521855503384227)
XLA Ops:
  8.6 3.2 slice.98
  26.0 3.2 slice.103
  32.3 3.2 slice.105
  46.4 8.9 %collective-permute-done.1 = bf16[1536,768]{1,0:T(8,128)(2,1)} collective-permute-done((bf16[1536,768]{1,0:T(8,128)(2,1)}, bf16[1536,768]{1,0:T(8,128)(2,1)}, u32[]{:S(2)}, u32[]{:S(2)}) %collective-permute-start.1) | collective-permute-done | bytes 2359328 | tf_op jit(solution)/shard_map/ppermute | solution.py:199
  59.9 46.2 %collective-permute-done.2 = bf16[1536,768]{1,0:T(8,128)(2,1)} collective-permute-done((bf16[1536,768]{1,0:T(8,128)(2,1)}, bf16[1536,768]{1,0:T(8,128)(2,1)}, u32[]{:S(2)}, u32[]{:S(2)}) %collective-permute-start.2) | collective-permute-done | bytes 2359328 | tf_op jit(solution)/shard_map/ppermute | solution.py:199
  114.1 32.7 %collective-permute-done.9.refs_4_ = bf16[256,4096]{1,0:T(8,128)(2,1)S(1)} collective-permute-done((bf16[256,4096]{1,0:T(8,128)(2,1)}, bf16[256,4096]{1,0:T(8,128)(2,1)S(1)}, u32[]{:S(2)}, u32[]{:S(2)}) %collective-permute-start.9) | collective-permute-done | bytes 2097184 | tf_op jit(solution)/shard_map/ppermute | solution.py:192
  148.6 43.2 %collective-permute-done.4.refs_4_ = bf16[256,4096]{1,0:T(8,128)(2,1)S(1)} collective-permute-done((bf16[256,4096]{1,0:T(8,128)(2,1)}, bf16[256,4096]{1,0:T(8,128)(2,1)S(1)}, u32[]{:S(2)}, u32[]{:S(2)}) %collective-permute-start.4) | collective-permute-done | bytes 2097184 | tf_op jit(solution)/shard_map/ppermute | solution.py:192
  193.5 4.4 broadcast_select_fusion
  197.9 5.1 shard_map.29.refs_4_
  203.1 4.8 shard_map.30.refs_5_
  207.8 6.2 %shard_map.31.refs_5_ = bf16[1536,8192]{1,0:T(8,128)(2,1)} custom-call(bf16[1536,1536]{1,0:T(8,128)(2,1)S(1)} %get-tuple-element.75.refs_0_, bf16[1536,1536]{1,0:T(8,128)(2,1)S(1)} %get-tuple-element.76.refs_1_.l_ref, bf16[1536,8192]{1,0:T(8,128)(2,1)} %refs_2_.23, bf16[256,4096]{1,0:T(8,128)(2,1)} %collective-permute-done.8.refs_3_, ...), custom_call_target="tpu_custom_call", output_to_operand_aliasing={{}: (5, {})} | custom-call | flops 2147483648 | bytes 10485760 | tf_op jit(solution)/shard_map/pallas_call | solution.py:47
  214.0 22.8 %collective-permute-done.10.refs_5_ = bf16[256,4096]{1,0:T(8,128)(2,1)} collective-permute-done((bf16[256,4096]{1,0:T(8,128)(2,1)}, bf16[256,4096]{1,0:T(8,128)(2,1)}, u32[]{:S(2)}, u32[]{:S(2)}) %collective-permute-start.10) | collective-permute-done | bytes 2097184 | tf_op jit(solution)/shard_map/ppermute | solution.py:192
  237.2 5.8 %shard_map.32.refs_6_ = bf16[1536,8192]{1,0:T(8,128)(2,1)} custom-call(bf16[1536,1536]{1,0:T(8,128)(2,1)S(1)} %get-tuple-element.75.refs_0_, bf16[1536,1536]{1,0:T(8,128)(2,1)S(1)} %get-tuple-element.76.refs_1_.l_ref, bf16[1536,8192]{1,0:T(8,128)(2,1)} %refs_2_.23, bf16[256,4096]{1,0:T(8,128)(2,1)S(1)} %copy-done.1, ...), custom_call_target="tpu_custom_call", output_to_operand_aliasing={{}: (5, {})} | custom-call | flops 2147483648 | bytes 10485760 | tf_op jit(solution)/shard_map/pallas_call | solution.py:47
  243.0 7.6 %shard_map.33.refs_6_ = bf16[1536,8192]{1,0:T(8,128)(2,1)} custom-call(bf16[1536,1536]{1,0:T(8,128)(2,1)S(1)} %get-tuple-element.75.refs_0_, bf16[1536,1536]{1,0:T(8,128)(2,1)S(1)} %get-tuple-element.76.refs_1_.l_ref, bf16[1536,8192]{1,0:T(8,128)(2,1)} %refs_2_.23, bf16[256,4096]{1,0:T(8,128)(2,1)} %collective-permute-done.8.refs_3_, ...), custom_call_target="tpu_custom_call", output_to_operand_aliasing={{}: (6, {})} | custom-call | flops 3221225472 | bytes 14680064 | tf_op jit(solution)/shard_map/pallas_call | solution.py:47
  250.6 31.2 %collective-permute-done.5.refs_5_ = bf16[256,4096]{1,0:T(8,128)(2,1)} collective-permute-done((bf16[256,4096]{1,0:T(8,128)(2,1)}, bf16[256,4096]{1,0:T(8,128)(2,1)}, u32[]{:S(2)}, u32[]{:S(2)}) %collective-permute-start.5) | collective-permute-done | bytes 2097184 | tf_op jit(solution)/shard_map/ppermute | solution.py:192
  282.2 7.2 %shard_map.34.refs_7_ = bf16[1536,8192]{1,0:T(8,128)(2,1)} custom-call(bf16[1536,1536]{1,0:T(8,128)(2,1)S(1)} %get-tuple-element.75.refs_0_, bf16[1536,1536]{1,0:T(8,128)(2,1)S(1)} %get-tuple-element.76.refs_1_.l_ref, bf16[1536,8192]{1,0:T(8,128)(2,1)} %refs_2_.23, bf16[256,4096]{1,0:T(8,128)(2,1)S(1)} %copy-done.1, ...), custom_call_target="tpu_custom_call", output_to_operand_aliasing={{}: (6, {})} | custom-call | flops 3221225472 | bytes 14680064 | tf_op jit(solution)/shard_map/pallas_call | solution.py:47
  289.4 37.3 %collective-permute-done.11.refs_6_ = bf16[256,4096]{1,0:T(8,128)(2,1)} collective-permute-done((bf16[256,4096]{1,0:T(8,128)(2,1)}, bf16[256,4096]{1,0:T(8,128)(2,1)}, u32[]{:S(2)}, u32[]{:S(2)}) %collective-permute-start.11) | collective-permute-done | bytes 2097184 | tf_op jit(solution)/shard_map/ppermute | solution.py:192
  326.7 3.7 collective-permute-start.16
  330.4 9.0 %shard_map.35.refs_7_ = bf16[1536,8192]{1,0:T(8,128)(2,1)} custom-call(bf16[1536,1536]{1,0:T(8,128)(2,1)S(1)} %get-tuple-element.75.refs_0_, bf16[1536,1536]{1,0:T(8,128)(2,1)S(1)} %get-tuple-element.76.refs_1_.l_ref, bf16[1536,8192]{1,0:T(8,128)(2,1)} %refs_2_.23, bf16[256,4096]{1,0:T(8,128)(2,1)} %collective-permute-done.8.refs_3_, ...), custom_call_target="tpu_custom_call", output_to_operand_aliasing={{}: (7, {})} | custom-call | flops 4294967296 | bytes 18874368 | tf_op jit(solution)/shard_map/pallas_call | solution.py:47
  339.4 32.2 %collective-permute-done.6.refs_6_ = bf16[256,4096]{1,0:T(8,128)(2,1)} collective-permute-done((bf16[256,4096]{1,0:T(8,128)(2,1)}, bf16[256,4096]{1,0:T(8,128)(2,1)}, u32[]{:S(2)}, u32[]{:S(2)}) %collective-permute-start.6) | collective-permute-done | bytes 2097184 | tf_op jit(solution)/shard_map/ppermute | solution.py:192
  371.6 3.3 collective-permute-start.15
  374.9 8.7 %shard_map.36.refs_8_ = bf16[1536,8192]{1,0:T(8,128)(2,1)} custom-call(bf16[1536,1536]{1,0:T(8,128)(2,1)S(1)} %get-tuple-element.75.refs_0_, bf16[1536,1536]{1,0:T(8,128)(2,1)S(1)} %get-tuple-element.76.refs_1_.l_ref, bf16[1536,8192]{1,0:T(8,128)(2,1)} %refs_2_.23, bf16[256,4096]{1,0:T(8,128)(2,1)S(1)} %copy-done.1, ...), custom_call_target="tpu_custom_call", output_to_operand_aliasing={{}: (7, {})} | custom-call | flops 4294967296 | bytes 18874368 | tf_op jit(solution)/shard_map/pallas_call | solution.py:47
  383.6 33.0 %collective-permute-done.12.refs_7_ = bf16[256,4096]{1,0:T(8,128)(2,1)} collective-permute-done((bf16[256,4096]{1,0:T(8,128)(2,1)}, bf16[256,4096]{1,0:T(8,128)(2,1)}, u32[]{:S(2)}, u32[]{:S(2)}) %collective-permute-start.12) | collective-permute-done | bytes 2097184 | tf_op jit(solution)/shard_map/ppermute | solution.py:192
  419.1 10.5 %shard_map.37.refs_8_ = bf16[1536,8192]{1,0:T(8,128)(2,1)} custom-call(bf16[1536,1536]{1,0:T(8,128)(2,1)S(1)} %get-tuple-element.75.refs_0_, bf16[1536,1536]{1,0:T(8,128)(2,1)S(1)} %get-tuple-element.76.refs_1_.l_ref, bf16[1536,8192]{1,0:T(8,128)(2,1)} %refs_2_.23, bf16[256,4096]{1,0:T(8,128)(2,1)} %collective-permute-done.8.refs_3_, ...), custom_call_target="tpu_custom_call", output_to_operand_aliasing={{}: (8, {})} | custom-call | flops 5368709120 | bytes 23068672 | tf_op jit(solution)/shard_map/pallas_call | solution.py:47
  429.6 31.9 %collective-permute-done.7.refs_7_ = bf16[256,4096]{1,0:T(8,128)(2,1)} collective-permute-done((bf16[256,4096]{1,0:T(8,128)(2,1)}, bf16[256,4096]{1,0:T(8,128)(2,1)}, u32[]{:S(2)}, u32[]{:S(2)}) %collective-permute-start.7) | collective-permute-done | bytes 2097184 | tf_op jit(solution)/shard_map/ppermute | solution.py:192
  461.5 10.1 %shard_map.38.refs_8_ = bf16[1536,8192]{1,0:T(8,128)(2,1)} custom-call(bf16[1536,1536]{1,0:T(8,128)(2,1)S(1)} %get-tuple-element.75.refs_0_, bf16[1536,1536]{1,0:T(8,128)(2,1)S(1)} %get-tuple-element.76.refs_1_.l_ref, bf16[1536,8192]{1,0:T(8,128)(2,1)} %refs_2_.23, bf16[256,4096]{1,0:T(8,128)(2,1)S(1)} %copy-done.1, ...), custom_call_target="tpu_custom_call", output_to_operand_aliasing={{}: (8, {})} | custom-call | flops 5368709120 | bytes 23068672 | tf_op jit(solution)/shard_map/pallas_call | solution.py:47
  471.6 11.3 %shard_map.39 = (bf16[1536,8192]{1,0:T(8,128)(2,1)}, f32[256,4096]{1,0:T(8,128)S(1)}) custom-call(bf16[1536,1536]{1,0:T(8,128)(2,1)S(1)} %get-tuple-element.75.refs_0_, bf16[1536,1536]{1,0:T(8,128)(2,1)S(1)} %get-tuple-element.76.refs_1_.l_ref, bf16[1536,8192]{1,0:T(8,128)(2,1)} %refs_2_.23, ...), custom_call_target="tpu_custom_call", output_to_operand_aliasing={{0}: (8, {})} | custom-call | flops 5905580032 | bytes 25165824 | tf_op jit(solution)/shard_map/pallas_call | solution.py:47
  483.0 11.0 %shard_map.40 = (bf16[1536,8192]{1,0:T(8,128)(2,1)}, f32[256,4096]{1,0:T(8,128)S(1)}) custom-call(bf16[1536,1536]{1,0:T(8,128)(2,1)S(1)} %get-tuple-element.75.refs_0_, bf16[1536,1536]{1,0:T(8,128)(2,1)S(1)} %get-tuple-element.76.refs_1_.l_ref, bf16[1536,8192]{1,0:T(8,128)(2,1)} %refs_2_.23, ...), custom_call_target="tpu_custom_call", output_to_operand_aliasing={{0}: (8, {})} | custom-call | flops 5905580032 | bytes 25165824 | tf_op jit(solution)/shard_map/pallas_call | solution.py:47
  497.4 12.6 %collective-permute-done.16.b_ref = bf16[256,4096]{1,0:T(8,128)(2,1)} collective-permute-done((bf16[256,4096]{1,0:T(8,128)(2,1)}, bf16[256,4096]{1,0:T(8,128)(2,1)}, u32[]{:S(2)}, u32[]{:S(2)}) %collective-permute-start.16) | collective-permute-done | bytes 2097184 | tf_op jit(solution)/shard_map/ppermute | solution.py:192
  510.1 22.4 %collective-permute-done.15.b_ref = bf16[256,2048]{1,0:T(8,128)(2,1)} collective-permute-done((bf16[256,2048]{1,0:T(8,128)(2,1)}, bf16[256,2048]{1,0:T(8,128)(2,1)}, u32[]{:S(2)}, u32[]{:S(2)}) %collective-permute-start.15) | collective-permute-done | bytes 1048608 | tf_op jit(solution)/shard_map/ppermute | solution.py:192
  532.5 11.1 %collective-permute-done.14.b_ref = bf16[256,1024]{1,0:T(8,128)(2,1)S(1)} collective-permute-done((bf16[256,1024]{1,0:T(8,128)(2,1)S(1)}, bf16[256,1024]{1,0:T(8,128)(2,1)S(1)}, u32[]{:S(2)}, u32[]{:S(2)}) %collective-permute-start.14) | collective-permute-done | bytes 524320 | tf_op jit(solution)/shard_map/ppermute | solution.py:192
  543.7 4.6 collective-permute-done.13.b_ref
  (72 shorter events, 59.7 us)
Async XLA Ops:
  0.0 46.0 %collective-permute-start = (bf16[1536,768]{1,0:T(8,128)(2,1)}, bf16[1536,768]{1,0:T(8,128)(2,1)}, u32[]{:S(2)}, u32[]{:S(2)}) collective-permute-start(bf16[1536,768]{1,0:T(8,128)(2,1)} %param.2), channel_id=1, source_target_pairs={{0,1},{1,0},{2,3},{3,2},{4,5},{5,4},{6,7},{7,6}} | collective-permute-start | bytes 7077896 | tf_op jit(solution)/shard_map/ppermute | solution.py:199
  0.8 54.5 %collective-permute-start.1 = (bf16[1536,768]{1,0:T(8,128)(2,1)}, bf16[1536,768]{1,0:T(8,128)(2,1)}, u32[]{:S(2)}, u32[]{:S(2)}) collective-permute-start(bf16[1536,768]{1,0:T(8,128)(2,1)} %param.2), channel_id=1, source_target_pairs={{0,3},{1,2},{2,1},{3,0},{4,7},{5,6},{6,5},{7,4}} | collective-permute-start | bytes 7077896 | tf_op jit(solution)/shard_map/ppermute | solution.py:199
  3.4 102.7 %collective-permute-start.2 = (bf16[1536,768]{1,0:T(8,128)(2,1)}, bf16[1536,768]{1,0:T(8,128)(2,1)}, u32[]{:S(2)}, u32[]{:S(2)}) collective-permute-start(bf16[1536,768]{1,0:T(8,128)(2,1)} %param.2), channel_id=1, source_target_pairs={{0,2},{1,3},{2,0},{3,1},{4,6},{5,7},{6,4},{7,5}} | collective-permute-start | bytes 7077896 | tf_op jit(solution)/shard_map/ppermute | solution.py:199
  8.2 102.0 %collective-permute-start.8 = (bf16[256,4096]{1,0:T(8,128)(2,1)}, bf16[256,4096]{1,0:T(8,128)(2,1)}, u32[]{:S(2)}, u32[]{:S(2)}) collective-permute-start(bf16[256,4096]{1,0:T(8,128)(2,1)} %slice.97), channel_id=1, source_target_pairs={{0,4},{4,0},{1,5},{5,1},{2,6},{6,2},{3,7},{7,3}} | collective-permute-start | bytes 6291464 | tf_op jit(solution)/shard_map/ppermute | solution.py:192
  11.8 98.8 %collective-permute-start.3 = (bf16[256,4096]{1,0:T(8,128)(2,1)}, bf16[256,4096]{1,0:T(8,128)(2,1)S(1)}, u32[]{:S(2)}, u32[]{:S(2)}) collective-permute-start(bf16[256,4096]{1,0:T(8,128)(2,1)} %slice.98), channel_id=1, source_target_pairs={{0,4},{4,0},{1,5},{5,1},{2,6},{6,2},{3,7},{7,3}} | collective-permute-start | bytes 6291464 | tf_op jit(solution)/shard_map/ppermute | solution.py:192
  46.0 100.8 %collective-permute-start.9 = (bf16[256,4096]{1,0:T(8,128)(2,1)}, bf16[256,4096]{1,0:T(8,128)(2,1)S(1)}, u32[]{:S(2)}, u32[]{:S(2)}) collective-permute-start(bf16[256,4096]{1,0:T(8,128)(2,1)} %slice.99), channel_id=1, source_target_pairs={{0,4},{4,0},{1,5},{5,1},{2,6},{6,2},{3,7},{7,3}} | collective-permute-start | bytes 6291464 | tf_op jit(solution)/shard_map/ppermute | solution.py:192
  55.4 136.4 %collective-permute-start.4 = (bf16[256,4096]{1,0:T(8,128)(2,1)}, bf16[256,4096]{1,0:T(8,128)(2,1)S(1)}, u32[]{:S(2)}, u32[]{:S(2)}) collective-permute-start(bf16[256,4096]{1,0:T(8,128)(2,1)} %slice.100), channel_id=1, source_target_pairs={{0,4},{4,0},{1,5},{5,1},{2,6},{6,2},{3,7},{7,3}} | collective-permute-start | bytes 6291464 | tf_op jit(solution)/shard_map/ppermute | solution.py:192
  59.6 48.2 %copy-start.8 = (bf16[1536,768]{1,0:T(8,128)(2,1)S(1)}, bf16[1536,768]{1,0:T(8,128)(2,1)}, u32[]{:S(2)}) copy-start(bf16[1536,768]{1,0:T(8,128)(2,1)} %param.2) | copy-start | bytes 7077892
  106.1 130.7 %collective-permute-start.10 = (bf16[256,4096]{1,0:T(8,128)(2,1)}, bf16[256,4096]{1,0:T(8,128)(2,1)}, u32[]{:S(2)}, u32[]{:S(2)}) collective-permute-start(bf16[256,4096]{1,0:T(8,128)(2,1)} %slice.101), channel_id=1, source_target_pairs={{0,4},{4,0},{1,5},{5,1},{2,6},{6,2},{3,7},{7,3}} | collective-permute-start | bytes 6291464 | tf_op jit(solution)/shard_map/ppermute | solution.py:192
  110.2 83.4 %copy-start.6 = (bf16[1536,1536]{1,0:T(8,128)(2,1)}, bf16[1536,1536]{1,0:T(8,128)(2,1)S(1)}, u32[]{:S(2)}) copy-start(bf16[1536,1536]{1,0:T(8,128)(2,1)S(1)} %get-tuple-element.82) | copy-start | bytes 14155780
  110.2 83.4 %copy-start.7 = (bf16[1536,1536]{1,0:T(8,128)(2,1)}, bf16[1536,1536]{1,0:T(8,128)(2,1)S(1)}, u32[]{:S(2)}) copy-start(bf16[1536,1536]{1,0:T(8,128)(2,1)S(1)} %get-tuple-element.81) | copy-start | bytes 14155780
  110.2 171.5 %collective-permute-start.5 = (bf16[256,4096]{1,0:T(8,128)(2,1)}, bf16[256,4096]{1,0:T(8,128)(2,1)}, u32[]{:S(2)}, u32[]{:S(2)}) collective-permute-start(bf16[256,4096]{1,0:T(8,128)(2,1)} %slice.102), channel_id=1, source_target_pairs={{0,4},{4,0},{1,5},{5,1},{2,6},{6,2},{3,7},{7,3}} | collective-permute-start | bytes 6291464 | tf_op jit(solution)/shard_map/ppermute | solution.py:192
  110.6 1.6 copy-start
  112.2 214.5 %collective-permute-start.11 = (bf16[256,4096]{1,0:T(8,128)(2,1)}, bf16[256,4096]{1,0:T(8,128)(2,1)}, u32[]{:S(2)}, u32[]{:S(2)}) collective-permute-start(bf16[256,4096]{1,0:T(8,128)(2,1)} %slice.103), channel_id=1, source_target_pairs={{0,4},{4,0},{1,5},{5,1},{2,6},{6,2},{3,7},{7,3}} | collective-permute-start | bytes 6291464 | tf_op jit(solution)/shard_map/ppermute | solution.py:192
  146.8 1.3 copy-start.4
  148.1 223.5 %collective-permute-start.6 = (bf16[256,4096]{1,0:T(8,128)(2,1)}, bf16[256,4096]{1,0:T(8,128)(2,1)}, u32[]{:S(2)}, u32[]{:S(2)}) collective-permute-start(bf16[256,4096]{1,0:T(8,128)(2,1)} %slice.104), channel_id=1, source_target_pairs={{0,4},{4,0},{1,5},{5,1},{2,6},{6,2},{3,7},{7,3}} | collective-permute-start | bytes 6291464 | tf_op jit(solution)/shard_map/ppermute | solution.py:192
  191.8 1.4 copy-start.2
  193.1 223.5 %collective-permute-start.12 = (bf16[256,4096]{1,0:T(8,128)(2,1)}, bf16[256,4096]{1,0:T(8,128)(2,1)}, u32[]{:S(2)}, u32[]{:S(2)}) collective-permute-start(bf16[256,4096]{1,0:T(8,128)(2,1)} %slice.105), channel_id=1, source_target_pairs={{0,4},{4,0},{1,5},{5,1},{2,6},{6,2},{3,7},{7,3}} | collective-permute-start | bytes 6291464 | tf_op jit(solution)/shard_map/ppermute | solution.py:192
  197.9 5.1 copy-start.1
  203.1 4.8 copy-start.5
  207.8 29.4 %copy-start.3 = (bf16[256,4096]{1,0:T(8,128)(2,1)S(1)}, bf16[256,4096]{1,0:T(8,128)(2,1)}, u32[]{:S(2)}) copy-start(bf16[256,4096]{1,0:T(8,128)(2,1)} %copy-done.2) | copy-start | bytes 6291460
  236.8 224.7 %collective-permute-start.7 = (bf16[256,4096]{1,0:T(8,128)(2,1)}, bf16[256,4096]{1,0:T(8,128)(2,1)}, u32[]{:S(2)}, u32[]{:S(2)}) collective-permute-start(bf16[256,4096]{1,0:T(8,128)(2,1)} %slice.106), channel_id=1, source_target_pairs={{0,4},{4,0},{1,5},{5,1},{2,6},{6,2},{3,7},{7,3}} | collective-permute-start | bytes 6291464 | tf_op jit(solution)/shard_map/ppermute | solution.py:192
  281.8 215.6 %collective-permute-start.17 = (bf16[256,512]{1,0:T(8,128)(2,1)}, bf16[256,512]{1,0:T(8,128)(2,1)}, u32[]{:S(2)}, u32[]{:S(2)}) collective-permute-start(bf16[256,512]{1,0:T(8,128)(2,1)} %shard_map.28), channel_id=1, source_target_pairs={{0,4},{4,0},{1,5},{5,1},{2,6},{6,2},{3,7},{7,3}} | collective-permute-start | bytes 786440 | tf_op jit(solution)/shard_map/ppermute | solution.py:192
  326.7 183.3 %collective-permute-start.16 = (bf16[256,4096]{1,0:T(8,128)(2,1)}, bf16[256,4096]{1,0:T(8,128)(2,1)}, u32[]{:S(2)}, u32[]{:S(2)}) collective-permute-start(bf16[256,4096]{1,0:T(8,128)(2,1)} %slice.107), channel_id=1, source_target_pairs={{0,4},{1,5},{2,6},{3,7}} | collective-permute-start | bytes 6291464 | tf_op jit(solution)/shard_map/ppermute | solution.py:192
  339.4 77.2 %copy-start.9 = (bf16[256,1024]{1,0:T(8,128)(2,1)S(1)}, bf16[256,1024]{1,0:T(8,128)(2,1)}, u32[]{:S(2)}) copy-start(bf16[256,1024]{1,0:T(8,128)(2,1)} %slice.109) | copy-start | bytes 1572868
  371.6 160.9 %collective-permute-start.15 = (bf16[256,2048]{1,0:T(8,128)(2,1)}, bf16[256,2048]{1,0:T(8,128)(2,1)}, u32[]{:S(2)}, u32[]{:S(2)}) collective-permute-start(bf16[256,2048]{1,0:T(8,128)(2,1)} %slice.108), channel_id=1, source_target_pairs={{0,4},{1,5},{2,6},{3,7}} | collective-permute-start | bytes 3145736 | tf_op jit(solution)/shard_map/ppermute | solution.py:192
  416.6 127.0 %collective-permute-start.14 = (bf16[256,1024]{1,0:T(8,128)(2,1)S(1)}, bf16[256,1024]{1,0:T(8,128)(2,1)S(1)}, u32[]{:S(2)}, u32[]{:S(2)}) collective-permute-start(bf16[256,1024]{1,0:T(8,128)(2,1)S(1)} %copy-done.9), channel_id=1, source_target_pairs={{0,4},{1,5},{2,6},{3,7}} | collective-permute-start | bytes 1572872 | tf_op jit(solution)/shard_map/ppermute | solution.py:192
  494.9 53.3 %collective-permute-start.13 = (bf16[256,512]{1,0:T(8,128)(2,1)S(1)}, bf16[256,512]{1,0:T(8,128)(2,1)S(1)}, u32[]{:S(2)}, u32[]{:S(2)}) collective-permute-start(bf16[256,512]{1,0:T(8,128)(2,1)S(1)} %slice.110), channel_id=1, source_target_pairs={{0,4},{1,5},{2,6},{3,7}} | collective-permute-start | bytes 786440 | tf_op jit(solution)/shard_map/ppermute | solution.py:192

commit v4 on v3

--- a/solution.py
+++ b/solution.py
@@ -134,27 +134,44 @@
     )(l_last, piece, acc, x)
 
 
-def cut_kernel(row, start, b_ref, out_ref, buf, sems):
+def cut_kernel(row, start, b_ref, out_ref, sem):
     @pl.when(lax.axis_index("row") == 0)
     def _():
-        fetch = pltpu.make_async_copy(b_ref.at[pl.ds(row, BLOCK), pl.ds(start, buf.shape[1])], buf, sems.at[0])
-        fetch.start()
-        fetch.wait()
-        store = pltpu.make_async_copy(buf, out_ref, sems.at[1])
-        store.start()
-        store.wait()
+        copy = pltpu.make_async_copy(b_ref.at[pl.ds(row, BLOCK), pl.ds(start, out_ref.shape[1])], out_ref, sem)
+        copy.start()
+        copy.wait()
 
 
 def cut(b, row, start, width):
     return pl.pallas_call(
         functools.partial(cut_kernel, row, start),
         in_specs=[pl.BlockSpec(memory_space=pltpu.HBM)],
-        out_specs=pl.BlockSpec(memory_space=pltpu.HBM),
+        out_specs=pl.BlockSpec(memory_space=pl.ANY),
         out_shape=jax.ShapeDtypeStruct((BLOCK, width), b.dtype),
-        scratch_shapes=[pltpu.VMEM((BLOCK, width), b.dtype), pltpu.SemaphoreType.DMA((2,))],
-        compiler_params=pltpu.CompilerParams(vmem_limit_bytes=60 << 20),
+        scratch_shapes=[pltpu.SemaphoreType.DMA],
+        compiler_params=pltpu.CompilerParams(vmem_limit_bytes=48 << 20),
         cost_estimate=pl.CostEstimate(flops=2 * BLOCK * width, bytes_accessed=BLOCK * width * 4, transcendentals=0),
     )(b)
+
+
+def keep_kernel(row, piece_ref, out_ref, sem):
+    @pl.when(lax.axis_index("row") == row)
+    def _():
+        copy = pltpu.make_async_copy(piece_ref, out_ref, sem)
+        copy.start()
+        copy.wait()
+
+
+def keep(row, piece):
+    return pl.pallas_call(
+        functools.partial(keep_kernel, row),
+        in_specs=[pl.BlockSpec(memory_space=pltpu.VMEM)],
+        out_specs=pl.BlockSpec(memory_space=pltpu.HBM),
+        out_shape=jax.ShapeDtypeStruct(piece.shape, piece.dtype),
+        scratch_shapes=[pltpu.SemaphoreType.DMA],
+        compiler_params=pltpu.CompilerParams(vmem_limit_bytes=1 << 20),
+        cost_estimate=pl.CostEstimate(flops=2 * piece.size, bytes_accessed=4 * piece.size, transcendentals=0),
+    )(piece)
 
 
 def weave(even, odd):
@@ -195,6 +212,7 @@
         source = rhs_loc
         for i in range(len(order) - 1):
             source = send(i, source)
+        got[final, cols - first] = keep(grid_rows - 1, got[final, cols - first])
         l_core, l_chip, l_both = (
             lax.ppermute(tri_loc, "col", [(c, c ^ d) for c in range(grid_cols)]) for d in (1, 2, 3))
         p = lax.axis_index("row")

time: 550 us -> 557 us (1.013)
  Pallas kernels: 99.1 us -> 107 us
    ppermute x15, waiting for transfers between devices: 315 us -> 325 us  [send(): lax.ppermute(piece, 'row', down_row if i and j == final else swap_row)]
    pallas_call x1, Pallas kernels: 1.65 us -> 9.05 us  [cut(): pl.pallas_call(functools.partial(cut_kernel, row, start), in_specs=[pl.Bl...]
    ppermute x3, waiting for transfers between devices: 55.1 us -> 48.1 us  [local_trmm(): lax.ppermute(tri_loc, 'col', [(c, c ^ d) for c in range(grid_cols)])]
  transfers between devices with their start and end apart: 18 -> 18, of which waited for: 14 -> 14; matrix products, arithmetic and copies ran while one was open for 9% -> 9% of each run, Pallas kernels for 18% -> 19%
where the time goes in v4:
time: 557 us; the launch traced here: 556 us
  waiting for transfers between devices  373 us (67%)
  Pallas kernels  107 us (19%)
  local copies, waits for them, and re-layouts  44.9 us (8%)
  starting transfers between devices  21.1 us (4%)
  other arithmetic  9.05 us (2%)
    ppermute x15, waiting for transfers between devices, send(): lax.ppermute(piece, 'row', down_row if i and j == final else swap_row)  325 us
    pallas_call x12, Pallas kernels, row_block(): pl.pallas_call(functools.partial(block_kernel, count, len(aliases)), grid...  97.3 us
    ppermute x3, waiting for transfers between devices, local_trmm(): lax.ppermute(tri_loc, 'col', [(c, c ^ d) for c in range(grid_cols)])  48.1 us
    slice x14, local copies, waits for them, and re-layouts, send(): source[j * BLOCK:(j + 1) * BLOCK, off:off + w]  39.9 us
    ppermute x15, starting transfers between devices, send(): lax.ppermute(piece, 'row', down_row if i and j == final else swap_row)  17.7 us
  transfers between devices with their start and end apart: 18, of which 14 were waited for; matrix products, arithmetic and copies ran while one was open for 9% of the time, Pallas kernels for 19%

profile of v4, /device:TPU:0, one launch (start us, length us, event | category | flops | bytes accessed | tf_op | source)
XLA Modules:
  0.0 555.8 jit_solution(14514052689608665474)
XLA Ops:
  3.4 9.0 %shard_map.28 = bf16[256,512]{1,0:T(8,128)(2,1)} custom-call(bf16[1536,8192]{1,0:T(8,128)(2,1)} %refs_2_.23), custom_call_target="tpu_custom_call" | custom-call | flops 262144 | bytes 524288 | tf_op jit(solution)/shard_map/pallas_call | solution.py:146
  15.6 3.2 slice.98
  33.4 3.2 slice.103
  39.7 3.2 slice.105
  46.1 3.2 slice.107
  59.9 46.2 %collective-permute-done.2 = bf16[1536,768]{1,0:T(8,128)(2,1)} collective-permute-done((bf16[1536,768]{1,0:T(8,128)(2,1)}, bf16[1536,768]{1,0:T(8,128)(2,1)}, u32[]{:S(2)}, u32[]{:S(2)}) %collective-permute-start.2) | collective-permute-done | bytes 2359328 | tf_op jit(solution)/shard_map/ppermute | solution.py:217
  114.1 40.1 %collective-permute-done.9.refs_4_ = bf16[256,4096]{1,0:T(8,128)(2,1)S(1)} collective-permute-done((bf16[256,4096]{1,0:T(8,128)(2,1)}, bf16[256,4096]{1,0:T(8,128)(2,1)S(1)}, u32[]{:S(2)}, u32[]{:S(2)}) %collective-permute-start.9) | collective-permute-done | bytes 2097184 | tf_op jit(solution)/shard_map/ppermute | solution.py:209
  155.5 43.6 %collective-permute-done.4.refs_4_ = bf16[256,4096]{1,0:T(8,128)(2,1)S(1)} collective-permute-done((bf16[256,4096]{1,0:T(8,128)(2,1)}, bf16[256,4096]{1,0:T(8,128)(2,1)S(1)}, u32[]{:S(2)}, u32[]{:S(2)}) %collective-permute-start.4) | collective-permute-done | bytes 2097184 | tf_op jit(solution)/shard_map/ppermute | solution.py:209
  200.5 4.4 broadcast_select_fusion
  204.9 5.1 shard_map.29.refs_4_
  210.1 4.8 shard_map.30.refs_5_
  214.8 6.2 %shard_map.31.refs_5_ = bf16[1536,8192]{1,0:T(8,128)(2,1)} custom-call(bf16[1536,1536]{1,0:T(8,128)(2,1)S(1)} %get-tuple-element.75.refs_0_, bf16[1536,1536]{1,0:T(8,128)(2,1)S(1)} %get-tuple-element.76.refs_1_.l_ref, bf16[1536,8192]{1,0:T(8,128)(2,1)} %refs_2_.23, bf16[256,4096]{1,0:T(8,128)(2,1)} %collective-permute-done.8.refs_3_, ...), custom_call_target="tpu_custom_call", output_to_operand_aliasing={{}: (5, {})} | custom-call | flops 2147483648 | bytes 10485760 | tf_op jit(solution)/shard_map/pallas_call | solution.py:47
  221.0 23.2 %collective-permute-done.10.refs_5_ = bf16[256,4096]{1,0:T(8,128)(2,1)} collective-permute-done((bf16[256,4096]{1,0:T(8,128)(2,1)}, bf16[256,4096]{1,0:T(8,128)(2,1)}, u32[]{:S(2)}, u32[]{:S(2)}) %collective-permute-start.10) | collective-permute-done | bytes 2097184 | tf_op jit(solution)/shard_map/ppermute | solution.py:209
  244.2 5.8 %shard_map.32.refs_6_ = bf16[1536,8192]{1,0:T(8,128)(2,1)} custom-call(bf16[1536,1536]{1,0:T(8,128)(2,1)S(1)} %get-tuple-element.75.refs_0_, bf16[1536,1536]{1,0:T(8,128)(2,1)S(1)} %get-tuple-element.76.refs_1_.l_ref, bf16[1536,8192]{1,0:T(8,128)(2,1)} %refs_2_.23, bf16[256,4096]{1,0:T(8,128)(2,1)S(1)} %copy-done.1, ...), custom_call_target="tpu_custom_call", output_to_operand_aliasing={{}: (5, {})} | custom-call | flops 2147483648 | bytes 10485760 | tf_op jit(solution)/shard_map/pallas_call | solution.py:47
  250.0 7.6 %shard_map.33.refs_6_ = bf16[1536,8192]{1,0:T(8,128)(2,1)} custom-call(bf16[1536,1536]{1,0:T(8,128)(2,1)S(1)} %get-tuple-element.75.refs_0_, bf16[1536,1536]{1,0:T(8,128)(2,1)S(1)} %get-tuple-element.76.refs_1_.l_ref, bf16[1536,8192]{1,0:T(8,128)(2,1)} %refs_2_.23, bf16[256,4096]{1,0:T(8,128)(2,1)} %collective-permute-done.8.refs_3_, ...), custom_call_target="tpu_custom_call", output_to_operand_aliasing={{}: (6, {})} | custom-call | flops 3221225472 | bytes 14680064 | tf_op jit(solution)/shard_map/pallas_call | solution.py:47
  257.6 31.6 %collective-permute-done.5.refs_5_ = bf16[256,4096]{1,0:T(8,128)(2,1)} collective-permute-done((bf16[256,4096]{1,0:T(8,128)(2,1)}, bf16[256,4096]{1,0:T(8,128)(2,1)}, u32[]{:S(2)}, u32[]{:S(2)}) %collective-permute-start.5) | collective-permute-done | bytes 2097184 | tf_op jit(solution)/shard_map/ppermute | solution.py:209
  289.2 7.2 %shard_map.34.refs_7_ = bf16[1536,8192]{1,0:T(8,128)(2,1)} custom-call(bf16[1536,1536]{1,0:T(8,128)(2,1)S(1)} %get-tuple-element.75.refs_0_, bf16[1536,1536]{1,0:T(8,128)(2,1)S(1)} %get-tuple-element.76.refs_1_.l_ref, bf16[1536,8192]{1,0:T(8,128)(2,1)} %refs_2_.23, bf16[256,4096]{1,0:T(8,128)(2,1)S(1)} %copy-done.1, ...), custom_call_target="tpu_custom_call", output_to_operand_aliasing={{}: (6, {})} | custom-call | flops 3221225472 | bytes 14680064 | tf_op jit(solution)/shard_map/pallas_call | solution.py:47
  296.4 37.7 %collective-permute-done.11.refs_6_ = bf16[256,4096]{1,0:T(8,128)(2,1)} collective-permute-done((bf16[256,4096]{1,0:T(8,128)(2,1)}, bf16[256,4096]{1,0:T(8,128)(2,1)}, u32[]{:S(2)}, u32[]{:S(2)}) %collective-permute-start.11) | collective-permute-done | bytes 2097184 | tf_op jit(solution)/shard_map/ppermute | solution.py:209
  334.1 3.3 collective-permute-start.16
  337.4 9.0 %shard_map.35.refs_7_ = bf16[1536,8192]{1,0:T(8,128)(2,1)} custom-call(bf16[1536,1536]{1,0:T(8,128)(2,1)S(1)} %get-tuple-element.75.refs_0_, bf16[1536,1536]{1,0:T(8,128)(2,1)S(1)} %get-tuple-element.76.refs_1_.l_ref, bf16[1536,8192]{1,0:T(8,128)(2,1)} %refs_2_.23, bf16[256,4096]{1,0:T(8,128)(2,1)} %collective-permute-done.8.refs_3_, ...), custom_call_target="tpu_custom_call", output_to_operand_aliasing={{}: (7, {})} | custom-call | flops 4294967296 | bytes 18874368 | tf_op jit(solution)/shard_map/pallas_call | solution.py:47
  346.4 32.6 %collective-permute-done.6.refs_6_ = bf16[256,4096]{1,0:T(8,128)(2,1)} collective-permute-done((bf16[256,4096]{1,0:T(8,128)(2,1)}, bf16[256,4096]{1,0:T(8,128)(2,1)}, u32[]{:S(2)}, u32[]{:S(2)}) %collective-permute-start.6) | collective-permute-done | bytes 2097184 | tf_op jit(solution)/shard_map/ppermute | solution.py:209
  381.9 8.7 %shard_map.36.refs_8_ = bf16[1536,8192]{1,0:T(8,128)(2,1)} custom-call(bf16[1536,1536]{1,0:T(8,128)(2,1)S(1)} %get-tuple-element.75.refs_0_, bf16[1536,1536]{1,0:T(8,128)(2,1)S(1)} %get-tuple-element.76.refs_1_.l_ref, bf16[1536,8192]{1,0:T(8,128)(2,1)} %refs_2_.23, bf16[256,4096]{1,0:T(8,128)(2,1)S(1)} %copy-done.1, ...), custom_call_target="tpu_custom_call", output_to_operand_aliasing={{}: (7, {})} | custom-call | flops 4294967296 | bytes 18874368 | tf_op jit(solution)/shard_map/pallas_call | solution.py:47
  390.6 33.4 %collective-permute-done.12.refs_7_ = bf16[256,4096]{1,0:T(8,128)(2,1)} collective-permute-done((bf16[256,4096]{1,0:T(8,128)(2,1)}, bf16[256,4096]{1,0:T(8,128)(2,1)}, u32[]{:S(2)}, u32[]{:S(2)}) %collective-permute-start.12) | collective-permute-done | bytes 2097184 | tf_op jit(solution)/shard_map/ppermute | solution.py:209
  426.1 10.5 %shard_map.37.refs_8_ = bf16[1536,8192]{1,0:T(8,128)(2,1)} custom-call(bf16[1536,1536]{1,0:T(8,128)(2,1)S(1)} %get-tuple-element.75.refs_0_, bf16[1536,1536]{1,0:T(8,128)(2,1)S(1)} %get-tuple-element.76.refs_1_.l_ref, bf16[1536,8192]{1,0:T(8,128)(2,1)} %refs_2_.23, bf16[256,4096]{1,0:T(8,128)(2,1)} %collective-permute-done.8.refs_3_, ...), custom_call_target="tpu_custom_call", output_to_operand_aliasing={{}: (8, {})} | custom-call | flops 5368709120 | bytes 23068672 | tf_op jit(solution)/shard_map/pallas_call | solution.py:47
  436.6 32.3 %collective-permute-done.7.refs_7_ = bf16[256,4096]{1,0:T(8,128)(2,1)} collective-permute-done((bf16[256,4096]{1,0:T(8,128)(2,1)}, bf16[256,4096]{1,0:T(8,128)(2,1)}, u32[]{:S(2)}, u32[]{:S(2)}) %collective-permute-start.7) | collective-permute-done | bytes 2097184 | tf_op jit(solution)/shard_map/ppermute | solution.py:209
  468.9 10.1 %shard_map.38.refs_8_ = bf16[1536,8192]{1,0:T(8,128)(2,1)} custom-call(bf16[1536,1536]{1,0:T(8,128)(2,1)S(1)} %get-tuple-element.75.refs_0_, bf16[1536,1536]{1,0:T(8,128)(2,1)S(1)} %get-tuple-element.76.refs_1_.l_ref, bf16[1536,8192]{1,0:T(8,128)(2,1)} %refs_2_.23, bf16[256,4096]{1,0:T(8,128)(2,1)S(1)} %copy-done.1, ...), custom_call_target="tpu_custom_call", output_to_operand_aliasing={{}: (8, {})} | custom-call | flops 5368709120 | bytes 23068672 | tf_op jit(solution)/shard_map/pallas_call | solution.py:47
  479.0 11.3 %shard_map.39 = (bf16[1536,8192]{1,0:T(8,128)(2,1)}, f32[256,4096]{1,0:T(8,128)S(1)}) custom-call(bf16[1536,1536]{1,0:T(8,128)(2,1)S(1)} %get-tuple-element.75.refs_0_, bf16[1536,1536]{1,0:T(8,128)(2,1)S(1)} %get-tuple-element.76.refs_1_.l_ref, bf16[1536,8192]{1,0:T(8,128)(2,1)} %refs_2_.23, ...), custom_call_target="tpu_custom_call", output_to_operand_aliasing={{0}: (8, {})} | custom-call | flops 5905580032 | bytes 25165824 | tf_op jit(solution)/shard_map/pallas_call | solution.py:47
  490.3 11.0 %shard_map.40 = (bf16[1536,8192]{1,0:T(8,128)(2,1)}, f32[256,4096]{1,0:T(8,128)S(1)}) custom-call(bf16[1536,1536]{1,0:T(8,128)(2,1)S(1)} %get-tuple-element.75.refs_0_, bf16[1536,1536]{1,0:T(8,128)(2,1)S(1)} %get-tuple-element.76.refs_1_.l_ref, bf16[1536,8192]{1,0:T(8,128)(2,1)} %refs_2_.23, ...), custom_call_target="tpu_custom_call", output_to_operand_aliasing={{0}: (8, {})} | custom-call | flops 5905580032 | bytes 25165824 | tf_op jit(solution)/shard_map/pallas_call | solution.py:47
  505.4 11.6 %collective-permute-done.16.b_ref = bf16[256,4096]{1,0:T(8,128)(2,1)} collective-permute-done((bf16[256,4096]{1,0:T(8,128)(2,1)}, bf16[256,4096]{1,0:T(8,128)(2,1)}, u32[]{:S(2)}, u32[]{:S(2)}) %collective-permute-start.16) | collective-permute-done | bytes 2097184 | tf_op jit(solution)/shard_map/ppermute | solution.py:209
  517.0 22.4 %collective-permute-done.15.b_ref = bf16[256,2048]{1,0:T(8,128)(2,1)} collective-permute-done((bf16[256,2048]{1,0:T(8,128)(2,1)}, bf16[256,2048]{1,0:T(8,128)(2,1)}, u32[]{:S(2)}, u32[]{:S(2)}) %collective-permute-start.15) | collective-permute-done | bytes 1048608 | tf_op jit(solution)/shard_map/ppermute | solution.py:209
  539.5 11.1 %collective-permute-done.14.b_ref = bf16[256,1024]{1,0:T(8,128)(2,1)S(1)} collective-permute-done((bf16[256,1024]{1,0:T(8,128)(2,1)S(1)}, bf16[256,1024]{1,0:T(8,128)(2,1)S(1)}, u32[]{:S(2)}, u32[]{:S(2)}) %collective-permute-start.14) | collective-permute-done | bytes 524320 | tf_op jit(solution)/shard_map/ppermute | solution.py:209
  550.6 5.0 collective-permute-done.13.b_ref
  (73 shorter events, 57.8 us)
Async XLA Ops:
  0.0 53.4 %collective-permute-start = (bf16[1536,768]{1,0:T(8,128)(2,1)}, bf16[1536,768]{1,0:T(8,128)(2,1)}, u32[]{:S(2)}, u32[]{:S(2)}) collective-permute-start(bf16[1536,768]{1,0:T(8,128)(2,1)} %param.2), channel_id=1, source_target_pairs={{0,1},{1,0},{2,3},{3,2},{4,5},{5,4},{6,7},{7,6}} | collective-permute-start | bytes 7077896 | tf_op jit(solution)/shard_map/ppermute | solution.py:217
  0.8 54.5 %collective-permute-start.1 = (bf16[1536,768]{1,0:T(8,128)(2,1)}, bf16[1536,768]{1,0:T(8,128)(2,1)}, u32[]{:S(2)}, u32[]{:S(2)}) collective-permute-start(bf16[1536,768]{1,0:T(8,128)(2,1)} %param.2), channel_id=1, source_target_pairs={{0,3},{1,2},{2,1},{3,0},{4,7},{5,6},{6,5},{7,4}} | collective-permute-start | bytes 7077896 | tf_op jit(solution)/shard_map/ppermute | solution.py:217
  3.4 102.7 %collective-permute-start.2 = (bf16[1536,768]{1,0:T(8,128)(2,1)}, bf16[1536,768]{1,0:T(8,128)(2,1)}, u32[]{:S(2)}, u32[]{:S(2)}) collective-permute-start(bf16[1536,768]{1,0:T(8,128)(2,1)} %param.2), channel_id=1, source_target_pairs={{0,2},{1,3},{2,0},{3,1},{4,6},{5,7},{6,4},{7,5}} | collective-permute-start | bytes 7077896 | tf_op jit(solution)/shard_map/ppermute | solution.py:217
  15.6 94.6 %collective-permute-start.8 = (bf16[256,4096]{1,0:T(8,128)(2,1)}, bf16[256,4096]{1,0:T(8,128)(2,1)}, u32[]{:S(2)}, u32[]{:S(2)}) collective-permute-start(bf16[256,4096]{1,0:T(8,128)(2,1)} %slice.97), channel_id=1, source_target_pairs={{0,4},{4,0},{1,5},{5,1},{2,6},{6,2},{3,7},{7,3}} | collective-permute-start | bytes 6291464 | tf_op jit(solution)/shard_map/ppermute | solution.py:209
  18.8 91.8 %collective-permute-start.3 = (bf16[256,4096]{1,0:T(8,128)(2,1)}, bf16[256,4096]{1,0:T(8,128)(2,1)S(1)}, u32[]{:S(2)}, u32[]{:S(2)}) collective-permute-start(bf16[256,4096]{1,0:T(8,128)(2,1)} %slice.98), channel_id=1, source_target_pairs={{0,4},{4,0},{1,5},{5,1},{2,6},{6,2},{3,7},{7,3}} | collective-permute-start | bytes 6291464 | tf_op jit(solution)/shard_map/ppermute | solution.py:209
  53.4 100.8 %collective-permute-start.9 = (bf16[256,4096]{1,0:T(8,128)(2,1)}, bf16[256,4096]{1,0:T(8,128)(2,1)S(1)}, u32[]{:S(2)}, u32[]{:S(2)}) collective-permute-start(bf16[256,4096]{1,0:T(8,128)(2,1)} %slice.99), channel_id=1, source_target_pairs={{0,4},{4,0},{1,5},{5,1},{2,6},{6,2},{3,7},{7,3}} | collective-permute-start | bytes 6291464 | tf_op jit(solution)/shard_map/ppermute | solution.py:209
  55.4 143.8 %collective-permute-start.4 = (bf16[256,4096]{1,0:T(8,128)(2,1)}, bf16[256,4096]{1,0:T(8,128)(2,1)S(1)}, u32[]{:S(2)}, u32[]{:S(2)}) collective-permute-start(bf16[256,4096]{1,0:T(8,128)(2,1)} %slice.100), channel_id=1, source_target_pairs={{0,4},{4,0},{1,5},{5,1},{2,6},{6,2},{3,7},{7,3}} | collective-permute-start | bytes 6291464 | tf_op jit(solution)/shard_map/ppermute | solution.py:209
  59.6 48.2 %copy-start.8 = (bf16[1536,768]{1,0:T(8,128)(2,1)S(1)}, bf16[1536,768]{1,0:T(8,128)(2,1)}, u32[]{:S(2)}) copy-start(bf16[1536,768]{1,0:T(8,128)(2,1)} %param.2) | copy-start | bytes 7077892
  106.1 138.1 %collective-permute-start.10 = (bf16[256,4096]{1,0:T(8,128)(2,1)}, bf16[256,4096]{1,0:T(8,128)(2,1)}, u32[]{:S(2)}, u32[]{:S(2)}) collective-permute-start(bf16[256,4096]{1,0:T(8,128)(2,1)} %slice.101), channel_id=1, source_target_pairs={{0,4},{4,0},{1,5},{5,1},{2,6},{6,2},{3,7},{7,3}} | collective-permute-start | bytes 6291464 | tf_op jit(solution)/shard_map/ppermute | solution.py:209
  110.2 90.3 %copy-start.6 = (bf16[1536,1536]{1,0:T(8,128)(2,1)}, bf16[1536,1536]{1,0:T(8,128)(2,1)S(1)}, u32[]{:S(2)}) copy-start(bf16[1536,1536]{1,0:T(8,128)(2,1)S(1)} %get-tuple-element.82) | copy-start | bytes 14155780
  110.2 90.3 %copy-start.7 = (bf16[1536,1536]{1,0:T(8,128)(2,1)}, bf16[1536,1536]{1,0:T(8,128)(2,1)S(1)}, u32[]{:S(2)}) copy-start(bf16[1536,1536]{1,0:T(8,128)(2,1)S(1)} %get-tuple-element.81) | copy-start | bytes 14155780
  110.2 178.9 %collective-permute-start.5 = (bf16[256,4096]{1,0:T(8,128)(2,1)}, bf16[256,4096]{1,0:T(8,128)(2,1)}, u32[]{:S(2)}, u32[]{:S(2)}) collective-permute-start(bf16[256,4096]{1,0:T(8,128)(2,1)} %slice.102), channel_id=1, source_target_pairs={{0,4},{4,0},{1,5},{5,1},{2,6},{6,2},{3,7},{7,3}} | collective-permute-start | bytes 6291464 | tf_op jit(solution)/shard_map/ppermute | solution.py:209
  110.6 1.6 copy-start
  112.2 221.9 %collective-permute-start.11 = (bf16[256,4096]{1,0:T(8,128)(2,1)}, bf16[256,4096]{1,0:T(8,128)(2,1)}, u32[]{:S(2)}, u32[]{:S(2)}) collective-permute-start(bf16[256,4096]{1,0:T(8,128)(2,1)} %slice.103), channel_id=1, source_target_pairs={{0,4},{4,0},{1,5},{5,1},{2,6},{6,2},{3,7},{7,3}} | collective-permute-start | bytes 6291464 | tf_op jit(solution)/shard_map/ppermute | solution.py:209
  154.2 1.3 copy-start.4
  155.5 223.5 %collective-permute-start.6 = (bf16[256,4096]{1,0:T(8,128)(2,1)}, bf16[256,4096]{1,0:T(8,128)(2,1)}, u32[]{:S(2)}, u32[]{:S(2)}) collective-permute-start(bf16[256,4096]{1,0:T(8,128)(2,1)} %slice.104), channel_id=1, source_target_pairs={{0,4},{4,0},{1,5},{5,1},{2,6},{6,2},{3,7},{7,3}} | collective-permute-start | bytes 6291464 | tf_op jit(solution)/shard_map/ppermute | solution.py:209
  199.2 1.4 copy-start.2
  200.5 223.5 %collective-permute-start.12 = (bf16[256,4096]{1,0:T(8,128)(2,1)}, bf16[256,4096]{1,0:T(8,128)(2,1)}, u32[]{:S(2)}, u32[]{:S(2)}) collective-permute-start(bf16[256,4096]{1,0:T(8,128)(2,1)} %slice.105), channel_id=1, source_target_pairs={{0,4},{4,0},{1,5},{5,1},{2,6},{6,2},{3,7},{7,3}} | collective-permute-start | bytes 6291464 | tf_op jit(solution)/shard_map/ppermute | solution.py:209
  204.9 5.1 copy-start.1
  210.0 4.8 copy-start.5
  214.8 29.4 %copy-start.3 = (bf16[256,4096]{1,0:T(8,128)(2,1)S(1)}, bf16[256,4096]{1,0:T(8,128)(2,1)}, u32[]{:S(2)}) copy-start(bf16[256,4096]{1,0:T(8,128)(2,1)} %copy-done.2) | copy-start | bytes 6291460
  244.2 224.7 %collective-permute-start.7 = (bf16[256,4096]{1,0:T(8,128)(2,1)}, bf16[256,4096]{1,0:T(8,128)(2,1)}, u32[]{:S(2)}, u32[]{:S(2)}) collective-permute-start(bf16[256,4096]{1,0:T(8,128)(2,1)} %slice.106), channel_id=1, source_target_pairs={{0,4},{4,0},{1,5},{5,1},{2,6},{6,2},{3,7},{7,3}} | collective-permute-start | bytes 6291464 | tf_op jit(solution)/shard_map/ppermute | solution.py:209
  289.1 215.1 %collective-permute-start.17 = (bf16[256,512]{1,0:T(8,128)(2,1)}, bf16[256,512]{1,0:T(8,128)(2,1)}, u32[]{:S(2)}, u32[]{:S(2)}) collective-permute-start(bf16[256,512]{1,0:T(8,128)(2,1)} %shard_map.28), channel_id=1, source_target_pairs={{0,4},{4,0},{1,5},{5,1},{2,6},{6,2},{3,7},{7,3}} | collective-permute-start | bytes 786440 | tf_op jit(solution)/shard_map/ppermute | solution.py:209
  334.1 182.9 %collective-permute-start.16 = (bf16[256,4096]{1,0:T(8,128)(2,1)}, bf16[256,4096]{1,0:T(8,128)(2,1)}, u32[]{:S(2)}, u32[]{:S(2)}) collective-permute-start(bf16[256,4096]{1,0:T(8,128)(2,1)} %slice.107), channel_id=1, source_target_pairs={{0,4},{1,5},{2,6},{3,7}} | collective-permute-start | bytes 6291464 | tf_op jit(solution)/shard_map/ppermute | solution.py:209
  346.4 77.6 %copy-start.9 = (bf16[256,1024]{1,0:T(8,128)(2,1)S(1)}, bf16[256,1024]{1,0:T(8,128)(2,1)}, u32[]{:S(2)}) copy-start(bf16[256,1024]{1,0:T(8,128)(2,1)} %slice.109) | copy-start | bytes 1572868
  379.0 160.4 %collective-permute-start.15 = (bf16[256,2048]{1,0:T(8,128)(2,1)}, bf16[256,2048]{1,0:T(8,128)(2,1)}, u32[]{:S(2)}, u32[]{:S(2)}) collective-permute-start(bf16[256,2048]{1,0:T(8,128)(2,1)} %slice.108), channel_id=1, source_target_pairs={{0,4},{1,5},{2,6},{3,7}} | collective-permute-start | bytes 3145736 | tf_op jit(solution)/shard_map/ppermute | solution.py:209
  424.0 126.6 %collective-permute-start.14 = (bf16[256,1024]{1,0:T(8,128)(2,1)S(1)}, bf16[256,1024]{1,0:T(8,128)(2,1)S(1)}, u32[]{:S(2)}, u32[]{:S(2)}) collective-permute-start(bf16[256,1024]{1,0:T(8,128)(2,1)S(1)} %copy-done.9), channel_id=1, source_target_pairs={{0,4},{1,5},{2,6},{3,7}} | collective-permute-start | bytes 1572872 | tf_op jit(solution)/shard_map/ppermute | solution.py:209
  502.3 53.3 %collective-permute-start.13 = (bf16[256,512]{1,0:T(8,128)(2,1)S(1)}, bf16[256,512]{1,0:T(8,128)(2,1)S(1)}, u32[]{:S(2)}, u32[]{:S(2)}) collective-permute-start(bf16[256,512]{1,0:T(8,128)(2,1)S(1)} %slice.110), channel_id=1, source_target_pairs={{0,4},{1,5},{2,6},{3,7}} | collective-permute-start | bytes 786440 | tf_op jit(solution)/shard_map/ppermute | solution.py:209

commit v5 on v4

--- a/solution.py
+++ b/solution.py
@@ -11,50 +11,44 @@
 BLOCK = 256
 
 
-def block_kernel(count, aliased, *refs):
-    lo_ref, lr_ref, bo_ref = refs[:3]
-    rem_refs = refs[3:3 + count]
-    out_refs = refs[3 + count + aliased:]
-    acc = jnp.dot(lo_ref[...], bo_ref[...], preferred_element_type=jnp.float32)
-    for j in range(count):
-        acc += jnp.dot(lr_ref[:, j * BLOCK:(j + 1) * BLOCK], rem_refs[j][...], preferred_element_type=jnp.float32)
-    for out_ref in out_refs:
-        out_ref[...] = acc.astype(out_ref.dtype)
-
-
-def row_block(step, count, start, tile, l_own, l_rem, b_own, pieces, x, partial=False):
-    depth = (step + 1) * BLOCK
+def bulk_kernel(steps, aliased, lo_ref, lr_ref, bo_ref, *refs):
+    rem_refs = refs[:steps - 1]
+    x_ref, acc_ref = refs[steps - 1 + aliased:]
+    for step in range(steps):
+        rows = slice(step * BLOCK, (step + 1) * BLOCK)
+        depth = (step + 1) * BLOCK
+        acc = jnp.dot(lo_ref[rows, :depth], bo_ref[:depth, :], preferred_element_type=jnp.float32)
+        for j in range(min(step + 1, steps - 1)):
+            columns = slice(j * BLOCK, (j + 1) * BLOCK)
+            acc += jnp.dot(lr_ref[rows, columns], rem_refs[j][...], preferred_element_type=jnp.float32)
+        x_ref[rows, :] = acc.astype(x_ref.dtype)
+    acc_ref[...] = acc
+
+
+def bulk(start, tile, l_own, l_rem, b_own, pieces, x):
     rows, cols = b_own.shape
+    steps = rows // BLOCK
     width = pieces[0].shape[1]
     base = start // tile
-    in_specs = [
-        pl.BlockSpec((BLOCK, depth), lambda n: (step, 0)),
-        pl.BlockSpec((BLOCK, count * BLOCK), lambda n: (step, 0)),
-        pl.BlockSpec((depth, tile), lambda n: (0, base + n)),
-    ]
-    in_specs += [pl.BlockSpec((BLOCK, tile), lambda n: (0, n))] * count
-    args = [l_own, l_rem, b_own, *pieces[:count]]
-    out_specs = [pl.BlockSpec((BLOCK, tile), lambda n: (step, base + n))]
-    out_shape = [jax.ShapeDtypeStruct((rows, cols), jnp.bfloat16)]
+    whole = pl.BlockSpec((rows, rows), lambda n: (0, 0), pipeline_mode=pl.Buffered(1))
+    column = pl.BlockSpec((rows, tile), lambda n: (0, base + n))
+    in_specs = [whole, whole, column] + [pl.BlockSpec((BLOCK, tile), lambda n: (0, n))] * (steps - 1)
+    args = [l_own, l_rem, b_own, *pieces]
     aliases = {}
     if x is not None:
         aliases = {len(args): 0}
         args.append(x)
         in_specs.append(pl.BlockSpec(memory_space=pltpu.HBM))
-    if partial:
-        out_specs.append(pl.BlockSpec((BLOCK, tile), lambda n: (0, n)))
-        out_shape.append(jax.ShapeDtypeStruct((BLOCK, width), jnp.float32))
-    return pl.pallas_call(
-        functools.partial(block_kernel, count, len(aliases)),
+    return pl.pallas_call(
+        functools.partial(bulk_kernel, steps, len(aliases)),
         grid=(width // tile,),
         in_specs=in_specs,
-        out_specs=out_specs,
-        out_shape=out_shape,
+        out_specs=[column, pl.BlockSpec((BLOCK, tile), lambda n: (0, n))],
+        out_shape=[jax.ShapeDtypeStruct((rows, cols), jnp.bfloat16), jax.ShapeDtypeStruct((BLOCK, width), jnp.float32)],
         input_output_aliases=aliases,
-        compiler_params=pltpu.CompilerParams(vmem_limit_bytes=24 << 20),
+        compiler_params=pltpu.CompilerParams(vmem_limit_bytes=32 << 20),
         cost_estimate=pl.CostEstimate(
-            flops=2 * BLOCK * (depth + count * BLOCK) * width,
-            bytes_accessed=(depth + count * BLOCK + BLOCK) * width * 2, transcendentals=0),
+            flops=2 * rows * rows * width, bytes_accessed=3 * rows * width * 2, transcendentals=0),
     )(*args)
 
 
@@ -224,14 +218,9 @@
         l_own = jnp.where(matches, same, other)
         l_rem = jnp.where(matches, other, same)
 
-        x = None
-        for j in range(final):
-            for h in range(2):
-                x, = row_block(j, j + 1, h * half, 1024, l_own, l_rem, rhs_loc, [got[k, h * half] for k in range(j + 1)], x)
-        acc = [None, None]
+        x, acc = None, [None, None]
         for h in range(2):
-            x, acc[h] = row_block(
-                final, final, h * half, 1024, l_own, l_rem, rhs_loc, [got[k, h * half] for k in range(final)], x, partial=True)
+            x, acc[h] = bulk(h * half, 512, l_own, l_rem, rhs_loc, [got[k, h * half] for k in range(final)], x)
         l_last = l_rem[final * BLOCK:, final * BLOCK:]
         off, w = tail[-1]
         acc_last = acc[1][:, off - half:off - half + w]

time: 557 us -> 574 us (1.031)
  waiting for transfers between devices: 373 us -> 426 us
  Pallas kernels: 107 us -> 58.4 us
  starting transfers between devices: 21.1 us -> 27.9 us
  local copies, waits for them, and re-layouts: 44.9 us -> 51.3 us
    ppermute x15, waiting for transfers between devices: 325 us -> 370 us  [send(): lax.ppermute(piece, 'row', down_row if i and j == final else swap_row)]
    pallas_call x12 -> x2, Pallas kernels: 97.3 us -> 57.3 us  [bulk(): pl.pallas_call(functools.partial(bulk_kernel, steps, len(aliases)), grid=...]
    pallas_call x1, Pallas kernels: 9.05 us -> 0.96 us  [cut(): pl.pallas_call(functools.partial(cut_kernel, row, start), in_specs=[pl.Bl...]
    ppermute x3, waiting for transfers between devices: 48.1 us -> 55.9 us  [local_trmm(): lax.ppermute(tri_loc, 'col', [(c, c ^ d) for c in range(grid_cols)])]
    unnamed x30 -> x40, local copies, waits for them, and re-layouts: 4.88 us -> 12.2 us
    ppermute x15, starting transfers between devices: 17.7 us -> 24.5 us  [send(): lax.ppermute(piece, 'row', down_row if i and j == final else swap_row)]
  transfers between devices with their start and end apart: 18 -> 18, of which waited for: 14 -> 15; matrix products, arithmetic and copies ran while one was open for 9% -> 9% of each run, Pallas kernels for 19% -> 10%
where the time goes in v5:
time: 574 us; the launch traced here: 573 us
  waiting for transfers between devices  426 us (74%)
  Pallas kernels  58.4 us (10%)
  local copies, waits for them, and re-layouts  51.3 us (9%)
  starting transfers between devices  27.9 us (5%)
  other arithmetic  9.52 us (2%)
    ppermute x15, waiting for transfers between devices, send(): lax.ppermute(piece, 'row', down_row if i and j == final else swap_row)  370 us
    pallas_call x2, Pallas kernels, bulk(): pl.pallas_call(functools.partial(bulk_kernel, steps, len(aliases)), grid=...  57.3 us
    ppermute x3, waiting for transfers between devices, local_trmm(): lax.ppermute(tri_loc, 'col', [(c, c ^ d) for c in range(grid_cols)])  55.9 us
    slice x14, local copies, waits for them, and re-layouts, send(): source[j * BLOCK:(j + 1) * BLOCK, off:off + w]  39 us
    ppermute x15, starting transfers between devices, send(): lax.ppermute(piece, 'row', down_row if i and j == final else swap_row)  24.5 us
    unnamed x40, local copies, waits for them, and re-layouts  12.2 us
  transfers between devices with their start and end apart: 18, of which 15 were waited for; matrix products, arithmetic and copies ran while one was open for 9% of the time, Pallas kernels for 10%

profile of v5, /device:TPU:0, one launch (start us, length us, event | category | flops | bytes accessed | tf_op | source)
XLA Modules:
  0.0 573.1 jit_solution(14735935897089907036)
XLA Ops:
  4.4 3.1 slice.97
  7.5 3.1 slice.98
  10.6 3.2 slice.99
  13.8 3.1 slice.100
  16.9 3.1 slice.101
  20.1 3.1 slice.102
  23.2 3.2 slice.103
  26.4 3.1 slice.104
  29.5 3.2 slice.105
  34.7 3.1 slice.106
  37.9 3.2 slice.107
  45.6 9.8 %collective-permute-done.1 = bf16[1536,768]{1,0:T(8,128)(2,1)} collective-permute-done((bf16[1536,768]{1,0:T(8,128)(2,1)}, bf16[1536,768]{1,0:T(8,128)(2,1)}, u32[]{:S(2)}, u32[]{:S(2)}) %collective-permute-start.1) | collective-permute-done | bytes 2359328 | tf_op jit(solution)/shard_map/ppermute | solution.py:211
  59.9 46.1 %collective-permute-done.2 = bf16[1536,768]{1,0:T(8,128)(2,1)S(1)} collective-permute-done((bf16[1536,768]{1,0:T(8,128)(2,1)}, bf16[1536,768]{1,0:T(8,128)(2,1)S(1)}, u32[]{:S(2)}, u32[]{:S(2)}) %collective-permute-start.2) | collective-permute-done | bytes 2359328 | tf_op jit(solution)/shard_map/ppermute | solution.py:211
  108.9 17.6 %collective-permute-done.11.refs_3_ = bf16[256,4096]{1,0:T(8,128)(2,1)} collective-permute-done((bf16[256,4096]{1,0:T(8,128)(2,1)}, bf16[256,4096]{1,0:T(8,128)(2,1)}, u32[]{:S(2)}, u32[]{:S(2)}) %collective-permute-start.11) | collective-permute-done | bytes 2097184 | tf_op jit(solution)/shard_map/ppermute | solution.py:203
  127.6 43.7 %collective-permute-done.10.refs_2_ = bf16[256,4096]{1,0:T(8,128)(2,1)S(1)} collective-permute-done((bf16[256,4096]{1,0:T(8,128)(2,1)}, bf16[256,4096]{1,0:T(8,128)(2,1)S(1)}, u32[]{:S(2)}, u32[]{:S(2)}) %collective-permute-start.10) | collective-permute-done | bytes 2097184 | tf_op jit(solution)/shard_map/ppermute | solution.py:203
  173.7 42.5 %collective-permute-done.9.refs_1_ = bf16[256,4096]{1,0:T(8,128)(2,1)S(1)} collective-permute-done((bf16[256,4096]{1,0:T(8,128)(2,1)}, bf16[256,4096]{1,0:T(8,128)(2,1)S(1)}, u32[]{:S(2)}, u32[]{:S(2)}) %collective-permute-start.9) | collective-permute-done | bytes 2097184 | tf_op jit(solution)/shard_map/ppermute | solution.py:203
  218.6 42.5 %collective-permute-done.8.refs_0_ = bf16[256,4096]{1,0:T(8,128)(2,1)S(1)} collective-permute-done((bf16[256,4096]{1,0:T(8,128)(2,1)S(1)}, bf16[256,4096]{1,0:T(8,128)(2,1)S(1)}, u32[]{:S(2)}, u32[]{:S(2)}) %collective-permute-start.8) | collective-permute-done | bytes 2097184 | tf_op jit(solution)/shard_map/ppermute | solution.py:203
  263.6 6.5 %broadcast_select_fusion = (bf16[1536,1536]{1,0:T(8,128)(2,1)S(1)}, bf16[1536,1536]{1,0:T(8,128)(2,1)}) fusion(bf16[1536,1536]{1,0:T(8,128)(2,1)} %copy-done.9, bf16[1536,1536]{1,0:T(8,128)(2,1)} %copy-done.8, pred[]{:T(512)S(6)} %eq.5), kind=kLoop, calls=%fused_computation | loop fusion | flops 4718592 | bytes 18874368 | tf_op jit(solution)/shard_map/jit(_where)/select_n | solution.py:218
  270.1 36.0 %collective-permute-done.7.refs_4_ = bf16[256,4096]{1,0:T(8,128)(2,1)S(1)} collective-permute-done((bf16[256,4096]{1,0:T(8,128)(2,1)}, bf16[256,4096]{1,0:T(8,128)(2,1)S(1)}, u32[]{:S(2)}, u32[]{:S(2)}) %collective-permute-start.7) | collective-permute-done | bytes 2097184 | tf_op jit(solution)/shard_map/ppermute | solution.py:203
  307.4 3.1 collective-permute-start.16
  315.4 28.7 %shard_map.29 = (bf16[1536,8192]{1,0:T(8,128)(2,1)}, f32[256,4096]{1,0:T(8,128)S(1)}) custom-call(bf16[1536,1536]{1,0:T(8,128)(2,1)S(1)} %get-tuple-element.75.lo_ref, bf16[1536,1536]{1,0:T(8,128)(2,1)} %get-tuple-element.76.lr_ref.l_ref, bf16[1536,8192]{1,0:T(8,128)(2,1)} %bo_ref.3, bf16[256,4096]{1,0:T(8,128)(2,1)S(1)} %copy-done.7, ...), custom_call_target="tpu_custom_call" | custom-call | flops 19327352832 | bytes 37748736 | tf_op jit(solution)/shard_map/pallas_call | solution.py:42
  344.0 7.1 %collective-permute-done.6.refs_3_ = bf16[256,4096]{1,0:T(8,128)(2,1)} collective-permute-done((bf16[256,4096]{1,0:T(8,128)(2,1)}, bf16[256,4096]{1,0:T(8,128)(2,1)}, u32[]{:S(2)}, u32[]{:S(2)}) %collective-permute-start.6) | collective-permute-done | bytes 2097184 | tf_op jit(solution)/shard_map/ppermute | solution.py:203
  352.3 43.8 %collective-permute-done.5.refs_2_ = bf16[256,4096]{1,0:T(8,128)(2,1)} collective-permute-done((bf16[256,4096]{1,0:T(8,128)(2,1)}, bf16[256,4096]{1,0:T(8,128)(2,1)}, u32[]{:S(2)}, u32[]{:S(2)}) %collective-permute-start.5) | collective-permute-done | bytes 2097184 | tf_op jit(solution)/shard_map/ppermute | solution.py:203
  396.1 3.1 collective-permute-start.15
  399.2 41.9 %collective-permute-done.4.refs_1_ = bf16[256,4096]{1,0:T(8,128)(2,1)} collective-permute-done((bf16[256,4096]{1,0:T(8,128)(2,1)}, bf16[256,4096]{1,0:T(8,128)(2,1)}, u32[]{:S(2)}, u32[]{:S(2)}) %collective-permute-start.4) | collective-permute-done | bytes 2097184 | tf_op jit(solution)/shard_map/ppermute | solution.py:203
  441.0 3.0 collective-permute-start.14
  444.1 41.9 %collective-permute-done.3.refs_0_ = bf16[256,4096]{1,0:T(8,128)(2,1)} collective-permute-done((bf16[256,4096]{1,0:T(8,128)(2,1)S(1)}, bf16[256,4096]{1,0:T(8,128)(2,1)}, u32[]{:S(2)}, u32[]{:S(2)}) %collective-permute-start.3) | collective-permute-done | bytes 2097184 | tf_op jit(solution)/shard_map/ppermute | solution.py:203
  487.6 28.6 %shard_map.30 = (bf16[1536,8192]{1,0:T(8,128)(2,1)}, f32[256,4096]{1,0:T(8,128)S(1)}) custom-call(bf16[1536,1536]{1,0:T(8,128)(2,1)S(1)} %get-tuple-element.75.lo_ref, bf16[1536,1536]{1,0:T(8,128)(2,1)} %get-tuple-element.76.lr_ref.l_ref, bf16[1536,8192]{1,0:T(8,128)(2,1)} %bo_ref.3, ...), custom_call_target="tpu_custom_call", output_to_operand_aliasing={{0}: (8, {})} | custom-call | flops 19327352832 | bytes 37748736 | tf_op jit(solution)/shard_map/pallas_call | solution.py:42
  520.2 14.9 %collective-permute-done.17.piece_ref = bf16[256,512]{1,0:T(8,128)(2,1)S(1)} collective-permute-done((bf16[256,512]{1,0:T(8,128)(2,1)S(1)}, bf16[256,512]{1,0:T(8,128)(2,1)S(1)}, u32[]{:S(2)}, u32[]{:S(2)}) %collective-permute-start.17) | collective-permute-done | bytes 262176 | tf_op jit(solution)/shard_map/ppermute | solution.py:203
  535.3 22.3 %collective-permute-done.15.b_ref = bf16[256,2048]{1,0:T(8,128)(2,1)S(1)} collective-permute-done((bf16[256,2048]{1,0:T(8,128)(2,1)}, bf16[256,2048]{1,0:T(8,128)(2,1)S(1)}, u32[]{:S(2)}, u32[]{:S(2)}) %collective-permute-start.15) | collective-permute-done | bytes 1048608 | tf_op jit(solution)/shard_map/ppermute | solution.py:203
  557.7 11.1 %collective-permute-done.14.b_ref = bf16[256,1024]{1,0:T(8,128)(2,1)S(1)} collective-permute-done((bf16[256,1024]{1,0:T(8,128)(2,1)S(1)}, bf16[256,1024]{1,0:T(8,128)(2,1)S(1)}, u32[]{:S(2)}, u32[]{:S(2)}) %collective-permute-start.14) | collective-permute-done | bytes 524320 | tf_op jit(solution)/shard_map/ppermute | solution.py:203
  568.8 4.3 collective-permute-done.13.b_ref
  (74 shorter events, 39.5 us)
Async XLA Ops:
  0.0 44.4 %collective-permute-start = (bf16[1536,768]{1,0:T(8,128)(2,1)}, bf16[1536,768]{1,0:T(8,128)(2,1)}, u32[]{:S(2)}, u32[]{:S(2)}) collective-permute-start(bf16[1536,768]{1,0:T(8,128)(2,1)} %param.2), channel_id=1, source_target_pairs={{0,1},{1,0},{2,3},{3,2},{4,5},{5,4},{6,7},{7,6}} | collective-permute-start | bytes 7077896 | tf_op jit(solution)/shard_map/ppermute | solution.py:211
  0.8 54.5 %collective-permute-start.1 = (bf16[1536,768]{1,0:T(8,128)(2,1)}, bf16[1536,768]{1,0:T(8,128)(2,1)}, u32[]{:S(2)}, u32[]{:S(2)}) collective-permute-start(bf16[1536,768]{1,0:T(8,128)(2,1)} %param.2), channel_id=1, source_target_pairs={{0,3},{1,2},{2,1},{3,0},{4,7},{5,6},{6,5},{7,4}} | collective-permute-start | bytes 7077896 | tf_op jit(solution)/shard_map/ppermute | solution.py:211
  3.4 102.6 %collective-permute-start.2 = (bf16[1536,768]{1,0:T(8,128)(2,1)}, bf16[1536,768]{1,0:T(8,128)(2,1)S(1)}, u32[]{:S(2)}, u32[]{:S(2)}) collective-permute-start(bf16[1536,768]{1,0:T(8,128)(2,1)} %param.2), channel_id=1, source_target_pairs={{0,2},{1,3},{2,0},{3,1},{4,6},{5,7},{6,4},{7,5}} | collective-permute-start | bytes 7077896 | tf_op jit(solution)/shard_map/ppermute | solution.py:211
  32.7 75.6 %collective-permute-start.12 = (bf16[256,4096]{1,0:T(8,128)(2,1)}, bf16[256,4096]{1,0:T(8,128)(2,1)}, u32[]{:S(2)}, u32[]{:S(2)}) collective-permute-start(bf16[256,4096]{1,0:T(8,128)(2,1)} %slice.105), channel_id=1, source_target_pairs={{0,4},{4,0},{1,5},{5,1},{2,6},{6,2},{3,7},{7,3}} | collective-permute-start | bytes 6291464 | tf_op jit(solution)/shard_map/ppermute | solution.py:203
  33.8 92.7 %collective-permute-start.11 = (bf16[256,4096]{1,0:T(8,128)(2,1)}, bf16[256,4096]{1,0:T(8,128)(2,1)}, u32[]{:S(2)}, u32[]{:S(2)}) collective-permute-start(bf16[256,4096]{1,0:T(8,128)(2,1)} %slice.103), channel_id=1, source_target_pairs={{0,4},{4,0},{1,5},{5,1},{2,6},{6,2},{3,7},{7,3}} | collective-permute-start | bytes 6291464 | tf_op jit(solution)/shard_map/ppermute | solution.py:203
  44.4 126.8 %collective-permute-start.10 = (bf16[256,4096]{1,0:T(8,128)(2,1)}, bf16[256,4096]{1,0:T(8,128)(2,1)S(1)}, u32[]{:S(2)}, u32[]{:S(2)}) collective-permute-start(bf16[256,4096]{1,0:T(8,128)(2,1)} %slice.101), channel_id=1, source_target_pairs={{0,4},{4,0},{1,5},{5,1},{2,6},{6,2},{3,7},{7,3}} | collective-permute-start | bytes 6291464 | tf_op jit(solution)/shard_map/ppermute | solution.py:203
  55.4 160.8 %collective-permute-start.9 = (bf16[256,4096]{1,0:T(8,128)(2,1)}, bf16[256,4096]{1,0:T(8,128)(2,1)S(1)}, u32[]{:S(2)}, u32[]{:S(2)}) collective-permute-start(bf16[256,4096]{1,0:T(8,128)(2,1)} %slice.99), channel_id=1, source_target_pairs={{0,4},{4,0},{1,5},{5,1},{2,6},{6,2},{3,7},{7,3}} | collective-permute-start | bytes 6291464 | tf_op jit(solution)/shard_map/ppermute | solution.py:203
  59.7 46.3 %copy-start.12 = (bf16[256,4096]{1,0:T(8,128)(2,1)S(1)}, bf16[256,4096]{1,0:T(8,128)(2,1)}, u32[]{:S(2)}) copy-start(bf16[256,4096]{1,0:T(8,128)(2,1)} %slice.97) | copy-start | bytes 6291460
  59.7 47.9 %copy-start.10 = (bf16[1536,768]{1,0:T(8,128)(2,1)S(1)}, bf16[1536,768]{1,0:T(8,128)(2,1)}, u32[]{:S(2)}) copy-start(bf16[1536,768]{1,0:T(8,128)(2,1)} %param.2) | copy-start | bytes 7077892
  106.0 155.2 %collective-permute-start.8 = (bf16[256,4096]{1,0:T(8,128)(2,1)S(1)}, bf16[256,4096]{1,0:T(8,128)(2,1)S(1)}, u32[]{:S(2)}, u32[]{:S(2)}) collective-permute-start(bf16[256,4096]{1,0:T(8,128)(2,1)S(1)} %copy-done.12), channel_id=1, source_target_pairs={{0,4},{4,0},{1,5},{5,1},{2,6},{6,2},{3,7},{7,3}} | collective-permute-start | bytes 6291464 | tf_op jit(solution)/shard_map/ppermute | solution.py:203
  108.2 154.2 %copy-start.11 = (bf16[256,4096]{1,0:T(8,128)(2,1)S(1)}, bf16[256,4096]{1,0:T(8,128)(2,1)}, u32[]{:S(2)}) copy-start(bf16[256,4096]{1,0:T(8,128)(2,1)} %slice.98) | copy-start | bytes 6291460
  108.3 197.8 %collective-permute-start.7 = (bf16[256,4096]{1,0:T(8,128)(2,1)}, bf16[256,4096]{1,0:T(8,128)(2,1)S(1)}, u32[]{:S(2)}, u32[]{:S(2)}) collective-permute-start(bf16[256,4096]{1,0:T(8,128)(2,1)} %slice.106), channel_id=1, source_target_pairs={{0,4},{4,0},{1,5},{5,1},{2,6},{6,2},{3,7},{7,3}} | collective-permute-start | bytes 6291464 | tf_op jit(solution)/shard_map/ppermute | solution.py:203
  108.8 154.7 %copy-start.8 = (bf16[1536,1536]{1,0:T(8,128)(2,1)}, bf16[1536,1536]{1,0:T(8,128)(2,1)S(1)}, u32[]{:S(2)}) copy-start(bf16[1536,1536]{1,0:T(8,128)(2,1)S(1)} %get-tuple-element.82) | copy-start | bytes 14155780
  108.8 154.7 %copy-start.9 = (bf16[1536,1536]{1,0:T(8,128)(2,1)}, bf16[1536,1536]{1,0:T(8,128)(2,1)S(1)}, u32[]{:S(2)}) copy-start(bf16[1536,1536]{1,0:T(8,128)(2,1)S(1)} %get-tuple-element.81) | copy-start | bytes 14155780
  126.5 224.7 %collective-permute-start.6 = (bf16[256,4096]{1,0:T(8,128)(2,1)}, bf16[256,4096]{1,0:T(8,128)(2,1)}, u32[]{:S(2)}, u32[]{:S(2)}) collective-permute-start(bf16[256,4096]{1,0:T(8,128)(2,1)} %slice.104), channel_id=1, source_target_pairs={{0,4},{4,0},{1,5},{5,1},{2,6},{6,2},{3,7},{7,3}} | collective-permute-start | bytes 6291464 | tf_op jit(solution)/shard_map/ppermute | solution.py:203
  171.3 1.3 copy-start
  172.6 223.5 %collective-permute-start.5 = (bf16[256,4096]{1,0:T(8,128)(2,1)}, bf16[256,4096]{1,0:T(8,128)(2,1)}, u32[]{:S(2)}, u32[]{:S(2)}) collective-permute-start(bf16[256,4096]{1,0:T(8,128)(2,1)} %slice.102), channel_id=1, source_target_pairs={{0,4},{4,0},{1,5},{5,1},{2,6},{6,2},{3,7},{7,3}} | collective-permute-start | bytes 6291464 | tf_op jit(solution)/shard_map/ppermute | solution.py:203
  216.2 1.3 copy-start.2
  217.5 223.5 %collective-permute-start.4 = (bf16[256,4096]{1,0:T(8,128)(2,1)}, bf16[256,4096]{1,0:T(8,128)(2,1)}, u32[]{:S(2)}, u32[]{:S(2)}) collective-permute-start(bf16[256,4096]{1,0:T(8,128)(2,1)} %slice.100), channel_id=1, source_target_pairs={{0,4},{4,0},{1,5},{5,1},{2,6},{6,2},{3,7},{7,3}} | collective-permute-start | bytes 6291464 | tf_op jit(solution)/shard_map/ppermute | solution.py:203
  262.5 223.5 %collective-permute-start.3 = (bf16[256,4096]{1,0:T(8,128)(2,1)S(1)}, bf16[256,4096]{1,0:T(8,128)(2,1)}, u32[]{:S(2)}, u32[]{:S(2)}) collective-permute-start(bf16[256,4096]{1,0:T(8,128)(2,1)S(1)} %copy-done.11), channel_id=1, source_target_pairs={{0,4},{4,0},{1,5},{5,1},{2,6},{6,2},{3,7},{7,3}} | collective-permute-start | bytes 6291464 | tf_op jit(solution)/shard_map/ppermute | solution.py:203
  306.1 1.3 copy-start.4
  307.4 227.8 %collective-permute-start.16 = (bf16[256,4096]{1,0:T(8,128)(2,1)}, bf16[256,4096]{1,0:T(8,128)(2,1)S(1)}, u32[]{:S(2)}, u32[]{:S(2)}) collective-permute-start(bf16[256,4096]{1,0:T(8,128)(2,1)} %slice.107), channel_id=1, source_target_pairs={{0,4},{1,5},{2,6},{3,7}} | collective-permute-start | bytes 6291464 | tf_op jit(solution)/shard_map/ppermute | solution.py:203
  310.6 1.6 copy-start.1
  312.2 1.6 copy-start.3
  313.8 1.6 copy-start.7
  315.4 219.8 %slice-start = ((s8[4718592]{0:T(1024)(128)(4,1)}), s8[4194304]{0:T(1024)(128)(4,1)S(1)}, s32[]{:S(2)}) async-start(s8[4718592]{0:T(1024)(128)(4,1)} %bitcast), calls=%async_computation | async-start | bytes 8388608
  351.2 183.9 %collective-permute-start.17 = (bf16[256,512]{1,0:T(8,128)(2,1)S(1)}, bf16[256,512]{1,0:T(8,128)(2,1)S(1)}, u32[]{:S(2)}, u32[]{:S(2)}) collective-permute-start(bf16[256,512]{1,0:T(8,128)(2,1)S(1)} %shard_map.28), channel_id=1, source_target_pairs={{0,4},{4,0},{1,5},{5,1},{2,6},{6,2},{3,7},{7,3}} | collective-permute-start | bytes 786440 | tf_op jit(solution)/shard_map/ppermute | solution.py:203
  396.1 161.5 %collective-permute-start.15 = (bf16[256,2048]{1,0:T(8,128)(2,1)}, bf16[256,2048]{1,0:T(8,128)(2,1)S(1)}, u32[]{:S(2)}, u32[]{:S(2)}) collective-permute-start(bf16[256,2048]{1,0:T(8,128)(2,1)} %slice.108), channel_id=1, source_target_pairs={{0,4},{1,5},{2,6},{3,7}} | collective-permute-start | bytes 3145736 | tf_op jit(solution)/shard_map/ppermute | solution.py:203
  441.0 127.7 %collective-permute-start.14 = (bf16[256,1024]{1,0:T(8,128)(2,1)S(1)}, bf16[256,1024]{1,0:T(8,128)(2,1)S(1)}, u32[]{:S(2)}, u32[]{:S(2)}) collective-permute-start(bf16[256,1024]{1,0:T(8,128)(2,1)S(1)} %slice.109), channel_id=1, source_target_pairs={{0,4},{1,5},{2,6},{3,7}} | collective-permute-start | bytes 1572872 | tf_op jit(solution)/shard_map/ppermute | solution.py:203
  486.0 1.6 copy-start.5
  487.6 47.6 %slice-start.1 = ((s8[4718592]{0:T(1024)(128)(4,1)}), s8[524288]{0:T(1024)(128)(4,1)S(1)}, s32[]{:S(2)}) async-start(s8[4718592]{0:T(1024)(128)(4,1)} %bitcast), calls=%async_computation.1 | async-start | bytes 1048576
  517.2 56.0 %collective-permute-start.13 = (bf16[256,512]{1,0:T(8,128)(2,1)S(1)}, bf16[256,512]{1,0:T(8,128)(2,1)S(1)}, u32[]{:S(2)}, u32[]{:S(2)}) collective-permute-start(bf16[256,512]{1,0:T(8,128)(2,1)S(1)} %slice.110), channel_id=1, source_target_pairs={{0,4},{1,5},{2,6},{3,7}} | collective-permute-start | bytes 786440 | tf_op jit(solution)/shard_map/ppermute | solution.py:203
  (1 other events, 1.3 us)

commit v6 on v5

--- a/solution.py
+++ b/solution.py
@@ -11,29 +11,47 @@
 BLOCK = 256
 
 
-def bulk_kernel(steps, aliased, lo_ref, lr_ref, bo_ref, *refs):
-    rem_refs = refs[:steps - 1]
-    x_ref, acc_ref = refs[steps - 1 + aliased:]
+def bulk_kernel(steps, aliased, *refs):
+    l_refs, bo_ref, rem_refs = refs[:4], refs[4], refs[5:4 + steps]
+    x_ref, acc_ref, last_ref, l_buf, sems = refs[4 + steps + aliased:]
+
+    @pl.when(pl.program_id(0) == 0)
+    def _():
+        row, col = lax.axis_index("row"), lax.axis_index("col")
+        copies = []
+        for d in range(4):
+            chip, core = (col // 2 + d // 2) % 2, (col + d) % 2
+            side = (core + row) % 2
+            for j in range(steps // 2):
+                place = pl.multiple_of((2 * j + chip) * BLOCK, BLOCK)
+                copies.append(pltpu.make_async_copy(
+                    l_refs[d].at[:, pl.ds(j * BLOCK, BLOCK)], l_buf.at[side, :, pl.ds(place, BLOCK)], sems.at[len(copies)]))
+        for copy in copies:
+            copy.start()
+        for copy in copies:
+            copy.wait()
+        last_ref[...] = l_buf[1, (steps - 1) * BLOCK:, (steps - 1) * BLOCK:]
+
     for step in range(steps):
         rows = slice(step * BLOCK, (step + 1) * BLOCK)
         depth = (step + 1) * BLOCK
-        acc = jnp.dot(lo_ref[rows, :depth], bo_ref[:depth, :], preferred_element_type=jnp.float32)
+        acc = jnp.dot(l_buf[0, rows, :depth], bo_ref[:depth, :], preferred_element_type=jnp.float32)
         for j in range(min(step + 1, steps - 1)):
             columns = slice(j * BLOCK, (j + 1) * BLOCK)
-            acc += jnp.dot(lr_ref[rows, columns], rem_refs[j][...], preferred_element_type=jnp.float32)
+            acc += jnp.dot(l_buf[1, rows, columns], rem_refs[j][...], preferred_element_type=jnp.float32)
         x_ref[rows, :] = acc.astype(x_ref.dtype)
     acc_ref[...] = acc
 
 
-def bulk(start, tile, l_own, l_rem, b_own, pieces, x):
+def bulk(start, tile, l_parts, b_own, pieces, x):
     rows, cols = b_own.shape
     steps = rows // BLOCK
     width = pieces[0].shape[1]
     base = start // tile
-    whole = pl.BlockSpec((rows, rows), lambda n: (0, 0), pipeline_mode=pl.Buffered(1))
     column = pl.BlockSpec((rows, tile), lambda n: (0, base + n))
-    in_specs = [whole, whole, column] + [pl.BlockSpec((BLOCK, tile), lambda n: (0, n))] * (steps - 1)
-    args = [l_own, l_rem, b_own, *pieces]
+    in_specs = [pl.BlockSpec(memory_space=pltpu.HBM)] * 4 + [column]
+    in_specs += [pl.BlockSpec((BLOCK, tile), lambda n: (0, n))] * (steps - 1)
+    args = [*l_parts, b_own, *pieces]
     aliases = {}
     if x is not None:
         aliases = {len(args): 0}
@@ -43,10 +61,15 @@
         functools.partial(bulk_kernel, steps, len(aliases)),
         grid=(width // tile,),
         in_specs=in_specs,
-        out_specs=[column, pl.BlockSpec((BLOCK, tile), lambda n: (0, n))],
-        out_shape=[jax.ShapeDtypeStruct((rows, cols), jnp.bfloat16), jax.ShapeDtypeStruct((BLOCK, width), jnp.float32)],
+        out_specs=[column, pl.BlockSpec((BLOCK, tile), lambda n: (0, n)), pl.BlockSpec((BLOCK, BLOCK), lambda n: (0, 0))],
+        out_shape=[
+            jax.ShapeDtypeStruct((rows, cols), jnp.bfloat16),
+            jax.ShapeDtypeStruct((BLOCK, width), jnp.float32),
+            jax.ShapeDtypeStruct((BLOCK, BLOCK), jnp.bfloat16),
+        ],
+        scratch_shapes=[pltpu.VMEM((2, rows, rows), jnp.bfloat16), pltpu.SemaphoreType.DMA((2 * steps,))],
         input_output_aliases=aliases,
-        compiler_params=pltpu.CompilerParams(vmem_limit_bytes=32 << 20),
+        compiler_params=pltpu.CompilerParams(vmem_limit_bytes=50 << 20),
         cost_estimate=pl.CostEstimate(
             flops=2 * rows * rows * width, bytes_accessed=3 * rows * width * 2, transcendentals=0),
     )(*args)
@@ -58,7 +81,7 @@
 
     @pl.when(lax.axis_index("row") == row)
     def _():
-        l_copy = pltpu.make_async_copy(l_ref.at[rows, rows], l_buf, sems.at[0])
+        l_copy = pltpu.make_async_copy(l_ref, l_buf, sems.at[0])
         b_copy = pltpu.make_async_copy(b_ref, b_buf, sems.at[1])
         acc_copy = pltpu.make_async_copy(acc_ref.at[:, pl.ds(acc_start, b_ref.shape[1])], acc_buf, sems.at[2])
         l_copy.start()
@@ -79,7 +102,7 @@
         out_copy.wait()
 
 
-def finish(step, start, row, l_rem, piece, acc, acc_start, x):
+def finish(step, start, row, l_last, piece, acc, acc_start, x):
     width = piece.shape[1]
     return pl.pallas_call(
         functools.partial(finish_kernel, step, start, row, min(width, 512), acc_start),
@@ -87,7 +110,7 @@
         out_specs=pl.BlockSpec(memory_space=pltpu.HBM),
         out_shape=jax.ShapeDtypeStruct(x.shape, x.dtype),
         scratch_shapes=[
-            pltpu.VMEM((BLOCK, BLOCK), l_rem.dtype),
+            pltpu.VMEM((BLOCK, BLOCK), l_last.dtype),
             pltpu.VMEM((BLOCK, width), piece.dtype),
             pltpu.VMEM((BLOCK, width), acc.dtype),
             pltpu.VMEM((BLOCK, width), x.dtype),
@@ -97,7 +120,7 @@
         compiler_params=pltpu.CompilerParams(vmem_limit_bytes=12 << 20),
         cost_estimate=pl.CostEstimate(
             flops=2 * BLOCK * BLOCK * width, bytes_accessed=BLOCK * width * 8, transcendentals=0),
-    )(l_rem, piece, acc, x)
+    )(l_last, piece, acc, x)
 
 
 def last_kernel(step, start, row, l_ref, b_ref, acc_ref, x_in, x_ref, out_buf, sem):
@@ -168,12 +191,34 @@
     )(piece)
 
 
-def weave(even, odd):
-    count = even.shape[1] // BLOCK
-    parts = []
-    for j in range(count):
-        parts += [even[:, j * BLOCK:(j + 1) * BLOCK], odd[:, j * BLOCK:(j + 1) * BLOCK]]
-    return jnp.concatenate(parts, axis=1)
+def cut_many_kernel(places, b_ref, *refs):
+    count = len(places)
+    out_refs, bufs, sems = refs[:count], refs[count:2 * count], refs[2 * count]
+    fetches = [
+        pltpu.make_async_copy(b_ref.at[pl.ds(row, BLOCK), pl.ds(start, width)], bufs[i], sems.at[0, i])
+        for i, (row, start, width) in enumerate(places)]
+    stores = [pltpu.make_async_copy(bufs[i], out_refs[i], sems.at[1, i]) for i in range(count)]
+    for fetch in fetches:
+        fetch.start()
+    for fetch, store in zip(fetches, stores):
+        fetch.wait()
+        store.start()
+    for store in stores:
+        store.wait()
+
+
+def cut_many(b, places):
+    size = sum(width for _, _, width in places) * BLOCK
+    return pl.pallas_call(
+        functools.partial(cut_many_kernel, places),
+        in_specs=[pl.BlockSpec(memory_space=pltpu.HBM)],
+        out_specs=[pl.BlockSpec(memory_space=pltpu.HBM)] * len(places),
+        out_shape=[jax.ShapeDtypeStruct((BLOCK, width), b.dtype) for _, _, width in places],
+        scratch_shapes=[pltpu.VMEM((BLOCK, width), b.dtype) for _, _, width in places]
+        + [pltpu.SemaphoreType.DMA((2, len(places)))],
+        compiler_params=pltpu.CompilerParams(vmem_limit_bytes=48 << 20),
+        cost_estimate=pl.CostEstimate(flops=2 * size, bytes_accessed=4 * size, transcendentals=0),
+    )(b)
 
 
 def solution(mesh):
@@ -196,39 +241,33 @@
 
         got = {}
 
-        def send(i, source):
-            j, off, w = order[i]
-            piece = source[j * BLOCK:(j + 1) * BLOCK, off:off + w] if i else cut(source, j * BLOCK, off, w)
-            source, piece = lax.optimization_barrier((source, piece))
+        def send(i, piece):
+            j, off, _ = order[i]
             got[j, off] = lax.ppermute(piece, "row", down_row if i and j == final else swap_row)
-            return source
-
-        source = rhs_loc
-        for i in range(len(order) - 1):
-            source = send(i, source)
+
+        places = [(j * BLOCK, off, w) for j, off, w in order]
+        piece = cut(rhs_loc, *places[0])
+        send(0, piece)
+        piece, = cut_many(rhs_loc, places[1:2])
+        send(1, piece)
+        pieces = cut_many(rhs_loc, places[2:-1])
+        for i, piece in enumerate(pieces):
+            send(2 + i, piece)
         got[final, cols - first] = keep(grid_rows - 1, got[final, cols - first])
         l_core, l_chip, l_both = (
             lax.ppermute(tri_loc, "col", [(c, c ^ d) for c in range(grid_cols)]) for d in (1, 2, 3))
-        p = lax.axis_index("row")
-        q = lax.axis_index("col")
-        on_first = q < 2
-        same = weave(jnp.where(on_first, tri_loc, l_chip), jnp.where(on_first, l_chip, tri_loc))
-        other = weave(jnp.where(on_first, l_core, l_both), jnp.where(on_first, l_both, l_core))
-        matches = (q % 2) == p
-        l_own = jnp.where(matches, same, other)
-        l_rem = jnp.where(matches, other, same)
+        l_parts = [tri_loc, l_core, l_chip, l_both]
 
         x, acc = None, [None, None]
         for h in range(2):
-            x, acc[h] = bulk(h * half, 512, l_own, l_rem, rhs_loc, [got[k, h * half] for k in range(final)], x)
-        l_last = l_rem[final * BLOCK:, final * BLOCK:]
+            x, acc[h], l_last = bulk(h * half, 512, l_parts, rhs_loc, [got[k, h * half] for k in range(final)], x)
         off, w = tail[-1]
         acc_last = acc[1][:, off - half:off - half + w]
-        source, acc[1] = lax.optimization_barrier((source, acc[1]))
-        send(len(order) - 1, source)
+        source, acc[1] = lax.optimization_barrier((rhs_loc, acc[1]))
+        send(len(order) - 1, source[final * BLOCK:, off:off + w])
         for off, w in [(cols - first, first), *tail[:-1]]:
             h = off // half
-            x = finish(final, off, grid_rows - 1, l_rem, got[final, off], acc[h], off - h * half, x)
+            x = finish(final, off, grid_rows - 1, l_last, got[final, off], acc[h], off - h * half, x)
         off, w = tail[-1]
         return finish_last(final, off, grid_rows - 1, l_last, got[final, off], acc_last, x)
 

time: 574 us -> 557 us (0.970)
  local copies, waits for them, and re-layouts: 51.3 us -> 6.38 us
  Pallas kernels: 58.4 us -> 78.9 us
  waiting for transfers between devices: 426 us -> 437 us
  other arithmetic: 9.52 us -> 0 us
  starting transfers between devices: 27.9 us -> 34 us
    ppermute x15, waiting for transfers between devices: 370 us -> 437 us  [send(): lax.ppermute(piece, 'row', down_row if i and j == final else swap_row)]
    ppermute x3, waiting for transfers between devices: 55.9 us -> 0.01 us  [local_trmm(): lax.ppermute(tri_loc, 'col', [(c, c ^ d) for c in range(grid_cols)])]
    slice x15 -> x1, local copies, waits for them, and re-layouts: 39 us -> 0.97 us  [local_trmm(): send(len(order) - 1, source[final * BLOCK:, off:off + w])]
    pallas_call x0 -> x2, Pallas kernels: none -> 15.6 us  [cut_many(): pl.pallas_call(functools.partial(cut_many_kernel, places), in_specs=[pl.B...]
    select_n x3 -> x0, other arithmetic: 9.52 us -> none  [the longest x1 6.53 us: local_trmm(): l_own = jnp.where(matches, same, other)]
    unnamed x40 -> x14, local copies, waits for them, and re-layouts: 12.2 us -> 4.33 us
    ppermute x15, starting transfers between devices: 24.5 us -> 32 us  [send(): lax.ppermute(piece, 'row', down_row if i and j == final else swap_row)]
  transfers between devices with their start and end apart: 18 -> 18, of which waited for: 15 -> 14; matrix products, arithmetic and copies ran while one was open for 9% -> 0% of each run, Pallas kernels for 10% -> 12%
where the time goes in v6:
time: 557 us
  waiting for transfers between devices  437 us (78%)
  Pallas kernels  78.9 us (14%)
  starting transfers between devices  34 us (6%)
  local copies, waits for them, and re-layouts  6.38 us (1%)
    ppermute x15, waiting for transfers between devices, send(): lax.ppermute(piece, 'row', down_row if i and j == final else swap_row)  437 us
    pallas_call x2, Pallas kernels, bulk(): pl.pallas_call(functools.partial(bulk_kernel, steps, len(aliases)), grid=...  62.2 us
    ppermute x15, starting transfers between devices, send(): lax.ppermute(piece, 'row', down_row if i and j == final else swap_row)  32 us
    pallas_call x2, Pallas kernels, cut_many(): pl.pallas_call(functools.partial(cut_many_kernel, places), in_specs=[pl.B...  15.6 us
  transfers between devices with their start and end apart: 18, of which 14 were waited for; matrix products, arithmetic and copies ran while one was open for 0% of the time, Pallas kernels for 12%

profile of v6, /device:TPU:0, one launch (start us, length us, event | category | flops | bytes accessed | tf_op | source)
XLA Modules:
  0.0 556.7 jit_solution(10946039292338788096)
XLA Ops:
  0.0 13.9 %shard_map.28 = (bf16[256,4096]{1,0:T(8,128)(2,1)S(1)}, bf16[256,4096]{1,0:T(8,128)(2,1)S(1)}, bf16[256,4096]{1,0:T(8,128)(2,1)}, bf16[256,4096]{1,0:T(8,128)(2,...) custom-call(bf16[1536,8192]{1,0:T(8,128)(2,1)} %b_ref.5), custom_call_target="tpu_custom_call" | custom-call | flops 22544384 | bytes 45088768 | tf_op jit(solution)/shard_map/pallas_call | solution.py:212
  13.9 3.4 collective-permute-start.10
  17.3 2.0 collective-permute-start.12
  19.3 44.6 %collective-permute-done.10.refs_7_ = bf16[256,4096]{1,0:T(8,128)(2,1)S(1)} collective-permute-done((bf16[256,4096]{1,0:T(8,128)(2,1)}, bf16[256,4096]{1,0:T(8,128)(2,1)S(1)}, u32[]{:S(2)}, u32[]{:S(2)}) %collective-permute-start.10) | collective-permute-done | bytes 2097184 | tf_op jit(solution)/shard_map/ppermute | solution.py:246
  63.9 2.0 collective-permute-start.1
  67.7 41.3 %collective-permute-done.11.refs_8_ = bf16[256,4096]{1,0:T(8,128)(2,1)} collective-permute-done((bf16[256,4096]{1,0:T(8,128)(2,1)}, bf16[256,4096]{1,0:T(8,128)(2,1)}, u32[]{:S(2)}, u32[]{:S(2)}) %collective-permute-start.11) | collective-permute-done | bytes 2097184 | tf_op jit(solution)/shard_map/ppermute | solution.py:246
  109.0 2.0 collective-permute-start.8
  111.0 42.9 %collective-permute-done.12.refs_9_ = bf16[256,4096]{1,0:T(8,128)(2,1)} collective-permute-done((bf16[256,4096]{1,0:T(8,128)(2,1)}, bf16[256,4096]{1,0:T(8,128)(2,1)}, u32[]{:S(2)}, u32[]{:S(2)}) %collective-permute-start.12) | collective-permute-done | bytes 2097184 | tf_op jit(solution)/shard_map/ppermute | solution.py:246
  153.9 2.0 collective-permute-start.3
  155.9 42.9 %collective-permute-done.9.refs_6_ = bf16[256,4096]{1,0:T(8,128)(2,1)} collective-permute-done((bf16[256,4096]{1,0:T(8,128)(2,1)S(1)}, bf16[256,4096]{1,0:T(8,128)(2,1)}, u32[]{:S(2)}, u32[]{:S(2)}) %collective-permute-start.9) | collective-permute-done | bytes 2097184 | tf_op jit(solution)/shard_map/ppermute | solution.py:246
  198.8 44.8 %collective-permute-done.8.refs_5_ = bf16[256,4096]{1,0:T(8,128)(2,1)S(1)} collective-permute-done((bf16[256,4096]{1,0:T(8,128)(2,1)S(1)}, bf16[256,4096]{1,0:T(8,128)(2,1)S(1)}, u32[]{:S(2)}, u32[]{:S(2)}) %collective-permute-start.8) | collective-permute-done | bytes 2097184 | tf_op jit(solution)/shard_map/ppermute | solution.py:246
  243.7 2.0 collective-permute-start.4
  245.7 42.9 %collective-permute-done.3.refs_5_ = bf16[256,4096]{1,0:T(8,128)(2,1)S(1)} collective-permute-done((bf16[256,4096]{1,0:T(8,128)(2,1)S(1)}, bf16[256,4096]{1,0:T(8,128)(2,1)S(1)}, u32[]{:S(2)}, u32[]{:S(2)}) %collective-permute-start.3) | collective-permute-done | bytes 2097184 | tf_op jit(solution)/shard_map/ppermute | solution.py:246
  288.6 2.0 collective-permute-start.5
  290.7 2.0 collective-permute-start.7
  293.7 2.6 collective-permute-start.16
  296.3 31.1 %shard_map.30 = (bf16[1536,8192]{1,0:T(8,128)(2,1)}, f32[256,4096]{1,0:T(8,128)}, bf16[256,256]{1,0:T(8,128)(2,1)}) custom-call(bf16[1536,768]{1,0:T(8,128)(2,1)} %refs_0_.3, bf16[1536,768]{1,0:T(8,128)(2,1)} %collective-permute-done.refs_1_, bf16[1536,768]{1,0:T(8,128)(2,1)} %collective-permute-done.1.refs_2_, ...), custom_call_target="tpu_custom_call" | custom-call | flops 19327352832 | bytes 37748736 | tf_op jit(solution)/shard_map/pallas_call | solution.py:60
  327.4 6.3 %collective-permute-done.4.refs_6_ = bf16[256,4096]{1,0:T(8,128)(2,1)} collective-permute-done((bf16[256,4096]{1,0:T(8,128)(2,1)}, bf16[256,4096]{1,0:T(8,128)(2,1)}, u32[]{:S(2)}, u32[]{:S(2)}) %collective-permute-start.4) | collective-permute-done | bytes 2097184 | tf_op jit(solution)/shard_map/ppermute | solution.py:246
  333.7 2.0 collective-permute-start.17
  335.7 42.9 %collective-permute-done.5.refs_7_ = bf16[256,4096]{1,0:T(8,128)(2,1)} collective-permute-done((bf16[256,4096]{1,0:T(8,128)(2,1)}, bf16[256,4096]{1,0:T(8,128)(2,1)}, u32[]{:S(2)}, u32[]{:S(2)}) %collective-permute-start.5) | collective-permute-done | bytes 2097184 | tf_op jit(solution)/shard_map/ppermute | solution.py:246
  378.6 4.0 collective-permute-start.15
  382.6 41.0 %collective-permute-done.6.refs_8_ = bf16[256,4096]{1,0:T(8,128)(2,1)} collective-permute-done((bf16[256,4096]{1,0:T(8,128)(2,1)}, bf16[256,4096]{1,0:T(8,128)(2,1)}, u32[]{:S(2)}, u32[]{:S(2)}) %collective-permute-start.6) | collective-permute-done | bytes 2097184 | tf_op jit(solution)/shard_map/ppermute | solution.py:246
  423.5 3.9 collective-permute-start.14
  427.5 41.0 %collective-permute-done.7.refs_9_ = bf16[256,4096]{1,0:T(8,128)(2,1)} collective-permute-done((bf16[256,4096]{1,0:T(8,128)(2,1)S(1)}, bf16[256,4096]{1,0:T(8,128)(2,1)}, u32[]{:S(2)}, u32[]{:S(2)}) %collective-permute-start.7) | collective-permute-done | bytes 2097184 | tf_op jit(solution)/shard_map/ppermute | solution.py:246
  468.5 31.1 %shard_map.31 = (bf16[1536,8192]{1,0:T(8,128)(2,1)}, f32[256,4096]{1,0:T(8,128)}, bf16[256,256]{1,0:T(8,128)(2,1)S(1)}) custom-call(bf16[1536,768]{1,0:T(8,128)(2,1)} %refs_0_.3, bf16[1536,768]{1,0:T(8,128)(2,1)} %collective-permute-done.refs_1_, bf16[1536,768]{1,0:T(8,128)(2,1)} %collective-permute-done.1.refs_2_, ...), custom_call_target="tpu_custom_call", output_to_operand_aliasing={{0}: (10, {})} | custom-call | flops 19327352832 | bytes 37748736 | tf_op jit(solution)/shard_map/pallas_call | solution.py:60
  500.6 3.9 collective-permute-start.13
  504.5 14.0 %collective-permute-done.17.piece_ref = bf16[256,512]{1,0:T(8,128)(2,1)S(1)} collective-permute-done((bf16[256,512]{1,0:T(8,128)(2,1)S(1)}, bf16[256,512]{1,0:T(8,128)(2,1)S(1)}, u32[]{:S(2)}, u32[]{:S(2)}) %collective-permute-start.17) | collective-permute-done | bytes 262176 | tf_op jit(solution)/shard_map/ppermute | solution.py:246
  519.6 2.2 copy-done
  521.8 2.1 copy-done.2
  524.0 16.9 %collective-permute-done.15.b_ref = bf16[256,2048]{1,0:T(8,128)(2,1)S(1)} collective-permute-done((bf16[256,2048]{1,0:T(8,128)(2,1)S(1)}, bf16[256,2048]{1,0:T(8,128)(2,1)S(1)}, u32[]{:S(2)}, u32[]{:S(2)}) %collective-permute-start.15) | collective-permute-done | bytes 1048608 | tf_op jit(solution)/shard_map/ppermute | solution.py:246
  541.0 11.2 %collective-permute-done.14.b_ref = bf16[256,1024]{1,0:T(8,128)(2,1)S(1)} collective-permute-done((bf16[256,1024]{1,0:T(8,128)(2,1)S(1)}, bf16[256,1024]{1,0:T(8,128)(2,1)S(1)}, u32[]{:S(2)}, u32[]{:S(2)}) %collective-permute-start.14) | collective-permute-done | bytes 524320 | tf_op jit(solution)/shard_map/ppermute | solution.py:246
  552.2 4.4 collective-permute-done.13.b_ref
  (31 shorter events, 5.0 us)
Async XLA Ops:
  0.0 19.3 %copy-start.3 = (bf16[1536,768]{1,0:T(8,128)(2,1)S(1)}, bf16[1536,768]{1,0:T(8,128)(2,1)}, u32[]{:S(2)}) copy-start(bf16[1536,768]{1,0:T(8,128)(2,1)} %refs_0_.3) | copy-start | bytes 7077892
  13.9 50.0 %collective-permute-start.10 = (bf16[256,4096]{1,0:T(8,128)(2,1)}, bf16[256,4096]{1,0:T(8,128)(2,1)S(1)}, u32[]{:S(2)}, u32[]{:S(2)}) collective-permute-start(bf16[256,4096]{1,0:T(8,128)(2,1)} %get-tuple-element.30), channel_id=1, source_target_pairs={{0,4},{4,0},{1,5},{5,1},{2,6},{6,2},{3,7},{7,3}} | collective-permute-start | bytes 6291464 | tf_op jit(solution)/shard_map/ppermute | solution.py:246
  17.2 91.7 %collective-permute-start.11 = (bf16[256,4096]{1,0:T(8,128)(2,1)}, bf16[256,4096]{1,0:T(8,128)(2,1)}, u32[]{:S(2)}, u32[]{:S(2)}) collective-permute-start(bf16[256,4096]{1,0:T(8,128)(2,1)} %get-tuple-element.31), channel_id=1, source_target_pairs={{0,4},{4,0},{1,5},{5,1},{2,6},{6,2},{3,7},{7,3}} | collective-permute-start | bytes 6291464 | tf_op jit(solution)/shard_map/ppermute | solution.py:246
  17.3 136.6 %collective-permute-start.12 = (bf16[256,4096]{1,0:T(8,128)(2,1)}, bf16[256,4096]{1,0:T(8,128)(2,1)}, u32[]{:S(2)}, u32[]{:S(2)}) collective-permute-start(bf16[256,4096]{1,0:T(8,128)(2,1)} %get-tuple-element.32), channel_id=1, source_target_pairs={{0,4},{4,0},{1,5},{5,1},{2,6},{6,2},{3,7},{7,3}} | collective-permute-start | bytes 6291464 | tf_op jit(solution)/shard_map/ppermute | solution.py:246
  19.2 271.4 %copy-start.5 = (bf16[256,4096]{1,0:T(8,128)(2,1)S(1)}, bf16[256,4096]{1,0:T(8,128)(2,1)}, u32[]{:S(2)}) copy-start(bf16[256,4096]{1,0:T(8,128)(2,1)} %get-tuple-element.28) | copy-start | bytes 6291460
  19.2 179.6 %collective-permute-start.9 = (bf16[256,4096]{1,0:T(8,128)(2,1)S(1)}, bf16[256,4096]{1,0:T(8,128)(2,1)}, u32[]{:S(2)}, u32[]{:S(2)}) collective-permute-start(bf16[256,4096]{1,0:T(8,128)(2,1)S(1)} %get-tuple-element.29), channel_id=1, source_target_pairs={{0,4},{4,0},{1,5},{5,1},{2,6},{6,2},{3,7},{7,3}} | collective-permute-start | bytes 6291464 | tf_op jit(solution)/shard_map/ppermute | solution.py:246
  19.3 271.4 %collective-permute-start = (bf16[1536,768]{1,0:T(8,128)(2,1)S(1)}, bf16[1536,768]{1,0:T(8,128)(2,1)}, u32[]{:S(2)}, u32[]{:S(2)}) collective-permute-start(bf16[1536,768]{1,0:T(8,128)(2,1)S(1)} %copy-done.3), channel_id=1, source_target_pairs={{0,1},{1,0},{2,3},{3,2},{4,5},{5,4},{6,7},{7,6}} | collective-permute-start | bytes 7077896 | tf_op jit(solution)/shard_map/ppermute | solution.py:258
  63.9 3.8 copy-start.6
  63.9 226.8 %collective-permute-start.1 = (bf16[1536,768]{1,0:T(8,128)(2,1)S(1)}, bf16[1536,768]{1,0:T(8,128)(2,1)}, u32[]{:S(2)}, u32[]{:S(2)}) collective-permute-start(bf16[1536,768]{1,0:T(8,128)(2,1)S(1)} %copy-done.3), channel_id=1, source_target_pairs={{0,2},{1,3},{2,0},{3,1},{4,6},{5,7},{6,4},{7,5}} | collective-permute-start | bytes 7077896 | tf_op jit(solution)/shard_map/ppermute | solution.py:258
  109.0 134.7 %collective-permute-start.8 = (bf16[256,4096]{1,0:T(8,128)(2,1)S(1)}, bf16[256,4096]{1,0:T(8,128)(2,1)S(1)}, u32[]{:S(2)}, u32[]{:S(2)}) collective-permute-start(bf16[256,4096]{1,0:T(8,128)(2,1)S(1)} %shard_map.29), channel_id=1, source_target_pairs={{0,4},{4,0},{1,5},{5,1},{2,6},{6,2},{3,7},{7,3}} | collective-permute-start | bytes 6291464 | tf_op jit(solution)/shard_map/ppermute | solution.py:246
  153.9 134.7 %collective-permute-start.3 = (bf16[256,4096]{1,0:T(8,128)(2,1)S(1)}, bf16[256,4096]{1,0:T(8,128)(2,1)S(1)}, u32[]{:S(2)}, u32[]{:S(2)}) collective-permute-start(bf16[256,4096]{1,0:T(8,128)(2,1)S(1)} %get-tuple-element.24), channel_id=1, source_target_pairs={{0,4},{4,0},{1,5},{5,1},{2,6},{6,2},{3,7},{7,3}} | collective-permute-start | bytes 6291464 | tf_op jit(solution)/shard_map/ppermute | solution.py:246
  198.8 94.8 %collective-permute-start.2 = (bf16[1536,768]{1,0:T(8,128)(2,1)S(1)}, bf16[1536,768]{1,0:T(8,128)(2,1)}, u32[]{:S(2)}, u32[]{:S(2)}) collective-permute-start(bf16[1536,768]{1,0:T(8,128)(2,1)S(1)} %copy-done.3), channel_id=1, source_target_pairs={{0,3},{1,2},{2,1},{3,0},{4,7},{5,6},{6,5},{7,4}} | collective-permute-start | bytes 7077896 | tf_op jit(solution)/shard_map/ppermute | solution.py:258
  243.7 90.0 %collective-permute-start.4 = (bf16[256,4096]{1,0:T(8,128)(2,1)}, bf16[256,4096]{1,0:T(8,128)(2,1)}, u32[]{:S(2)}, u32[]{:S(2)}) collective-permute-start(bf16[256,4096]{1,0:T(8,128)(2,1)} %get-tuple-element.25), channel_id=1, source_target_pairs={{0,4},{4,0},{1,5},{5,1},{2,6},{6,2},{3,7},{7,3}} | collective-permute-start | bytes 6291464 | tf_op jit(solution)/shard_map/ppermute | solution.py:246
  288.6 90.0 %collective-permute-start.5 = (bf16[256,4096]{1,0:T(8,128)(2,1)}, bf16[256,4096]{1,0:T(8,128)(2,1)}, u32[]{:S(2)}, u32[]{:S(2)}) collective-permute-start(bf16[256,4096]{1,0:T(8,128)(2,1)} %get-tuple-element.26), channel_id=1, source_target_pairs={{0,4},{4,0},{1,5},{5,1},{2,6},{6,2},{3,7},{7,3}} | collective-permute-start | bytes 6291464 | tf_op jit(solution)/shard_map/ppermute | solution.py:246
  290.6 132.9 %collective-permute-start.6 = (bf16[256,4096]{1,0:T(8,128)(2,1)}, bf16[256,4096]{1,0:T(8,128)(2,1)}, u32[]{:S(2)}, u32[]{:S(2)}) collective-permute-start(bf16[256,4096]{1,0:T(8,128)(2,1)} %get-tuple-element.27), channel_id=1, source_target_pairs={{0,4},{4,0},{1,5},{5,1},{2,6},{6,2},{3,7},{7,3}} | collective-permute-start | bytes 6291464 | tf_op jit(solution)/shard_map/ppermute | solution.py:246
  290.7 3.0 copy-start.4
  290.7 177.8 %collective-permute-start.7 = (bf16[256,4096]{1,0:T(8,128)(2,1)S(1)}, bf16[256,4096]{1,0:T(8,128)(2,1)}, u32[]{:S(2)}, u32[]{:S(2)}) collective-permute-start(bf16[256,4096]{1,0:T(8,128)(2,1)S(1)} %copy-done.5), channel_id=1, source_target_pairs={{0,4},{4,0},{1,5},{5,1},{2,6},{6,2},{3,7},{7,3}} | collective-permute-start | bytes 6291464 | tf_op jit(solution)/shard_map/ppermute | solution.py:246
  293.7 228.1 %collective-permute-start.16 = (bf16[256,4096]{1,0:T(8,128)(2,1)S(1)}, bf16[256,4096]{1,0:T(8,128)(2,1)S(1)}, u32[]{:S(2)}, u32[]{:S(2)}) collective-permute-start(bf16[256,4096]{1,0:T(8,128)(2,1)S(1)} %copy-done.4), channel_id=1, source_target_pairs={{0,4},{1,5},{2,6},{3,7}} | collective-permute-start | bytes 6291464 | tf_op jit(solution)/shard_map/ppermute | solution.py:246
  333.7 184.8 %collective-permute-start.17 = (bf16[256,512]{1,0:T(8,128)(2,1)S(1)}, bf16[256,512]{1,0:T(8,128)(2,1)S(1)}, u32[]{:S(2)}, u32[]{:S(2)}) collective-permute-start(bf16[256,512]{1,0:T(8,128)(2,1)S(1)} %shard_map.32), channel_id=1, source_target_pairs={{0,4},{4,0},{1,5},{5,1},{2,6},{6,2},{3,7},{7,3}} | collective-permute-start | bytes 786440 | tf_op jit(solution)/shard_map/ppermute | solution.py:246
  378.6 162.3 %collective-permute-start.15 = (bf16[256,2048]{1,0:T(8,128)(2,1)S(1)}, bf16[256,2048]{1,0:T(8,128)(2,1)S(1)}, u32[]{:S(2)}, u32[]{:S(2)}) collective-permute-start(bf16[256,2048]{1,0:T(8,128)(2,1)S(1)} %get-tuple-element.39), channel_id=1, source_target_pairs={{0,4},{1,5},{2,6},{3,7}} | collective-permute-start | bytes 3145736 | tf_op jit(solution)/shard_map/ppermute | solution.py:246
  423.5 128.6 %collective-permute-start.14 = (bf16[256,1024]{1,0:T(8,128)(2,1)S(1)}, bf16[256,1024]{1,0:T(8,128)(2,1)S(1)}, u32[]{:S(2)}, u32[]{:S(2)}) collective-permute-start(bf16[256,1024]{1,0:T(8,128)(2,1)S(1)} %get-tuple-element.37), channel_id=1, source_target_pairs={{0,4},{1,5},{2,6},{3,7}} | collective-permute-start | bytes 1572872 | tf_op jit(solution)/shard_map/ppermute | solution.py:246
  500.6 56.1 %collective-permute-start.13 = (bf16[256,512]{1,0:T(8,128)(2,1)S(1)}, bf16[256,512]{1,0:T(8,128)(2,1)S(1)}, u32[]{:S(2)}, u32[]{:S(2)}) collective-permute-start(bf16[256,512]{1,0:T(8,128)(2,1)S(1)} %slice.6), channel_id=1, source_target_pairs={{0,4},{1,5},{2,6},{3,7}} | collective-permute-start | bytes 786440 | tf_op jit(solution)/shard_map/ppermute | solution.py:246
  519.6 2.2 copy-start
  521.8 2.2 copy-start.2
  524.0 17.0 %copy-start.1 = (f32[256,4096]{1,0:T(8,128)S(1)}, f32[256,4096]{1,0:T(8,128)}, u32[]{:S(2)}) copy-start(f32[256,4096]{1,0:T(8,128)} %get-tuple-element.38.acc_ref) | copy-start | bytes 12582916

commit v7 on v6

--- a/solution.py
+++ b/solution.py
@@ -11,9 +11,9 @@
 BLOCK = 256
 
 
-def bulk_kernel(steps, aliased, *refs):
+def bulk_kernel(steps, aliased, early, *refs):
     l_refs, bo_ref, rem_refs = refs[:4], refs[4], refs[5:4 + steps]
-    x_ref, acc_ref, last_ref, l_buf, sems = refs[4 + steps + aliased:]
+    x_ref, acc_ref, last_ref, l_buf, sems = refs[4 + steps + aliased + early:]
 
     @pl.when(pl.program_id(0) == 0)
     def _():
@@ -42,8 +42,16 @@
         x_ref[rows, :] = acc.astype(x_ref.dtype)
     acc_ref[...] = acc
 
-
-def bulk(start, tile, l_parts, b_own, pieces, x):
+    if early:
+        early_ref = refs[4 + steps]
+
+        @pl.when((pl.program_id(0) == pl.num_programs(0) - 1) & (lax.axis_index("row") == 1))
+        def _():
+            done = acc_ref[...] + jnp.dot(last_ref[...], early_ref[...], preferred_element_type=jnp.float32)
+            x_ref[(steps - 1) * BLOCK:, :] = done.astype(x_ref.dtype)
+
+
+def bulk(start, tile, l_parts, b_own, pieces, early, x):
     rows, cols = b_own.shape
     steps = rows // BLOCK
     width = pieces[0].shape[1]
@@ -52,13 +60,16 @@
     in_specs = [pl.BlockSpec(memory_space=pltpu.HBM)] * 4 + [column]
     in_specs += [pl.BlockSpec((BLOCK, tile), lambda n: (0, n))] * (steps - 1)
     args = [*l_parts, b_own, *pieces]
+    if early is not None:
+        args.append(early)
+        in_specs.append(pl.BlockSpec((BLOCK, tile), lambda n: (0, 0)))
     aliases = {}
     if x is not None:
         aliases = {len(args): 0}
         args.append(x)
         in_specs.append(pl.BlockSpec(memory_space=pltpu.HBM))
     return pl.pallas_call(
-        functools.partial(bulk_kernel, steps, len(aliases)),
+        functools.partial(bulk_kernel, steps, len(aliases), int(early is not None)),
         grid=(width // tile,),
         in_specs=in_specs,
         out_specs=[column, pl.BlockSpec((BLOCK, tile), lambda n: (0, n)), pl.BlockSpec((BLOCK, BLOCK), lambda n: (0, 0))],
@@ -260,12 +271,13 @@
 
         x, acc = None, [None, None]
         for h in range(2):
-            x, acc[h], l_last = bulk(h * half, 512, l_parts, rhs_loc, [got[k, h * half] for k in range(final)], x)
+            early = got[final, cols - first] if h == 1 else None
+            x, acc[h], l_last = bulk(h * half, first, l_parts, rhs_loc, [got[k, h * half] for k in range(final)], early, x)
         off, w = tail[-1]
         acc_last = acc[1][:, off - half:off - half + w]
         source, acc[1] = lax.optimization_barrier((rhs_loc, acc[1]))
         send(len(order) - 1, source[final * BLOCK:, off:off + w])
-        for off, w in [(cols - first, first), *tail[:-1]]:
+        for off, w in tail[:-1]:
             h = off // half
             x = finish(final, off, grid_rows - 1, l_last, got[final, off], acc[h], off - h * half, x)
         off, w = tail[-1]

time: 557 us -> 551 us (0.989)
  starting transfers between devices: 34 us -> 28.4 us
    ppermute x15, waiting for transfers between devices: 437 us -> 431 us  [send(): lax.ppermute(piece, 'row', down_row if i and j == final else swap_row)]
  transfers between devices with their start and end apart: 18 -> 18, of which waited for: 14 -> 10; matrix products, arithmetic and copies ran while one was open for 0% -> 0% of each run, Pallas kernels for 12% -> 14%
where the time goes in v7:
time: 551 us; the launch traced here: 550 us
  waiting for transfers between devices  436 us (79%)
  Pallas kernels  79 us (14%)
  starting transfers between devices  28.4 us (5%)
  local copies, waits for them, and re-layouts  6.37 us (1%)
    ppermute x15, waiting for transfers between devices, send(): lax.ppermute(piece, 'row', down_row if i and j == final else swap_row)  431 us
    pallas_call x2, Pallas kernels, bulk(): pl.pallas_call(functools.partial(bulk_kernel, steps, len(aliases), int(ea...  62.4 us
    ppermute x15, starting transfers between devices, send(): lax.ppermute(piece, 'row', down_row if i and j == final else swap_row)  26.7 us
    pallas_call x2, Pallas kernels, cut_many(): pl.pallas_call(functools.partial(cut_many_kernel, places), in_specs=[pl.B...  15.3 us
  transfers between devices with their start and end apart: 18, of which 10 were waited for; matrix products, arithmetic and copies ran while one was open for 0% of the time, Pallas kernels for 14%

profile of v7, /device:TPU:0, one launch (start us, length us, event | category | flops | bytes accessed | tf_op | source)
XLA Modules:
  0.0 550.3 jit_solution(16120201111717970133)
XLA Ops:
  0.0 1.7 shard_map.31
  1.8 3.4 collective-permute-start.9
  5.1 13.6 %shard_map.28 = (bf16[256,4096]{1,0:T(8,128)(2,1)S(1)}, bf16[256,4096]{1,0:T(8,128)(2,1)S(1)}, bf16[256,4096]{1,0:T(8,128)(2,1)}, bf16[256,4096]{1,0:T(8,128)(2,...) custom-call(bf16[1536,8192]{1,0:T(8,128)(2,1)} %refs_4_.3), custom_call_target="tpu_custom_call" | custom-call | flops 22544384 | bytes 45088768 | tf_op jit(solution)/shard_map/pallas_call | solution.py:223
  18.7 2.0 collective-permute-start.10
  20.8 1.1 shard_map.29
  21.9 0.9 collective-permute-start.8
  22.8 168.4 %collective-permute-done.8.piece_ref = bf16[256,512]{1,0:T(8,128)(2,1)S(1)} collective-permute-done((bf16[256,512]{1,0:T(8,128)(2,1)S(1)}, bf16[256,512]{1,0:T(8,128)(2,1)S(1)}, u32[]{:S(2)}, u32[]{:S(2)}) %collective-permute-start.8) | collective-permute-done | bytes 262176 | tf_op jit(solution)/shard_map/ppermute | solution.py:257
  191.5 1.3 copy-done.2
  192.8 1.4 collective-permute-start.1
  194.2 1.5 collective-permute-start.12
  196.3 46.7 %collective-permute-done.12.refs_8_ = bf16[256,4096]{1,0:T(8,128)(2,1)S(1)} collective-permute-done((bf16[256,4096]{1,0:T(8,128)(2,1)}, bf16[256,4096]{1,0:T(8,128)(2,1)S(1)}, u32[]{:S(2)}, u32[]{:S(2)}) %collective-permute-start.12) | collective-permute-done | bytes 2097184 | tf_op jit(solution)/shard_map/ppermute | solution.py:257
  242.9 1.5 collective-permute-start.4
  244.5 43.4 %collective-permute-done.13.refs_9_ = bf16[256,4096]{1,0:T(8,128)(2,1)S(1)} collective-permute-done((bf16[256,4096]{1,0:T(8,128)(2,1)}, bf16[256,4096]{1,0:T(8,128)(2,1)S(1)}, u32[]{:S(2)}, u32[]{:S(2)}) %collective-permute-start.13) | collective-permute-done | bytes 2097184 | tf_op jit(solution)/shard_map/ppermute | solution.py:257
  287.9 1.5 collective-permute-start.5
  289.9 5.4 collective-permute-done.1.refs_2_
  295.3 1.7 collective-permute-start.7
  297.1 1.4 copy-done.7
  298.5 2.7 collective-permute-start.17
  301.2 1.6 copy-done.3
  302.8 31.0 %shard_map.32 = (bf16[1536,8192]{1,0:T(8,128)(2,1)}, f32[256,4096]{1,0:T(8,128)}, bf16[256,256]{1,0:T(8,128)(2,1)}) custom-call(bf16[1536,768]{1,0:T(8,128)(2,1)} %refs_0_.3, bf16[1536,768]{1,0:T(8,128)(2,1)} %copy-done.7, bf16[1536,768]{1,0:T(8,128)(2,1)} %copy-done.6, bf16[1536,768]{1,0:T(8,128)(2,1)} %copy-done.5, bf16[1536,8192]{1,0:T(8,128)(2,1)} %refs_4_.3, ...), custom_call_target="tpu_custom_call" | custom-call | flops 19327352832 | bytes 37748736 | tf_op jit(solution)/shard_map/pallas_call | solution.py:71
  333.9 2.4 collective-permute-start.15
  336.3 41.5 %collective-permute-done.5.refs_7_ = bf16[256,4096]{1,0:T(8,128)(2,1)S(1)} collective-permute-done((bf16[256,4096]{1,0:T(8,128)(2,1)}, bf16[256,4096]{1,0:T(8,128)(2,1)S(1)}, u32[]{:S(2)}, u32[]{:S(2)}) %collective-permute-start.5) | collective-permute-done | bytes 2097184 | tf_op jit(solution)/shard_map/ppermute | solution.py:257
  377.8 3.5 collective-permute-start.16
  381.2 41.6 %collective-permute-done.6.refs_8_ = bf16[256,4096]{1,0:T(8,128)(2,1)} collective-permute-done((bf16[256,4096]{1,0:T(8,128)(2,1)}, bf16[256,4096]{1,0:T(8,128)(2,1)}, u32[]{:S(2)}, u32[]{:S(2)}) %collective-permute-start.6) | collective-permute-done | bytes 2097184 | tf_op jit(solution)/shard_map/ppermute | solution.py:257
  422.8 44.1 %collective-permute-done.7.refs_9_ = bf16[256,4096]{1,0:T(8,128)(2,1)} collective-permute-done((bf16[256,4096]{1,0:T(8,128)(2,1)}, bf16[256,4096]{1,0:T(8,128)(2,1)}, u32[]{:S(2)}, u32[]{:S(2)}) %collective-permute-start.7) | collective-permute-done | bytes 2097184 | tf_op jit(solution)/shard_map/ppermute | solution.py:257
  466.9 31.4 %shard_map.33 = (bf16[1536,8192]{1,0:T(8,128)(2,1)}, f32[256,4096]{1,0:T(8,128)}, bf16[256,256]{1,0:T(8,128)(2,1)S(1)}) custom-call(bf16[1536,768]{1,0:T(8,128)(2,1)} %refs_0_.3, bf16[1536,768]{1,0:T(8,128)(2,1)} %copy-done.7, bf16[1536,768]{1,0:T(8,128)(2,1)} %copy-done.6, bf16[1536,768]{1,0:T(8,128)(2,1)} %copy-done.5, ...), custom_call_target="tpu_custom_call", output_to_operand_aliasing={{0}: (11, {})} | custom-call | flops 19327352832 | bytes 37748736 | tf_op jit(solution)/shard_map/pallas_call | solution.py:71
  498.3 1.0 slice.6
  499.3 4.5 collective-permute-start.14
  503.8 1.1 slice.7.acc_ref
  504.9 6.9 %collective-permute-done.17.b_ref = bf16[256,4096]{1,0:T(8,128)(2,1)S(1)} collective-permute-done((bf16[256,4096]{1,0:T(8,128)(2,1)}, bf16[256,4096]{1,0:T(8,128)(2,1)S(1)}, u32[]{:S(2)}, u32[]{:S(2)}) %collective-permute-start.17) | collective-permute-done | bytes 2097184 | tf_op jit(solution)/shard_map/ppermute | solution.py:257
  511.8 33.6 %collective-permute-done.16.b_ref = bf16[256,2048]{1,0:T(8,128)(2,1)S(1)} collective-permute-done((bf16[256,2048]{1,0:T(8,128)(2,1)S(1)}, bf16[256,2048]{1,0:T(8,128)(2,1)S(1)}, u32[]{:S(2)}, u32[]{:S(2)}) %collective-permute-start.16) | collective-permute-done | bytes 1048608 | tf_op jit(solution)/shard_map/ppermute | solution.py:257
  545.4 4.9 collective-permute-done.14.b_ref
  (40 shorter events, 1.6 us)
Async XLA Ops:
  1.8 189.7 %collective-permute-start.9 = (bf16[256,4096]{1,0:T(8,128)(2,1)S(1)}, bf16[256,4096]{1,0:T(8,128)(2,1)S(1)}, u32[]{:S(2)}, u32[]{:S(2)}) collective-permute-start(bf16[256,4096]{1,0:T(8,128)(2,1)S(1)} %shard_map.31), channel_id=1, source_target_pairs={{0,4},{4,0},{1,5},{5,1},{2,6},{6,2},{3,7},{7,3}} | collective-permute-start | bytes 6291464 | tf_op jit(solution)/shard_map/ppermute | solution.py:257
  18.7 175.5 %collective-permute-start.3 = (bf16[256,4096]{1,0:T(8,128)(2,1)S(1)}, bf16[256,4096]{1,0:T(8,128)(2,1)S(1)}, u32[]{:S(2)}, u32[]{:S(2)}) collective-permute-start(bf16[256,4096]{1,0:T(8,128)(2,1)S(1)} %get-tuple-element.24), channel_id=1, source_target_pairs={{0,4},{4,0},{1,5},{5,1},{2,6},{6,2},{3,7},{7,3}} | collective-permute-start | bytes 6291464 | tf_op jit(solution)/shard_map/ppermute | solution.py:257
  18.7 177.0 %collective-permute-start.10 = (bf16[256,4096]{1,0:T(8,128)(2,1)S(1)}, bf16[256,4096]{1,0:T(8,128)(2,1)}, u32[]{:S(2)}, u32[]{:S(2)}) collective-permute-start(bf16[256,4096]{1,0:T(8,128)(2,1)S(1)} %get-tuple-element.29), channel_id=1, source_target_pairs={{0,4},{4,0},{1,5},{5,1},{2,6},{6,2},{3,7},{7,3}} | collective-permute-start | bytes 6291464 | tf_op jit(solution)/shard_map/ppermute | solution.py:257
  20.7 170.5 %copy-start.4 = (bf16[1536,768]{1,0:T(8,128)(2,1)S(1)}, bf16[1536,768]{1,0:T(8,128)(2,1)}, u32[]{:S(2)}) copy-start(bf16[1536,768]{1,0:T(8,128)(2,1)} %refs_0_.3) | copy-start | bytes 7077892
  20.7 175.5 %collective-permute-start.11 = (bf16[256,4096]{1,0:T(8,128)(2,1)}, bf16[256,4096]{1,0:T(8,128)(2,1)}, u32[]{:S(2)}, u32[]{:S(2)}) collective-permute-start(bf16[256,4096]{1,0:T(8,128)(2,1)} %get-tuple-element.30), channel_id=1, source_target_pairs={{0,4},{4,0},{1,5},{5,1},{2,6},{6,2},{3,7},{7,3}} | collective-permute-start | bytes 6291464 | tf_op jit(solution)/shard_map/ppermute | solution.py:257
  21.9 169.3 %collective-permute-start.8 = (bf16[256,512]{1,0:T(8,128)(2,1)S(1)}, bf16[256,512]{1,0:T(8,128)(2,1)S(1)}, u32[]{:S(2)}, u32[]{:S(2)}) collective-permute-start(bf16[256,512]{1,0:T(8,128)(2,1)S(1)} %shard_map.29), channel_id=1, source_target_pairs={{0,4},{4,0},{1,5},{5,1},{2,6},{6,2},{3,7},{7,3}} | collective-permute-start | bytes 786440 | tf_op jit(solution)/shard_map/ppermute | solution.py:257
  191.2 98.2 %collective-permute-start.2 = (bf16[1536,768]{1,0:T(8,128)(2,1)S(1)}, bf16[1536,768]{1,0:T(8,128)(2,1)S(1)}, u32[]{:S(2)}, u32[]{:S(2)}) collective-permute-start(bf16[1536,768]{1,0:T(8,128)(2,1)S(1)} %copy-done.4), channel_id=1, source_target_pairs={{0,3},{1,2},{2,1},{3,0},{4,7},{5,6},{6,5},{7,4}} | collective-permute-start | bytes 7077896 | tf_op jit(solution)/shard_map/ppermute | solution.py:269
  191.5 1.3 copy-start.2
  192.8 102.5 %collective-permute-start.1 = (bf16[1536,768]{1,0:T(8,128)(2,1)S(1)}, bf16[1536,768]{1,0:T(8,128)(2,1)S(1)}, u32[]{:S(2)}, u32[]{:S(2)}) collective-permute-start(bf16[1536,768]{1,0:T(8,128)(2,1)S(1)} %copy-done.4), channel_id=1, source_target_pairs={{0,2},{1,3},{2,0},{3,1},{4,6},{5,7},{6,4},{7,5}} | collective-permute-start | bytes 7077896 | tf_op jit(solution)/shard_map/ppermute | solution.py:269
  194.2 48.7 %collective-permute-start.12 = (bf16[256,4096]{1,0:T(8,128)(2,1)}, bf16[256,4096]{1,0:T(8,128)(2,1)S(1)}, u32[]{:S(2)}, u32[]{:S(2)}) collective-permute-start(bf16[256,4096]{1,0:T(8,128)(2,1)} %get-tuple-element.31), channel_id=1, source_target_pairs={{0,4},{4,0},{1,5},{5,1},{2,6},{6,2},{3,7},{7,3}} | collective-permute-start | bytes 6291464 | tf_op jit(solution)/shard_map/ppermute | solution.py:257
  195.7 92.1 %collective-permute-start.13 = (bf16[256,4096]{1,0:T(8,128)(2,1)}, bf16[256,4096]{1,0:T(8,128)(2,1)S(1)}, u32[]{:S(2)}, u32[]{:S(2)}) collective-permute-start(bf16[256,4096]{1,0:T(8,128)(2,1)} %get-tuple-element.32), channel_id=1, source_target_pairs={{0,4},{4,0},{1,5},{5,1},{2,6},{6,2},{3,7},{7,3}} | collective-permute-start | bytes 6291464 | tf_op jit(solution)/shard_map/ppermute | solution.py:257
  196.3 100.8 %collective-permute-start = (bf16[1536,768]{1,0:T(8,128)(2,1)S(1)}, bf16[1536,768]{1,0:T(8,128)(2,1)S(1)}, u32[]{:S(2)}, u32[]{:S(2)}) collective-permute-start(bf16[1536,768]{1,0:T(8,128)(2,1)S(1)} %copy-done.4), channel_id=1, source_target_pairs={{0,1},{1,0},{2,3},{3,2},{4,5},{5,4},{6,7},{7,6}} | collective-permute-start | bytes 7077896 | tf_op jit(solution)/shard_map/ppermute | solution.py:269
  242.9 54.2 %copy-start.10 = (bf16[256,4096]{1,0:T(8,128)(2,1)}, bf16[256,4096]{1,0:T(8,128)(2,1)S(1)}, u32[]{:S(2)}) copy-start(bf16[256,4096]{1,0:T(8,128)(2,1)S(1)} %collective-permute-done.12.refs_8_) | copy-start | bytes 6291460
  242.9 91.0 %collective-permute-start.4 = (bf16[256,4096]{1,0:T(8,128)(2,1)}, bf16[256,4096]{1,0:T(8,128)(2,1)S(1)}, u32[]{:S(2)}, u32[]{:S(2)}) collective-permute-start(bf16[256,4096]{1,0:T(8,128)(2,1)} %get-tuple-element.25), channel_id=1, source_target_pairs={{0,4},{4,0},{1,5},{5,1},{2,6},{6,2},{3,7},{7,3}} | collective-permute-start | bytes 6291464 | tf_op jit(solution)/shard_map/ppermute | solution.py:257
  287.9 9.2 %copy-start.11 = (bf16[256,4096]{1,0:T(8,128)(2,1)}, bf16[256,4096]{1,0:T(8,128)(2,1)S(1)}, u32[]{:S(2)}) copy-start(bf16[256,4096]{1,0:T(8,128)(2,1)S(1)} %collective-permute-done.13.refs_9_) | copy-start | bytes 6291460
  287.9 89.9 %collective-permute-start.5 = (bf16[256,4096]{1,0:T(8,128)(2,1)}, bf16[256,4096]{1,0:T(8,128)(2,1)S(1)}, u32[]{:S(2)}, u32[]{:S(2)}) collective-permute-start(bf16[256,4096]{1,0:T(8,128)(2,1)} %get-tuple-element.26), channel_id=1, source_target_pairs={{0,4},{4,0},{1,5},{5,1},{2,6},{6,2},{3,7},{7,3}} | collective-permute-start | bytes 6291464 | tf_op jit(solution)/shard_map/ppermute | solution.py:257
  289.4 7.7 %copy-start.5 = (bf16[1536,768]{1,0:T(8,128)(2,1)}, bf16[1536,768]{1,0:T(8,128)(2,1)S(1)}, u32[]{:S(2)}) copy-start(bf16[1536,768]{1,0:T(8,128)(2,1)S(1)} %collective-permute-done.2.refs_3_) | copy-start | bytes 7077892
  289.4 133.4 %collective-permute-start.6 = (bf16[256,4096]{1,0:T(8,128)(2,1)}, bf16[256,4096]{1,0:T(8,128)(2,1)}, u32[]{:S(2)}, u32[]{:S(2)}) collective-permute-start(bf16[256,4096]{1,0:T(8,128)(2,1)} %get-tuple-element.27), channel_id=1, source_target_pairs={{0,4},{4,0},{1,5},{5,1},{2,6},{6,2},{3,7},{7,3}} | collective-permute-start | bytes 6291464 | tf_op jit(solution)/shard_map/ppermute | solution.py:257
  295.3 1.8 copy-start.6
  295.3 171.6 %collective-permute-start.7 = (bf16[256,4096]{1,0:T(8,128)(2,1)}, bf16[256,4096]{1,0:T(8,128)(2,1)}, u32[]{:S(2)}, u32[]{:S(2)}) collective-permute-start(bf16[256,4096]{1,0:T(8,128)(2,1)} %get-tuple-element.28), channel_id=1, source_target_pairs={{0,4},{4,0},{1,5},{5,1},{2,6},{6,2},{3,7},{7,3}} | collective-permute-start | bytes 6291464 | tf_op jit(solution)/shard_map/ppermute | solution.py:257
  297.1 1.4 copy-start.7
  298.5 213.2 %collective-permute-start.17 = (bf16[256,4096]{1,0:T(8,128)(2,1)}, bf16[256,4096]{1,0:T(8,128)(2,1)S(1)}, u32[]{:S(2)}, u32[]{:S(2)}) collective-permute-start(bf16[256,4096]{1,0:T(8,128)(2,1)} %get-tuple-element.40), channel_id=1, source_target_pairs={{0,4},{1,5},{2,6},{3,7}} | collective-permute-start | bytes 6291464 | tf_op jit(solution)/shard_map/ppermute | solution.py:257
  301.2 1.6 copy-start.3
  333.9 133.0 %copy-start.8 = (bf16[256,4096]{1,0:T(8,128)(2,1)}, bf16[256,4096]{1,0:T(8,128)(2,1)S(1)}, u32[]{:S(2)}) copy-start(bf16[256,4096]{1,0:T(8,128)(2,1)S(1)} %collective-permute-done.4.refs_6_) | copy-start | bytes 6291460
  333.9 211.5 %collective-permute-start.15 = (bf16[256,1024]{1,0:T(8,128)(2,1)S(1)}, bf16[256,1024]{1,0:T(8,128)(2,1)S(1)}, u32[]{:S(2)}, u32[]{:S(2)}) collective-permute-start(bf16[256,1024]{1,0:T(8,128)(2,1)S(1)} %get-tuple-element.37), channel_id=1, source_target_pairs={{0,4},{1,5},{2,6},{3,7}} | collective-permute-start | bytes 1572872 | tf_op jit(solution)/shard_map/ppermute | solution.py:257
  377.8 89.2 %copy-start.9 = (bf16[256,4096]{1,0:T(8,128)(2,1)}, bf16[256,4096]{1,0:T(8,128)(2,1)S(1)}, u32[]{:S(2)}) copy-start(bf16[256,4096]{1,0:T(8,128)(2,1)S(1)} %collective-permute-done.5.refs_7_) | copy-start | bytes 6291460
  377.8 167.6 %collective-permute-start.16 = (bf16[256,2048]{1,0:T(8,128)(2,1)S(1)}, bf16[256,2048]{1,0:T(8,128)(2,1)S(1)}, u32[]{:S(2)}, u32[]{:S(2)}) collective-permute-start(bf16[256,2048]{1,0:T(8,128)(2,1)S(1)} %get-tuple-element.39), channel_id=1, source_target_pairs={{0,4},{1,5},{2,6},{3,7}} | collective-permute-start | bytes 3145736 | tf_op jit(solution)/shard_map/ppermute | solution.py:257
  466.9 44.8 %copy-start.1 = (f32[256,4096]{1,0:T(8,128)S(1)}, f32[256,4096]{1,0:T(8,128)}, u32[]{:S(2)}) copy-start(f32[256,4096]{1,0:T(8,128)} %get-tuple-element.41.acc_ref) | copy-start | bytes 12582916
  499.3 51.0 %collective-permute-start.14 = (bf16[256,512]{1,0:T(8,128)(2,1)S(1)}, bf16[256,512]{1,0:T(8,128)(2,1)S(1)}, u32[]{:S(2)}, u32[]{:S(2)}) collective-permute-start(bf16[256,512]{1,0:T(8,128)(2,1)S(1)} %slice.6), channel_id=1, source_target_pairs={{0,4},{1,5},{2,6},{3,7}} | collective-permute-start | bytes 786440 | tf_op jit(solution)/shard_map/ppermute | solution.py:257
  511.7 33.6 %copy-start = (f32[256,4096]{1,0:T(8,128)S(1)}, f32[256,4096]{1,0:T(8,128)}, u32[]{:S(2)}) copy-start(f32[256,4096]{1,0:T(8,128)} %get-tuple-element.38.acc_ref) | copy-start | bytes 12582916

commit v8 on v6

--- a/solution.py
+++ b/solution.py
@@ -11,9 +11,11 @@
 BLOCK = 256
 
 
-def bulk_kernel(steps, aliased, *refs):
-    l_refs, bo_ref, rem_refs = refs[:4], refs[4], refs[5:4 + steps]
-    x_ref, acc_ref, last_ref, l_buf, sems = refs[4 + steps + aliased:]
+def bulk_kernel(steps, *refs):
+    l_refs, bo_ref, early_ref = refs[:4], refs[4], refs[5]
+    rem_refs = [refs[6 + h * (steps - 1):6 + (h + 1) * (steps - 1)] for h in range(2)]
+    x_ref, acc_ref, last_ref, l_buf, sems = refs[4 + 2 * steps:]
+    tile_id, tiles = pl.program_id(0), pl.num_programs(0)
 
     @pl.when(pl.program_id(0) == 0)
     def _():
@@ -32,47 +34,49 @@
             copy.wait()
         last_ref[...] = l_buf[1, (steps - 1) * BLOCK:, (steps - 1) * BLOCK:]
 
-    for step in range(steps):
-        rows = slice(step * BLOCK, (step + 1) * BLOCK)
-        depth = (step + 1) * BLOCK
-        acc = jnp.dot(l_buf[0, rows, :depth], bo_ref[:depth, :], preferred_element_type=jnp.float32)
-        for j in range(min(step + 1, steps - 1)):
-            columns = slice(j * BLOCK, (j + 1) * BLOCK)
-            acc += jnp.dot(l_buf[1, rows, columns], rem_refs[j][...], preferred_element_type=jnp.float32)
-        x_ref[rows, :] = acc.astype(x_ref.dtype)
-    acc_ref[...] = acc
-
-
-def bulk(start, tile, l_parts, b_own, pieces, x):
+    def multiply(received):
+        for step in range(steps):
+            rows = slice(step * BLOCK, (step + 1) * BLOCK)
+            depth = (step + 1) * BLOCK
+            acc = jnp.dot(l_buf[0, rows, :depth], bo_ref[:depth, :], preferred_element_type=jnp.float32)
+            for j in range(min(step + 1, steps - 1)):
+                columns = slice(j * BLOCK, (j + 1) * BLOCK)
+                acc += jnp.dot(l_buf[1, rows, columns], received[j][...], preferred_element_type=jnp.float32)
+            x_ref[rows, :] = acc.astype(x_ref.dtype)
+        acc_ref[...] = acc
+
+    for h in range(2):
+        pl.when(tile_id // (tiles // 2) == h)(functools.partial(multiply, rem_refs[h]))
+
+    @pl.when((tile_id == tiles - 1) & (lax.axis_index("row") == 1))
+    def _():
+        done = acc_ref[...] + jnp.dot(last_ref[...], early_ref[...], preferred_element_type=jnp.float32)
+        x_ref[(steps - 1) * BLOCK:, :] = done.astype(x_ref.dtype)
+
+
+def bulk(tile, l_parts, b_own, early, halves):
     rows, cols = b_own.shape
     steps = rows // BLOCK
-    width = pieces[0].shape[1]
-    base = start // tile
-    column = pl.BlockSpec((rows, tile), lambda n: (0, base + n))
-    in_specs = [pl.BlockSpec(memory_space=pltpu.HBM)] * 4 + [column]
-    in_specs += [pl.BlockSpec((BLOCK, tile), lambda n: (0, n))] * (steps - 1)
-    args = [*l_parts, b_own, *pieces]
-    aliases = {}
-    if x is not None:
-        aliases = {len(args): 0}
-        args.append(x)
-        in_specs.append(pl.BlockSpec(memory_space=pltpu.HBM))
-    return pl.pallas_call(
-        functools.partial(bulk_kernel, steps, len(aliases)),
-        grid=(width // tile,),
+    tiles = cols // tile
+    column = pl.BlockSpec((rows, tile), lambda n: (0, n))
+    in_specs = [pl.BlockSpec(memory_space=pltpu.HBM)] * 4 + [column, pl.BlockSpec((BLOCK, tile), lambda n: (0, 0))]
+    in_specs += [pl.BlockSpec((BLOCK, tile), lambda n: (0, jnp.minimum(n, tiles // 2 - 1)))] * (steps - 1)
+    in_specs += [pl.BlockSpec((BLOCK, tile), lambda n: (0, jnp.maximum(n - tiles // 2, 0)))] * (steps - 1)
+    return pl.pallas_call(
+        functools.partial(bulk_kernel, steps),
+        grid=(tiles,),
         in_specs=in_specs,
         out_specs=[column, pl.BlockSpec((BLOCK, tile), lambda n: (0, n)), pl.BlockSpec((BLOCK, BLOCK), lambda n: (0, 0))],
         out_shape=[
             jax.ShapeDtypeStruct((rows, cols), jnp.bfloat16),
-            jax.ShapeDtypeStruct((BLOCK, width), jnp.float32),
+            jax.ShapeDtypeStruct((BLOCK, cols), jnp.float32),
             jax.ShapeDtypeStruct((BLOCK, BLOCK), jnp.bfloat16),
         ],
         scratch_shapes=[pltpu.VMEM((2, rows, rows), jnp.bfloat16), pltpu.SemaphoreType.DMA((2 * steps,))],
-        input_output_aliases=aliases,
         compiler_params=pltpu.CompilerParams(vmem_limit_bytes=50 << 20),
         cost_estimate=pl.CostEstimate(
-            flops=2 * rows * rows * width, bytes_accessed=3 * rows * width * 2, transcendentals=0),
-    )(*args)
+            flops=2 * rows * rows * cols, bytes_accessed=3 * rows * cols * 2, transcendentals=0),
+    )(*l_parts, b_own, early, *halves[0], *halves[1])
 
 
 def finish_kernel(step, start, row, tile, acc_start, l_ref, b_ref, acc_ref, x_in, x_ref, l_buf, b_buf, acc_buf, out_buf, sems):
@@ -191,31 +195,43 @@
     )(piece)
 
 
-def cut_many_kernel(places, b_ref, *refs):
+def cut_rest_kernel(places, b_ref, *refs):
     count = len(places)
-    out_refs, bufs, sems = refs[:count], refs[count:2 * count], refs[2 * count]
-    fetches = [
-        pltpu.make_async_copy(b_ref.at[pl.ds(row, BLOCK), pl.ds(start, width)], bufs[i], sems.at[0, i])
-        for i, (row, start, width) in enumerate(places)]
-    stores = [pltpu.make_async_copy(bufs[i], out_refs[i], sems.at[1, i]) for i in range(count)]
+    out_refs, (head, body, fetch_sems, store_sems) = refs[:count], refs[count:]
+    first_row, first_start, first_width = places[0]
+    fetches = [pltpu.make_async_copy(b_ref.at[pl.ds(first_row, BLOCK), pl.ds(first_start, first_width)], head, fetch_sems.at[0])]
+    stores = [pltpu.make_async_copy(head, out_refs[0], store_sems.at[0])]
+    if count > 1:
+        fetches.append(pltpu.make_async_copy(b_ref.at[pl.ds(BLOCK, body.shape[0])], body, fetch_sems.at[1]))
+        for i, (row, start, width) in list(enumerate(places))[1:]:
+            piece = body.at[pl.ds(row - BLOCK, BLOCK), pl.ds(start, width)]
+            stores.append(pltpu.make_async_copy(piece, out_refs[i], store_sems.at[i]))
     for fetch in fetches:
         fetch.start()
-    for fetch, store in zip(fetches, stores):
-        fetch.wait()
+    fetches[0].wait()
+    stores[0].start()
+    if count > 1:
+        fetches[1].wait()
+    for store in stores[1:]:
         store.start()
     for store in stores:
         store.wait()
 
 
-def cut_many(b, places):
+def cut_rest(b, places):
     size = sum(width for _, _, width in places) * BLOCK
-    return pl.pallas_call(
-        functools.partial(cut_many_kernel, places),
+    body = (b.shape[0] - BLOCK, b.shape[1]) if len(places) > 1 else (BLOCK, BLOCK)
+    return pl.pallas_call(
+        functools.partial(cut_rest_kernel, places),
         in_specs=[pl.BlockSpec(memory_space=pltpu.HBM)],
         out_specs=[pl.BlockSpec(memory_space=pltpu.HBM)] * len(places),
         out_shape=[jax.ShapeDtypeStruct((BLOCK, width), b.dtype) for _, _, width in places],
-        scratch_shapes=[pltpu.VMEM((BLOCK, width), b.dtype) for _, _, width in places]
-        + [pltpu.SemaphoreType.DMA((2, len(places)))],
+        scratch_shapes=[
+            pltpu.VMEM((BLOCK, places[0][2]), b.dtype),
+            pltpu.VMEM(body, b.dtype),
+            pltpu.SemaphoreType.DMA((2,)),
+            pltpu.SemaphoreType.DMA((len(places),)),
+        ],
         compiler_params=pltpu.CompilerParams(vmem_limit_bytes=48 << 20),
         cost_estimate=pl.CostEstimate(flops=2 * size, bytes_accessed=4 * size, transcendentals=0),
     )(b)
@@ -248,9 +264,9 @@
         places = [(j * BLOCK, off, w) for j, off, w in order]
         piece = cut(rhs_loc, *places[0])
         send(0, piece)
-        piece, = cut_many(rhs_loc, places[1:2])
+        piece, = cut_rest(rhs_loc, places[1:2])
         send(1, piece)
-        pieces = cut_many(rhs_loc, places[2:-1])
+        pieces = cut_rest(rhs_loc, places[2:-1])
         for i, piece in enumerate(pieces):
             send(2 + i, piece)
         got[final, cols - first] = keep(grid_rows - 1, got[final, cols - first])
@@ -258,16 +274,14 @@
             lax.ppermute(tri_loc, "col", [(c, c ^ d) for c in range(grid_cols)]) for d in (1, 2, 3))
         l_parts = [tri_loc, l_core, l_chip, l_both]
 
-        x, acc = None, [None, None]
-        for h in range(2):
-            x, acc[h], l_last = bulk(h * half, 512, l_parts, rhs_loc, [got[k, h * half] for k in range(final)], x)
+        halves = [[got[k, h * half] for k in range(final)] for h in range(2)]
+        x, acc, l_last = bulk(first, l_parts, rhs_loc, got[final, cols - first], halves)
         off, w = tail[-1]
-        acc_last = acc[1][:, off - half:off - half + w]
-        source, acc[1] = lax.optimization_barrier((rhs_loc, acc[1]))
+        acc_last = acc[:, off:off + w]
+        source, acc = lax.optimization_barrier((rhs_loc, acc))
         send(len(order) - 1, source[final * BLOCK:, off:off + w])
-        for off, w in [(cols - first, first), *tail[:-1]]:
-            h = off // half
-            x = finish(final, off, grid_rows - 1, l_last, got[final, off], acc[h], off - h * half, x)
+        for off, w in tail[:-1]:
+            x = finish(final, off, grid_rows - 1, l_last, got[final, off], acc, off, x)
         off, w = tail[-1]
         return finish_last(final, off, grid_rows - 1, l_last, got[final, off], acc_last, x)
 

time: 557 us -> 552 us (level); the launches traced: 557 us -> 544 us
  Pallas kernels: 78.9 us -> 73.2 us
    pallas_call x4 -> x3, Pallas kernels: 77.8 us -> 72 us  [the longest x1 56.5 us: bulk(): pl.pallas_call(functools.partial(bulk_kernel, steps), grid=(tiles,), in_s...]
  transfers between devices with their start and end apart: 18 -> 18, of which waited for: 14 -> 10; matrix products, arithmetic and copies ran while one was open for 0% -> 0% of each run, Pallas kernels for 12% -> 13%
where the time goes in v8:
time: 552 us; the launch traced here: 544 us
  waiting for transfers between devices  436 us (79%)
  Pallas kernels  73.2 us (13%)
  starting transfers between devices  28.6 us (5%)
  local copies, waits for them, and re-layouts  6.84 us (1%)
    ppermute x15, waiting for transfers between devices, send(): lax.ppermute(piece, 'row', down_row if i and j == final else swap_row)  436 us
    pallas_call x1, Pallas kernels, bulk(): pl.pallas_call(functools.partial(bulk_kernel, steps), grid=(tiles,), in_s...  56.5 us
    ppermute x15, starting transfers between devices, send(): lax.ppermute(piece, 'row', down_row if i and j == final else swap_row)  26.6 us
    pallas_call x2, Pallas kernels, cut_rest(): pl.pallas_call(functools.partial(cut_rest_kernel, places), in_specs=[pl.B...  15.5 us
  transfers between devices with their start and end apart: 18, of which 10 were waited for; matrix products, arithmetic and copies ran while one was open for 0% of the time, Pallas kernels for 13%

profile of v8, /device:TPU:0, one launch (start us, length us, event | category | flops | bytes accessed | tf_op | source)
XLA Modules:
  0.0 544.4 jit_solution(11216114297798463952)
XLA Ops:
  0.0 1.8 shard_map.30
  1.8 3.4 collective-permute-start.4
  5.1 13.8 %shard_map.31 = (bf16[256,4096]{1,0:T(8,128)(2,1)S(1)}, bf16[256,4096]{1,0:T(8,128)(2,1)S(1)}, bf16[256,4096]{1,0:T(8,128)(2,1)}, bf16[256,4096]{1,0:T(8,128)(2,...) custom-call(bf16[1536,8192]{1,0:T(8,128)(2,1)} %refs_4_.1), custom_call_target="tpu_custom_call" | custom-call | flops 22544384 | bytes 45088768 | tf_op jit(solution)/shard_map/pallas_call | solution.py:224
  19.0 2.0 collective-permute-start.6
  21.0 1.0 shard_map.28
  22.0 2.0 collective-permute-start.7
  24.0 123.1 %collective-permute-done.3.piece_ref = bf16[256,512]{1,0:T(8,128)(2,1)S(1)} collective-permute-done((bf16[256,512]{1,0:T(8,128)(2,1)S(1)}, bf16[256,512]{1,0:T(8,128)(2,1)S(1)}, u32[]{:S(2)}, u32[]{:S(2)}) %collective-permute-start.3) | collective-permute-done | bytes 262176 | tf_op jit(solution)/shard_map/ppermute | solution.py:262
  147.1 2.0 collective-permute-start.8
  149.2 2.0 collective-permute-start.10
  151.2 40.9 %collective-permute-done.7.refs_9_ = bf16[256,4096]{1,0:T(8,128)(2,1)S(1)} collective-permute-done((bf16[256,4096]{1,0:T(8,128)(2,1)}, bf16[256,4096]{1,0:T(8,128)(2,1)S(1)}, u32[]{:S(2)}, u32[]{:S(2)}) %collective-permute-start.7) | collective-permute-done | bytes 2097184 | tf_op jit(solution)/shard_map/ppermute | solution.py:262
  192.1 2.0 collective-permute-start.1
  194.0 42.9 %collective-permute-done.8.refs_10_ = bf16[256,4096]{1,0:T(8,128)(2,1)S(1)} collective-permute-done((bf16[256,4096]{1,0:T(8,128)(2,1)}, bf16[256,4096]{1,0:T(8,128)(2,1)S(1)}, u32[]{:S(2)}, u32[]{:S(2)}) %collective-permute-start.8) | collective-permute-done | bytes 2097184 | tf_op jit(solution)/shard_map/ppermute | solution.py:262
  237.0 44.9 %collective-permute-done.9.refs_11_ = bf16[256,4096]{1,0:T(8,128)(2,1)S(1)} collective-permute-done((bf16[256,4096]{1,0:T(8,128)(2,1)S(1)}, bf16[256,4096]{1,0:T(8,128)(2,1)S(1)}, u32[]{:S(2)}, u32[]{:S(2)}) %collective-permute-start.9) | collective-permute-done | bytes 2097184 | tf_op jit(solution)/shard_map/ppermute | solution.py:262
  281.9 44.9 %collective-permute-done.10.refs_12_ = bf16[256,4096]{1,0:T(8,128)(2,1)S(1)} collective-permute-done((bf16[256,4096]{1,0:T(8,128)(2,1)}, bf16[256,4096]{1,0:T(8,128)(2,1)S(1)}, u32[]{:S(2)}, u32[]{:S(2)}) %collective-permute-start.10) | collective-permute-done | bytes 2097184 | tf_op jit(solution)/shard_map/ppermute | solution.py:262
  326.9 2.0 collective-permute-start.12
  328.9 42.9 %collective-permute-done.11.refs_13_ = bf16[256,4096]{1,0:T(8,128)(2,1)S(1)} collective-permute-done((bf16[256,4096]{1,0:T(8,128)(2,1)}, bf16[256,4096]{1,0:T(8,128)(2,1)S(1)}, u32[]{:S(2)}, u32[]{:S(2)}) %collective-permute-start.11) | collective-permute-done | bytes 2097184 | tf_op jit(solution)/shard_map/ppermute | solution.py:262
  371.8 2.0 collective-permute-start.13
  373.9 42.9 %collective-permute-done.12.refs_14_ = bf16[256,4096]{1,0:T(8,128)(2,1)S(1)} collective-permute-done((bf16[256,4096]{1,0:T(8,128)(2,1)}, bf16[256,4096]{1,0:T(8,128)(2,1)S(1)}, u32[]{:S(2)}, u32[]{:S(2)}) %collective-permute-start.12) | collective-permute-done | bytes 2097184 | tf_op jit(solution)/shard_map/ppermute | solution.py:262
  416.8 3.9 collective-permute-start.15
  420.7 40.6 %collective-permute-done.13.refs_15_ = bf16[256,4096]{1,0:T(8,128)(2,1)S(1)} collective-permute-done((bf16[256,4096]{1,0:T(8,128)(2,1)}, bf16[256,4096]{1,0:T(8,128)(2,1)S(1)}, u32[]{:S(2)}, u32[]{:S(2)}) %collective-permute-start.13) | collective-permute-done | bytes 2097184 | tf_op jit(solution)/shard_map/ppermute | solution.py:262
  461.3 4.3 collective-permute-start.16
  465.7 1.4 collective-permute-start.17
  467.2 1.4 copy-done.3
  468.6 56.5 %shard_map.32 = (bf16[1536,8192]{1,0:T(8,128)(2,1)}, f32[256,8192]{1,0:T(8,128)}, bf16[256,256]{1,0:T(8,128)(2,1)S(1)}) custom-call(bf16[1536,768]{1,0:T(8,128)(2,1)} %refs_0_.1, bf16[1536,768]{1,0:T(8,128)(2,1)} %copy-done.3, bf16[1536,768]{1,0:T(8,128)(2,1)} %copy-done.2, bf16[1536,768]{1,0:T(8,128)(2,1)} %collective-permute-done.2.refs_3_, ...), custom_call_target="tpu_custom_call" | custom-call | flops 38654705664 | bytes 75497472 | tf_op jit(solution)/shard_map/pallas_call | solution.py:65
  525.1 1.0 slice.6
  526.1 1.3 collective-permute-start.14
  527.4 1.1 slice.7.acc_ref
  528.5 11.4 %collective-permute-done.17.b_ref = bf16[256,4096]{1,0:T(8,128)(2,1)S(1)} collective-permute-done((bf16[256,4096]{1,0:T(8,128)(2,1)S(1)}, bf16[256,4096]{1,0:T(8,128)(2,1)S(1)}, u32[]{:S(2)}, u32[]{:S(2)}) %collective-permute-start.17) | collective-permute-done | bytes 2097184 | tf_op jit(solution)/shard_map/ppermute | solution.py:262
  539.9 3.4 copy-done
  543.3 0.1 shard_map.34.x_in
  543.4 0.1 shard_map.35.x_in
  543.5 0.9 collective-permute-done.14.b_ref
  (39 shorter events, 0.2 us)
Async XLA Ops:
  1.8 147.4 %collective-permute-start.4 = (bf16[256,4096]{1,0:T(8,128)(2,1)S(1)}, bf16[256,4096]{1,0:T(8,128)(2,1)S(1)}, u32[]{:S(2)}, u32[]{:S(2)}) collective-permute-start(bf16[256,4096]{1,0:T(8,128)(2,1)S(1)} %shard_map.30), channel_id=1, source_target_pairs={{0,4},{4,0},{1,5},{5,1},{2,6},{6,2},{3,7},{7,3}} | collective-permute-start | bytes 6291464 | tf_op jit(solution)/shard_map/ppermute | solution.py:262
  18.9 130.2 %collective-permute-start.5 = (bf16[256,4096]{1,0:T(8,128)(2,1)S(1)}, bf16[256,4096]{1,0:T(8,128)(2,1)}, u32[]{:S(2)}, u32[]{:S(2)}) collective-permute-start(bf16[256,4096]{1,0:T(8,128)(2,1)S(1)} %get-tuple-element.22), channel_id=1, source_target_pairs={{0,4},{4,0},{1,5},{5,1},{2,6},{6,2},{3,7},{7,3}} | collective-permute-start | bytes 6291464 | tf_op jit(solution)/shard_map/ppermute | solution.py:262
  19.0 173.1 %copy-start.1 = (bf16[1536,768]{1,0:T(8,128)(2,1)S(1)}, bf16[1536,768]{1,0:T(8,128)(2,1)}, u32[]{:S(2)}) copy-start(bf16[1536,768]{1,0:T(8,128)(2,1)} %refs_0_.1) | copy-start | bytes 7077892
  19.0 446.8 %copy-start.4 = (bf16[256,4096]{1,0:T(8,128)(2,1)S(1)}, bf16[256,4096]{1,0:T(8,128)(2,1)}, u32[]{:S(2)}) copy-start(bf16[256,4096]{1,0:T(8,128)(2,1)} %get-tuple-element.37) | copy-start | bytes 6291460
  19.0 132.2 %collective-permute-start.6 = (bf16[256,4096]{1,0:T(8,128)(2,1)}, bf16[256,4096]{1,0:T(8,128)(2,1)}, u32[]{:S(2)}, u32[]{:S(2)}) collective-permute-start(bf16[256,4096]{1,0:T(8,128)(2,1)} %get-tuple-element.23), channel_id=1, source_target_pairs={{0,4},{4,0},{1,5},{5,1},{2,6},{6,2},{3,7},{7,3}} | collective-permute-start | bytes 6291464 | tf_op jit(solution)/shard_map/ppermute | solution.py:262
  21.9 125.2 %collective-permute-start.3 = (bf16[256,512]{1,0:T(8,128)(2,1)S(1)}, bf16[256,512]{1,0:T(8,128)(2,1)S(1)}, u32[]{:S(2)}, u32[]{:S(2)}) collective-permute-start(bf16[256,512]{1,0:T(8,128)(2,1)S(1)} %shard_map.28), channel_id=1, source_target_pairs={{0,4},{4,0},{1,5},{5,1},{2,6},{6,2},{3,7},{7,3}} | collective-permute-start | bytes 786440 | tf_op jit(solution)/shard_map/ppermute | solution.py:262
  22.0 170.1 %collective-permute-start.7 = (bf16[256,4096]{1,0:T(8,128)(2,1)}, bf16[256,4096]{1,0:T(8,128)(2,1)S(1)}, u32[]{:S(2)}, u32[]{:S(2)}) collective-permute-start(bf16[256,4096]{1,0:T(8,128)(2,1)} %get-tuple-element.24), channel_id=1, source_target_pairs={{0,4},{4,0},{1,5},{5,1},{2,6},{6,2},{3,7},{7,3}} | collective-permute-start | bytes 6291464 | tf_op jit(solution)/shard_map/ppermute | solution.py:262
  147.1 89.9 %collective-permute-start.8 = (bf16[256,4096]{1,0:T(8,128)(2,1)}, bf16[256,4096]{1,0:T(8,128)(2,1)S(1)}, u32[]{:S(2)}, u32[]{:S(2)}) collective-permute-start(bf16[256,4096]{1,0:T(8,128)(2,1)} %get-tuple-element.25), channel_id=1, source_target_pairs={{0,4},{4,0},{1,5},{5,1},{2,6},{6,2},{3,7},{7,3}} | collective-permute-start | bytes 6291464 | tf_op jit(solution)/shard_map/ppermute | solution.py:262
  149.1 132.8 %collective-permute-start.9 = (bf16[256,4096]{1,0:T(8,128)(2,1)S(1)}, bf16[256,4096]{1,0:T(8,128)(2,1)S(1)}, u32[]{:S(2)}, u32[]{:S(2)}) collective-permute-start(bf16[256,4096]{1,0:T(8,128)(2,1)S(1)} %get-tuple-element.26), channel_id=1, source_target_pairs={{0,4},{4,0},{1,5},{5,1},{2,6},{6,2},{3,7},{7,3}} | collective-permute-start | bytes 6291464 | tf_op jit(solution)/shard_map/ppermute | solution.py:262
  149.2 177.7 %collective-permute-start.10 = (bf16[256,4096]{1,0:T(8,128)(2,1)}, bf16[256,4096]{1,0:T(8,128)(2,1)S(1)}, u32[]{:S(2)}, u32[]{:S(2)}) collective-permute-start(bf16[256,4096]{1,0:T(8,128)(2,1)} %get-tuple-element.27), channel_id=1, source_target_pairs={{0,4},{4,0},{1,5},{5,1},{2,6},{6,2},{3,7},{7,3}} | collective-permute-start | bytes 6291464 | tf_op jit(solution)/shard_map/ppermute | solution.py:262
  151.2 220.6 %collective-permute-start.11 = (bf16[256,4096]{1,0:T(8,128)(2,1)}, bf16[256,4096]{1,0:T(8,128)(2,1)S(1)}, u32[]{:S(2)}, u32[]{:S(2)}) collective-permute-start(bf16[256,4096]{1,0:T(8,128)(2,1)} %get-tuple-element.28), channel_id=1, source_target_pairs={{0,4},{4,0},{1,5},{5,1},{2,6},{6,2},{3,7},{7,3}} | collective-permute-start | bytes 6291464 | tf_op jit(solution)/shard_map/ppermute | solution.py:262
  192.0 2.0 copy-start.5
  192.1 273.6 %collective-permute-start.1 = (bf16[1536,768]{1,0:T(8,128)(2,1)S(1)}, bf16[1536,768]{1,0:T(8,128)(2,1)S(1)}, u32[]{:S(2)}, u32[]{:S(2)}) collective-permute-start(bf16[1536,768]{1,0:T(8,128)(2,1)S(1)} %copy-done.1), channel_id=1, source_target_pairs={{0,2},{1,3},{2,0},{3,1},{4,6},{5,7},{6,4},{7,5}} | collective-permute-start | bytes 7077896 | tf_op jit(solution)/shard_map/ppermute | solution.py:274
  237.0 228.7 %copy-start.6 = (bf16[256,4096]{1,0:T(8,128)(2,1)}, bf16[256,4096]{1,0:T(8,128)(2,1)S(1)}, u32[]{:S(2)}) copy-start(bf16[256,4096]{1,0:T(8,128)(2,1)S(1)} %collective-permute-done.8.refs_10_) | copy-start | bytes 6291460
  237.0 230.2 %collective-permute-start = (bf16[1536,768]{1,0:T(8,128)(2,1)S(1)}, bf16[1536,768]{1,0:T(8,128)(2,1)S(1)}, u32[]{:S(2)}, u32[]{:S(2)}) collective-permute-start(bf16[1536,768]{1,0:T(8,128)(2,1)S(1)} %copy-done.1), channel_id=1, source_target_pairs={{0,1},{1,0},{2,3},{3,2},{4,5},{5,4},{6,7},{7,6}} | collective-permute-start | bytes 7077896 | tf_op jit(solution)/shard_map/ppermute | solution.py:274
  281.9 185.2 %copy-start.7 = (bf16[256,4096]{1,0:T(8,128)(2,1)}, bf16[256,4096]{1,0:T(8,128)(2,1)S(1)}, u32[]{:S(2)}) copy-start(bf16[256,4096]{1,0:T(8,128)(2,1)S(1)} %collective-permute-done.9.refs_11_) | copy-start | bytes 6291460
  281.9 186.7 %collective-permute-start.2 = (bf16[1536,768]{1,0:T(8,128)(2,1)S(1)}, bf16[1536,768]{1,0:T(8,128)(2,1)}, u32[]{:S(2)}, u32[]{:S(2)}) collective-permute-start(bf16[1536,768]{1,0:T(8,128)(2,1)S(1)} %copy-done.1), channel_id=1, source_target_pairs={{0,3},{1,2},{2,1},{3,0},{4,7},{5,6},{6,5},{7,4}} | collective-permute-start | bytes 7077896 | tf_op jit(solution)/shard_map/ppermute | solution.py:274
  326.9 140.3 %copy-start.8 = (bf16[256,4096]{1,0:T(8,128)(2,1)}, bf16[256,4096]{1,0:T(8,128)(2,1)S(1)}, u32[]{:S(2)}) copy-start(bf16[256,4096]{1,0:T(8,128)(2,1)S(1)} %collective-permute-done.10.refs_12_) | copy-start | bytes 6291460
  326.9 89.9 %collective-permute-start.12 = (bf16[256,4096]{1,0:T(8,128)(2,1)}, bf16[256,4096]{1,0:T(8,128)(2,1)S(1)}, u32[]{:S(2)}, u32[]{:S(2)}) collective-permute-start(bf16[256,4096]{1,0:T(8,128)(2,1)} %get-tuple-element.29), channel_id=1, source_target_pairs={{0,4},{4,0},{1,5},{5,1},{2,6},{6,2},{3,7},{7,3}} | collective-permute-start | bytes 6291464 | tf_op jit(solution)/shard_map/ppermute | solution.py:262
  371.8 95.4 %copy-start.9 = (bf16[256,4096]{1,0:T(8,128)(2,1)}, bf16[256,4096]{1,0:T(8,128)(2,1)S(1)}, u32[]{:S(2)}) copy-start(bf16[256,4096]{1,0:T(8,128)(2,1)S(1)} %collective-permute-done.11.refs_13_) | copy-start | bytes 6291460
  371.8 89.5 %collective-permute-start.13 = (bf16[256,4096]{1,0:T(8,128)(2,1)}, bf16[256,4096]{1,0:T(8,128)(2,1)S(1)}, u32[]{:S(2)}, u32[]{:S(2)}) collective-permute-start(bf16[256,4096]{1,0:T(8,128)(2,1)} %get-tuple-element.30), channel_id=1, source_target_pairs={{0,4},{4,0},{1,5},{5,1},{2,6},{6,2},{3,7},{7,3}} | collective-permute-start | bytes 6291464 | tf_op jit(solution)/shard_map/ppermute | solution.py:262
  416.8 50.4 %copy-start.10 = (bf16[256,4096]{1,0:T(8,128)(2,1)}, bf16[256,4096]{1,0:T(8,128)(2,1)S(1)}, u32[]{:S(2)}) copy-start(bf16[256,4096]{1,0:T(8,128)(2,1)S(1)} %collective-permute-done.12.refs_14_) | copy-start | bytes 6291460
  416.8 126.6 %collective-permute-start.15 = (bf16[256,1024]{1,0:T(8,128)(2,1)S(1)}, bf16[256,1024]{1,0:T(8,128)(2,1)S(1)}, u32[]{:S(2)}, u32[]{:S(2)}) collective-permute-start(bf16[256,1024]{1,0:T(8,128)(2,1)S(1)} %get-tuple-element.34), channel_id=1, source_target_pairs={{0,4},{1,5},{2,6},{3,7}} | collective-permute-start | bytes 1572872 | tf_op jit(solution)/shard_map/ppermute | solution.py:262
  461.3 5.9 %copy-start.11 = (bf16[256,4096]{1,0:T(8,128)(2,1)}, bf16[256,4096]{1,0:T(8,128)(2,1)S(1)}, u32[]{:S(2)}) copy-start(bf16[256,4096]{1,0:T(8,128)(2,1)S(1)} %collective-permute-done.13.refs_15_) | copy-start | bytes 6291460
  461.3 82.0 %collective-permute-start.16 = (bf16[256,2048]{1,0:T(8,128)(2,1)S(1)}, bf16[256,2048]{1,0:T(8,128)(2,1)S(1)}, u32[]{:S(2)}, u32[]{:S(2)}) collective-permute-start(bf16[256,2048]{1,0:T(8,128)(2,1)S(1)} %get-tuple-element.36), channel_id=1, source_target_pairs={{0,4},{1,5},{2,6},{3,7}} | collective-permute-start | bytes 3145736 | tf_op jit(solution)/shard_map/ppermute | solution.py:262
  465.7 2.9 copy-start.2
  465.7 74.2 %collective-permute-start.17 = (bf16[256,4096]{1,0:T(8,128)(2,1)S(1)}, bf16[256,4096]{1,0:T(8,128)(2,1)S(1)}, u32[]{:S(2)}, u32[]{:S(2)}) collective-permute-start(bf16[256,4096]{1,0:T(8,128)(2,1)S(1)} %copy-done.4), channel_id=1, source_target_pairs={{0,4},{1,5},{2,6},{3,7}} | collective-permute-start | bytes 6291464 | tf_op jit(solution)/shard_map/ppermute | solution.py:262
  467.2 1.4 copy-start.3
  526.1 18.3 %collective-permute-start.14 = (bf16[256,512]{1,0:T(8,128)(2,1)S(1)}, bf16[256,512]{1,0:T(8,128)(2,1)S(1)}, u32[]{:S(2)}, u32[]{:S(2)}) collective-permute-start(bf16[256,512]{1,0:T(8,128)(2,1)S(1)} %slice.6), channel_id=1, source_target_pairs={{0,4},{1,5},{2,6},{3,7}} | collective-permute-start | bytes 786440 | tf_op jit(solution)/shard_map/ppermute | solution.py:262
  539.9 3.4 copy-start

commit v9 on v7

--- a/solution.py
+++ b/solution.py
@@ -116,7 +116,7 @@
 def finish(step, start, row, l_last, piece, acc, acc_start, x):
     width = piece.shape[1]
     return pl.pallas_call(
-        functools.partial(finish_kernel, step, start, row, min(width, 512), acc_start),
+        functools.partial(finish_kernel, step, start, row, 512 if width % 512 == 0 else 256, acc_start),
         in_specs=[pl.BlockSpec(memory_space=pltpu.HBM)] * 4,
         out_specs=pl.BlockSpec(memory_space=pltpu.HBM),
         out_shape=jax.ShapeDtypeStruct(x.shape, x.dtype),
@@ -202,31 +202,43 @@
     )(piece)
 
 
-def cut_many_kernel(places, b_ref, *refs):
+def cut_rest_kernel(places, b_ref, *refs):
     count = len(places)
-    out_refs, bufs, sems = refs[:count], refs[count:2 * count], refs[2 * count]
-    fetches = [
-        pltpu.make_async_copy(b_ref.at[pl.ds(row, BLOCK), pl.ds(start, width)], bufs[i], sems.at[0, i])
-        for i, (row, start, width) in enumerate(places)]
-    stores = [pltpu.make_async_copy(bufs[i], out_refs[i], sems.at[1, i]) for i in range(count)]
+    out_refs, (head, body, fetch_sems, store_sems) = refs[:count], refs[count:]
+    first_row, first_start, first_width = places[0]
+    fetches = [pltpu.make_async_copy(b_ref.at[pl.ds(first_row, BLOCK), pl.ds(first_start, first_width)], head, fetch_sems.at[0])]
+    stores = [pltpu.make_async_copy(head, out_refs[0], store_sems.at[0])]
+    if count > 1:
+        fetches.append(pltpu.make_async_copy(b_ref.at[pl.ds(BLOCK, body.shape[0])], body, fetch_sems.at[1]))
+        for i, (row, start, width) in list(enumerate(places))[1:]:
+            piece = body.at[pl.ds(row - BLOCK, BLOCK), pl.ds(start, width)]
+            stores.append(pltpu.make_async_copy(piece, out_refs[i], store_sems.at[i]))
     for fetch in fetches:
         fetch.start()
-    for fetch, store in zip(fetches, stores):
-        fetch.wait()
+    fetches[0].wait()
+    stores[0].start()
+    if count > 1:
+        fetches[1].wait()
+    for store in stores[1:]:
         store.start()
     for store in stores:
         store.wait()
 
 
-def cut_many(b, places):
+def cut_rest(b, places):
     size = sum(width for _, _, width in places) * BLOCK
-    return pl.pallas_call(
-        functools.partial(cut_many_kernel, places),
+    body = (b.shape[0] - BLOCK, b.shape[1]) if len(places) > 1 else (BLOCK, BLOCK)
+    return pl.pallas_call(
+        functools.partial(cut_rest_kernel, places),
         in_specs=[pl.BlockSpec(memory_space=pltpu.HBM)],
         out_specs=[pl.BlockSpec(memory_space=pltpu.HBM)] * len(places),
         out_shape=[jax.ShapeDtypeStruct((BLOCK, width), b.dtype) for _, _, width in places],
-        scratch_shapes=[pltpu.VMEM((BLOCK, width), b.dtype) for _, _, width in places]
-        + [pltpu.SemaphoreType.DMA((2, len(places)))],
+        scratch_shapes=[
+            pltpu.VMEM((BLOCK, places[0][2]), b.dtype),
+            pltpu.VMEM(body, b.dtype),
+            pltpu.SemaphoreType.DMA((2,)),
+            pltpu.SemaphoreType.DMA((len(places),)),
+        ],
         compiler_params=pltpu.CompilerParams(vmem_limit_bytes=48 << 20),
         cost_estimate=pl.CostEstimate(flops=2 * size, bytes_accessed=4 * size, transcendentals=0),
     )(b)
@@ -247,7 +259,10 @@
 
         order = [(final, cols - first, first)]
         order += [(j, h * half, half) for j in range(final) for h in range(2)]
-        tail = [(0, half), (half, cols // 4), (half + cols // 4, cols // 8), (cols - 2 * first, first)]
+        tail, off = [], 0
+        for w in (half, cols // 4, 3 * first // 2, first, first // 2):
+            tail.append((off, w))
+            off += w
         order += [(final, off, w) for off, w in tail]
 
         got = {}
@@ -259,9 +274,9 @@
         places = [(j * BLOCK, off, w) for j, off, w in order]
         piece = cut(rhs_loc, *places[0])
         send(0, piece)
-        piece, = cut_many(rhs_loc, places[1:2])
+        piece, = cut_rest(rhs_loc, places[1:2])
         send(1, piece)
-        pieces = cut_many(rhs_loc, places[2:-1])
+        pieces = cut_rest(rhs_loc, places[2:-1])
         for i, piece in enumerate(pieces):
             send(2 + i, piece)
         got[final, cols - first] = keep(grid_rows - 1, got[final, cols - first])

time: 551 us -> 554 us (level)
    ppermute x15 -> x16, waiting for transfers between devices: 431 us -> 427 us  [send(): lax.ppermute(piece, 'row', down_row if i and j == final else swap_row)]
    ppermute x15 -> x16, starting transfers between devices: 26.7 us -> 30.1 us  [send(): lax.ppermute(piece, 'row', down_row if i and j == final else swap_row)]
    pallas_call x5 -> x6, Pallas kernels: 15.4 us -> 15.7 us  [the longest x2 15.6 us: cut_rest(): pl.pallas_call(functools.partial(cut_rest_kernel, places), in_specs=[pl.B...]
  transfers between devices with their start and end apart: 18 -> 19, of which waited for: 10 -> 10; matrix products, arithmetic and copies ran while one was open for 0% -> 0% of each run, Pallas kernels for 14% -> 14%
where the time goes in v9:
time: 554 us; the launch traced here: 550 us
  waiting for transfers between devices  433 us (78%)
  Pallas kernels  79.3 us (14%)
  starting transfers between devices  31.8 us (6%)
  local copies, waits for them, and re-layouts  6.26 us (1%)
    ppermute x16, waiting for transfers between devices, send(): lax.ppermute(piece, 'row', down_row if i and j == final else swap_row)  427 us
    pallas_call x2, Pallas kernels, bulk(): pl.pallas_call(functools.partial(bulk_kernel, steps, len(aliases), int(ea...  62.4 us
    ppermute x16, starting transfers between devices, send(): lax.ppermute(piece, 'row', down_row if i and j == final else swap_row)  30.1 us
    pallas_call x2, Pallas kernels, cut_rest(): pl.pallas_call(functools.partial(cut_rest_kernel, places), in_specs=[pl.B...  15.6 us
  transfers between devices with their start and end apart: 19, of which 10 were waited for; matrix products, arithmetic and copies ran while one was open for 0% of the time, Pallas kernels for 14%

profile of v9, /device:TPU:0, one launch (start us, length us, event | category | flops | bytes accessed | tf_op | source)
XLA Modules:
  0.0 550.4 jit_solution(17339760022148566430)
XLA Ops:
  0.0 1.8 shard_map.31
  1.8 3.4 collective-permute-start.9
  5.1 13.8 %shard_map.28 = (bf16[256,4096]{1,0:T(8,128)(2,1)S(1)}, bf16[256,4096]{1,0:T(8,128)(2,1)S(1)}, bf16[256,4096]{1,0:T(8,128)(2,1)}, bf16[256,4096]{1,0:T(8,128)(2,...) custom-call(bf16[1536,8192]{1,0:T(8,128)(2,1)} %refs_4_.3), custom_call_target="tpu_custom_call" | custom-call | flops 22675456 | bytes 45350912 | tf_op jit(solution)/shard_map/pallas_call | solution.py:231
  19.0 2.0 collective-permute-start.10
  21.0 1.1 shard_map.29
  23.1 168.1 %collective-permute-done.8.piece_ref = bf16[256,512]{1,0:T(8,128)(2,1)S(1)} collective-permute-done((bf16[256,512]{1,0:T(8,128)(2,1)S(1)}, bf16[256,512]{1,0:T(8,128)(2,1)S(1)}, u32[]{:S(2)}, u32[]{:S(2)}) %collective-permute-start.8) | collective-permute-done | bytes 262176 | tf_op jit(solution)/shard_map/ppermute | solution.py:272
  191.5 1.3 copy-done.2
  192.8 1.4 collective-permute-start.1
  194.2 1.5 collective-permute-start.12
  196.3 46.7 %collective-permute-done.12.refs_8_ = bf16[256,4096]{1,0:T(8,128)(2,1)S(1)} collective-permute-done((bf16[256,4096]{1,0:T(8,128)(2,1)}, bf16[256,4096]{1,0:T(8,128)(2,1)S(1)}, u32[]{:S(2)}, u32[]{:S(2)}) %collective-permute-start.12) | collective-permute-done | bytes 2097184 | tf_op jit(solution)/shard_map/ppermute | solution.py:272
  243.0 1.5 collective-permute-start.4
  244.5 43.4 %collective-permute-done.13.refs_9_ = bf16[256,4096]{1,0:T(8,128)(2,1)S(1)} collective-permute-done((bf16[256,4096]{1,0:T(8,128)(2,1)}, bf16[256,4096]{1,0:T(8,128)(2,1)S(1)}, u32[]{:S(2)}, u32[]{:S(2)}) %collective-permute-start.13) | collective-permute-done | bytes 2097184 | tf_op jit(solution)/shard_map/ppermute | solution.py:272
  287.9 1.5 collective-permute-start.5
  289.9 5.4 collective-permute-done.1.refs_2_
  295.3 1.7 collective-permute-start.7
  297.1 1.4 copy-done.7
  298.5 2.5 collective-permute-start.18
  301.1 1.6 copy-done.3
  302.7 31.0 %shard_map.32 = (bf16[1536,8192]{1,0:T(8,128)(2,1)}, f32[256,4096]{1,0:T(8,128)}, bf16[256,256]{1,0:T(8,128)(2,1)}) custom-call(bf16[1536,768]{1,0:T(8,128)(2,1)} %refs_0_.3, bf16[1536,768]{1,0:T(8,128)(2,1)} %copy-done.7, bf16[1536,768]{1,0:T(8,128)(2,1)} %copy-done.6, bf16[1536,768]{1,0:T(8,128)(2,1)} %copy-done.5, bf16[1536,8192]{1,0:T(8,128)(2,1)} %refs_4_.3, ...), custom_call_target="tpu_custom_call" | custom-call | flops 19327352832 | bytes 37748736 | tf_op jit(solution)/shard_map/pallas_call | solution.py:71
  333.8 2.5 collective-permute-start.15
  336.3 41.6 %collective-permute-done.5.refs_7_ = bf16[256,4096]{1,0:T(8,128)(2,1)} collective-permute-done((bf16[256,4096]{1,0:T(8,128)(2,1)}, bf16[256,4096]{1,0:T(8,128)(2,1)}, u32[]{:S(2)}, u32[]{:S(2)}) %collective-permute-start.5) | collective-permute-done | bytes 2097184 | tf_op jit(solution)/shard_map/ppermute | solution.py:272
  377.9 3.4 collective-permute-start.16
  381.3 41.5 %collective-permute-done.6.refs_8_ = bf16[256,4096]{1,0:T(8,128)(2,1)} collective-permute-done((bf16[256,4096]{1,0:T(8,128)(2,1)}, bf16[256,4096]{1,0:T(8,128)(2,1)}, u32[]{:S(2)}, u32[]{:S(2)}) %collective-permute-start.6) | collective-permute-done | bytes 2097184 | tf_op jit(solution)/shard_map/ppermute | solution.py:272
  422.8 3.5 collective-permute-start.17
  426.3 40.6 %collective-permute-done.7.refs_9_ = bf16[256,4096]{1,0:T(8,128)(2,1)} collective-permute-done((bf16[256,4096]{1,0:T(8,128)(2,1)}, bf16[256,4096]{1,0:T(8,128)(2,1)}, u32[]{:S(2)}, u32[]{:S(2)}) %collective-permute-start.7) | collective-permute-done | bytes 2097184 | tf_op jit(solution)/shard_map/ppermute | solution.py:272
  467.0 31.4 %shard_map.33 = (bf16[1536,8192]{1,0:T(8,128)(2,1)}, f32[256,4096]{1,0:T(8,128)}, bf16[256,256]{1,0:T(8,128)(2,1)S(1)}) custom-call(bf16[1536,768]{1,0:T(8,128)(2,1)} %refs_0_.3, bf16[1536,768]{1,0:T(8,128)(2,1)} %copy-done.7, bf16[1536,768]{1,0:T(8,128)(2,1)} %copy-done.6, bf16[1536,768]{1,0:T(8,128)(2,1)} %copy-done.5, ...), custom_call_target="tpu_custom_call", output_to_operand_aliasing={{0}: (11, {})} | custom-call | flops 19327352832 | bytes 37748736 | tf_op jit(solution)/shard_map/pallas_call | solution.py:71
  498.3 0.9 slice.6
  499.3 4.5 collective-permute-start.14
  503.7 1.0 slice.7.acc_ref
  504.7 7.0 %collective-permute-done.18.b_ref = bf16[256,4096]{1,0:T(8,128)(2,1)S(1)} collective-permute-done((bf16[256,4096]{1,0:T(8,128)(2,1)}, bf16[256,4096]{1,0:T(8,128)(2,1)S(1)}, u32[]{:S(2)}, u32[]{:S(2)}) %collective-permute-start.18) | collective-permute-done | bytes 2097184 | tf_op jit(solution)/shard_map/ppermute | solution.py:272
  511.8 36.4 %collective-permute-done.17.b_ref = bf16[256,2048]{1,0:T(8,128)(2,1)S(1)} collective-permute-done((bf16[256,2048]{1,0:T(8,128)(2,1)S(1)}, bf16[256,2048]{1,0:T(8,128)(2,1)S(1)}, u32[]{:S(2)}, u32[]{:S(2)}) %collective-permute-start.17) | collective-permute-done | bytes 1048608 | tf_op jit(solution)/shard_map/ppermute | solution.py:272
  548.4 2.0 collective-permute-done.14.b_ref
  (41 shorter events, 2.6 us)
Async XLA Ops:
  1.8 189.7 %collective-permute-start.9 = (bf16[256,4096]{1,0:T(8,128)(2,1)S(1)}, bf16[256,4096]{1,0:T(8,128)(2,1)S(1)}, u32[]{:S(2)}, u32[]{:S(2)}) collective-permute-start(bf16[256,4096]{1,0:T(8,128)(2,1)S(1)} %shard_map.31), channel_id=1, source_target_pairs={{0,4},{4,0},{1,5},{5,1},{2,6},{6,2},{3,7},{7,3}} | collective-permute-start | bytes 6291464 | tf_op jit(solution)/shard_map/ppermute | solution.py:272
  18.9 175.3 %collective-permute-start.3 = (bf16[256,4096]{1,0:T(8,128)(2,1)S(1)}, bf16[256,4096]{1,0:T(8,128)(2,1)S(1)}, u32[]{:S(2)}, u32[]{:S(2)}) collective-permute-start(bf16[256,4096]{1,0:T(8,128)(2,1)S(1)} %get-tuple-element.25), channel_id=1, source_target_pairs={{0,4},{4,0},{1,5},{5,1},{2,6},{6,2},{3,7},{7,3}} | collective-permute-start | bytes 6291464 | tf_op jit(solution)/shard_map/ppermute | solution.py:272
  19.0 176.8 %collective-permute-start.10 = (bf16[256,4096]{1,0:T(8,128)(2,1)S(1)}, bf16[256,4096]{1,0:T(8,128)(2,1)}, u32[]{:S(2)}, u32[]{:S(2)}) collective-permute-start(bf16[256,4096]{1,0:T(8,128)(2,1)S(1)} %get-tuple-element.30), channel_id=1, source_target_pairs={{0,4},{4,0},{1,5},{5,1},{2,6},{6,2},{3,7},{7,3}} | collective-permute-start | bytes 6291464 | tf_op jit(solution)/shard_map/ppermute | solution.py:272
  21.0 170.2 %copy-start.4 = (bf16[1536,768]{1,0:T(8,128)(2,1)S(1)}, bf16[1536,768]{1,0:T(8,128)(2,1)}, u32[]{:S(2)}) copy-start(bf16[1536,768]{1,0:T(8,128)(2,1)} %refs_0_.3) | copy-start | bytes 7077892
  21.0 175.3 %collective-permute-start.11 = (bf16[256,4096]{1,0:T(8,128)(2,1)}, bf16[256,4096]{1,0:T(8,128)(2,1)}, u32[]{:S(2)}, u32[]{:S(2)}) collective-permute-start(bf16[256,4096]{1,0:T(8,128)(2,1)} %get-tuple-element.31), channel_id=1, source_target_pairs={{0,4},{4,0},{1,5},{5,1},{2,6},{6,2},{3,7},{7,3}} | collective-permute-start | bytes 6291464 | tf_op jit(solution)/shard_map/ppermute | solution.py:272
  22.1 169.1 %collective-permute-start.8 = (bf16[256,512]{1,0:T(8,128)(2,1)S(1)}, bf16[256,512]{1,0:T(8,128)(2,1)S(1)}, u32[]{:S(2)}, u32[]{:S(2)}) collective-permute-start(bf16[256,512]{1,0:T(8,128)(2,1)S(1)} %shard_map.29), channel_id=1, source_target_pairs={{0,4},{4,0},{1,5},{5,1},{2,6},{6,2},{3,7},{7,3}} | collective-permute-start | bytes 786440 | tf_op jit(solution)/shard_map/ppermute | solution.py:272
  191.2 98.2 %collective-permute-start.2 = (bf16[1536,768]{1,0:T(8,128)(2,1)S(1)}, bf16[1536,768]{1,0:T(8,128)(2,1)S(1)}, u32[]{:S(2)}, u32[]{:S(2)}) collective-permute-start(bf16[1536,768]{1,0:T(8,128)(2,1)S(1)} %copy-done.4), channel_id=1, source_target_pairs={{0,3},{1,2},{2,1},{3,0},{4,7},{5,6},{6,5},{7,4}} | collective-permute-start | bytes 7077896 | tf_op jit(solution)/shard_map/ppermute | solution.py:284
  191.5 1.3 copy-start.2
  192.8 102.5 %collective-permute-start.1 = (bf16[1536,768]{1,0:T(8,128)(2,1)S(1)}, bf16[1536,768]{1,0:T(8,128)(2,1)S(1)}, u32[]{:S(2)}, u32[]{:S(2)}) collective-permute-start(bf16[1536,768]{1,0:T(8,128)(2,1)S(1)} %copy-done.4), channel_id=1, source_target_pairs={{0,2},{1,3},{2,0},{3,1},{4,6},{5,7},{6,4},{7,5}} | collective-permute-start | bytes 7077896 | tf_op jit(solution)/shard_map/ppermute | solution.py:284
  194.2 48.7 %collective-permute-start.12 = (bf16[256,4096]{1,0:T(8,128)(2,1)}, bf16[256,4096]{1,0:T(8,128)(2,1)S(1)}, u32[]{:S(2)}, u32[]{:S(2)}) collective-permute-start(bf16[256,4096]{1,0:T(8,128)(2,1)} %get-tuple-element.32), channel_id=1, source_target_pairs={{0,4},{4,0},{1,5},{5,1},{2,6},{6,2},{3,7},{7,3}} | collective-permute-start | bytes 6291464 | tf_op jit(solution)/shard_map/ppermute | solution.py:272
  195.8 92.1 %collective-permute-start.13 = (bf16[256,4096]{1,0:T(8,128)(2,1)}, bf16[256,4096]{1,0:T(8,128)(2,1)S(1)}, u32[]{:S(2)}, u32[]{:S(2)}) collective-permute-start(bf16[256,4096]{1,0:T(8,128)(2,1)} %get-tuple-element.33), channel_id=1, source_target_pairs={{0,4},{4,0},{1,5},{5,1},{2,6},{6,2},{3,7},{7,3}} | collective-permute-start | bytes 6291464 | tf_op jit(solution)/shard_map/ppermute | solution.py:272
  196.3 100.8 %collective-permute-start = (bf16[1536,768]{1,0:T(8,128)(2,1)S(1)}, bf16[1536,768]{1,0:T(8,128)(2,1)S(1)}, u32[]{:S(2)}, u32[]{:S(2)}) collective-permute-start(bf16[1536,768]{1,0:T(8,128)(2,1)S(1)} %copy-done.4), channel_id=1, source_target_pairs={{0,1},{1,0},{2,3},{3,2},{4,5},{5,4},{6,7},{7,6}} | collective-permute-start | bytes 7077896 | tf_op jit(solution)/shard_map/ppermute | solution.py:284
  243.0 55.6 %copy-start.9 = (bf16[256,4096]{1,0:T(8,128)(2,1)}, bf16[256,4096]{1,0:T(8,128)(2,1)S(1)}, u32[]{:S(2)}) copy-start(bf16[256,4096]{1,0:T(8,128)(2,1)S(1)} %collective-permute-done.12.refs_8_) | copy-start | bytes 6291460
  243.0 90.8 %collective-permute-start.4 = (bf16[256,4096]{1,0:T(8,128)(2,1)}, bf16[256,4096]{1,0:T(8,128)(2,1)S(1)}, u32[]{:S(2)}, u32[]{:S(2)}) collective-permute-start(bf16[256,4096]{1,0:T(8,128)(2,1)} %get-tuple-element.26), channel_id=1, source_target_pairs={{0,4},{4,0},{1,5},{5,1},{2,6},{6,2},{3,7},{7,3}} | collective-permute-start | bytes 6291464 | tf_op jit(solution)/shard_map/ppermute | solution.py:272
  287.9 7.4 %copy-start.10 = (bf16[256,4096]{1,0:T(8,128)(2,1)}, bf16[256,4096]{1,0:T(8,128)(2,1)S(1)}, u32[]{:S(2)}) copy-start(bf16[256,4096]{1,0:T(8,128)(2,1)S(1)} %collective-permute-done.13.refs_9_) | copy-start | bytes 6291460
  287.9 90.0 %collective-permute-start.5 = (bf16[256,4096]{1,0:T(8,128)(2,1)}, bf16[256,4096]{1,0:T(8,128)(2,1)}, u32[]{:S(2)}, u32[]{:S(2)}) collective-permute-start(bf16[256,4096]{1,0:T(8,128)(2,1)} %get-tuple-element.27), channel_id=1, source_target_pairs={{0,4},{4,0},{1,5},{5,1},{2,6},{6,2},{3,7},{7,3}} | collective-permute-start | bytes 6291464 | tf_op jit(solution)/shard_map/ppermute | solution.py:272
  289.4 9.1 %copy-start.5 = (bf16[1536,768]{1,0:T(8,128)(2,1)}, bf16[1536,768]{1,0:T(8,128)(2,1)S(1)}, u32[]{:S(2)}) copy-start(bf16[1536,768]{1,0:T(8,128)(2,1)S(1)} %collective-permute-done.2.refs_3_) | copy-start | bytes 7077892
  289.4 133.4 %collective-permute-start.6 = (bf16[256,4096]{1,0:T(8,128)(2,1)}, bf16[256,4096]{1,0:T(8,128)(2,1)}, u32[]{:S(2)}, u32[]{:S(2)}) collective-permute-start(bf16[256,4096]{1,0:T(8,128)(2,1)} %get-tuple-element.28), channel_id=1, source_target_pairs={{0,4},{4,0},{1,5},{5,1},{2,6},{6,2},{3,7},{7,3}} | collective-permute-start | bytes 6291464 | tf_op jit(solution)/shard_map/ppermute | solution.py:272
  295.3 5.8 %copy-start.6 = (bf16[1536,768]{1,0:T(8,128)(2,1)}, bf16[1536,768]{1,0:T(8,128)(2,1)S(1)}, u32[]{:S(2)}) copy-start(bf16[1536,768]{1,0:T(8,128)(2,1)S(1)} %collective-permute-done.1.refs_2_) | copy-start | bytes 7077892
  295.3 171.6 %collective-permute-start.7 = (bf16[256,4096]{1,0:T(8,128)(2,1)}, bf16[256,4096]{1,0:T(8,128)(2,1)}, u32[]{:S(2)}, u32[]{:S(2)}) collective-permute-start(bf16[256,4096]{1,0:T(8,128)(2,1)} %get-tuple-element.29), channel_id=1, source_target_pairs={{0,4},{4,0},{1,5},{5,1},{2,6},{6,2},{3,7},{7,3}} | collective-permute-start | bytes 6291464 | tf_op jit(solution)/shard_map/ppermute | solution.py:272
  297.1 1.4 copy-start.7
  298.5 213.2 %collective-permute-start.18 = (bf16[256,4096]{1,0:T(8,128)(2,1)}, bf16[256,4096]{1,0:T(8,128)(2,1)S(1)}, u32[]{:S(2)}, u32[]{:S(2)}) collective-permute-start(bf16[256,4096]{1,0:T(8,128)(2,1)} %get-tuple-element.42), channel_id=1, source_target_pairs={{0,4},{1,5},{2,6},{3,7}} | collective-permute-start | bytes 6291464 | tf_op jit(solution)/shard_map/ppermute | solution.py:272
  301.1 1.6 copy-start.3
  333.7 133.2 %copy-start.8 = (bf16[256,4096]{1,0:T(8,128)(2,1)}, bf16[256,4096]{1,0:T(8,128)(2,1)S(1)}, u32[]{:S(2)}) copy-start(bf16[256,4096]{1,0:T(8,128)(2,1)S(1)} %collective-permute-done.4.refs_6_) | copy-start | bytes 6291460
  333.8 214.5 %collective-permute-start.15 = (bf16[256,512]{1,0:T(8,128)(2,1)S(1)}, bf16[256,512]{1,0:T(8,128)(2,1)S(1)}, u32[]{:S(2)}, u32[]{:S(2)}) collective-permute-start(bf16[256,512]{1,0:T(8,128)(2,1)S(1)} %get-tuple-element.38), channel_id=1, source_target_pairs={{0,4},{1,5},{2,6},{3,7}} | collective-permute-start | bytes 786440 | tf_op jit(solution)/shard_map/ppermute | solution.py:272
  377.9 170.3 %collective-permute-start.16 = (bf16[256,768]{1,0:T(8,128)(2,1)S(1)}, bf16[256,768]{1,0:T(8,128)(2,1)S(1)}, u32[]{:S(2)}, u32[]{:S(2)}) collective-permute-start(bf16[256,768]{1,0:T(8,128)(2,1)S(1)} %get-tuple-element.40), channel_id=1, source_target_pairs={{0,4},{1,5},{2,6},{3,7}} | collective-permute-start | bytes 1179656 | tf_op jit(solution)/shard_map/ppermute | solution.py:272
  422.8 125.3 %collective-permute-start.17 = (bf16[256,2048]{1,0:T(8,128)(2,1)S(1)}, bf16[256,2048]{1,0:T(8,128)(2,1)S(1)}, u32[]{:S(2)}, u32[]{:S(2)}) collective-permute-start(bf16[256,2048]{1,0:T(8,128)(2,1)S(1)} %get-tuple-element.41), channel_id=1, source_target_pairs={{0,4},{1,5},{2,6},{3,7}} | collective-permute-start | bytes 3145736 | tf_op jit(solution)/shard_map/ppermute | solution.py:272
  467.0 44.8 %copy-start.1 = (f32[256,4096]{1,0:T(8,128)S(1)}, f32[256,4096]{1,0:T(8,128)}, u32[]{:S(2)}) copy-start(f32[256,4096]{1,0:T(8,128)} %get-tuple-element.43.acc_ref) | copy-start | bytes 12582916
  499.3 51.1 %collective-permute-start.14 = (bf16[256,256]{1,0:T(8,128)(2,1)S(1)}, bf16[256,256]{1,0:T(8,128)(2,1)S(1)}, u32[]{:S(2)}, u32[]{:S(2)}) collective-permute-start(bf16[256,256]{1,0:T(8,128)(2,1)S(1)} %slice.6), channel_id=1, source_target_pairs={{0,4},{1,5},{2,6},{3,7}} | collective-permute-start | bytes 393224 | tf_op jit(solution)/shard_map/ppermute | solution.py:272
  511.8 36.4 %copy-start = (f32[256,4096]{1,0:T(8,128)S(1)}, f32[256,4096]{1,0:T(8,128)}, u32[]{:S(2)}) copy-start(f32[256,4096]{1,0:T(8,128)} %get-tuple-element.39.acc_ref) | copy-start | bytes 12582916

commit v10 on v7

--- a/solution.py
+++ b/solution.py
@@ -80,7 +80,7 @@
         ],
         scratch_shapes=[pltpu.VMEM((2, rows, rows), jnp.bfloat16), pltpu.SemaphoreType.DMA((2 * steps,))],
         input_output_aliases=aliases,
-        compiler_params=pltpu.CompilerParams(vmem_limit_bytes=50 << 20),
+        compiler_params=pltpu.CompilerParams(vmem_limit_bytes=60 << 20),
         cost_estimate=pl.CostEstimate(
             flops=2 * rows * rows * width, bytes_accessed=3 * rows * width * 2, transcendentals=0),
     )(*args)
@@ -116,7 +116,7 @@
 def finish(step, start, row, l_last, piece, acc, acc_start, x):
     width = piece.shape[1]
     return pl.pallas_call(
-        functools.partial(finish_kernel, step, start, row, min(width, 512), acc_start),
+        functools.partial(finish_kernel, step, start, row, 512 if width % 512 == 0 else 256, acc_start),
         in_specs=[pl.BlockSpec(memory_space=pltpu.HBM)] * 4,
         out_specs=pl.BlockSpec(memory_space=pltpu.HBM),
         out_shape=jax.ShapeDtypeStruct(x.shape, x.dtype),
@@ -247,7 +247,10 @@
 
         order = [(final, cols - first, first)]
         order += [(j, h * half, half) for j in range(final) for h in range(2)]
-        tail = [(0, half), (half, cols // 4), (half + cols // 4, cols // 8), (cols - 2 * first, first)]
+        tail, off = [], 0
+        for w in (half, cols // 4, 3 * first // 2, first, first // 2):
+            tail.append((off, w))
+            off += w
         order += [(final, off, w) for off, w in tail]
 
         got = {}

time: 551 us -> 553 us (level)
  waiting for transfers between devices: 436 us -> 430 us
    ppermute x15 -> x16, waiting for transfers between devices: 431 us -> 423 us  [send(): lax.ppermute(piece, 'row', down_row if i and j == final else swap_row)]
    ppermute x15 -> x16, starting transfers between devices: 26.7 us -> 29.8 us  [send(): lax.ppermute(piece, 'row', down_row if i and j == final else swap_row)]
  transfers between devices with their start and end apart: 18 -> 19, of which waited for: 10 -> 10; matrix products, arithmetic and copies ran while one was open for 0% -> 0% of each run, Pallas kernels for 14% -> 14%
where the time goes in v10:
time: 553 us; the launch traced here: 549 us
  waiting for transfers between devices  430 us (78%)
  Pallas kernels  79.3 us (14%)
  starting transfers between devices  31.5 us (6%)
  local copies, waits for them, and re-layouts  8.16 us (1%)
    ppermute x16, waiting for transfers between devices, send(): lax.ppermute(piece, 'row', down_row if i and j == final else swap_row)  423 us
    pallas_call x2, Pallas kernels, bulk(): pl.pallas_call(functools.partial(bulk_kernel, steps, len(aliases), int(ea...  62.5 us
    ppermute x16, starting transfers between devices, send(): lax.ppermute(piece, 'row', down_row if i and j == final else swap_row)  29.8 us
    pallas_call x2, Pallas kernels, cut_many(): pl.pallas_call(functools.partial(cut_many_kernel, places), in_specs=[pl.B...  15.5 us
  transfers between devices with their start and end apart: 19, of which 10 were waited for; matrix products, arithmetic and copies ran while one was open for 0% of the time, Pallas kernels for 14%

profile of v10, /device:TPU:0, one launch (start us, length us, event | category | flops | bytes accessed | tf_op | source)
XLA Modules:
  0.0 549.1 jit_solution(14400322955514619363)
XLA Ops:
  0.0 1.7 shard_map.31
  1.8 3.4 collective-permute-start.9
  5.1 13.7 %shard_map.28 = (bf16[256,4096]{1,0:T(8,128)(2,1)S(1)}, bf16[256,4096]{1,0:T(8,128)(2,1)S(1)}, bf16[256,4096]{1,0:T(8,128)(2,1)}, bf16[256,4096]{1,0:T(8,128)(2,...) custom-call(bf16[1536,8192]{1,0:T(8,128)(2,1)} %refs_4_.3), custom_call_target="tpu_custom_call" | custom-call | flops 22675456 | bytes 45350912 | tf_op jit(solution)/shard_map/pallas_call | solution.py:223
  18.8 1.0 copy-done.4
  19.9 2.0 collective-permute-start.10
  21.9 1.1 shard_map.29
  23.0 0.9 collective-permute-start.8
  24.0 167.2 %collective-permute-done.8.piece_ref = bf16[256,512]{1,0:T(8,128)(2,1)S(1)} collective-permute-done((bf16[256,512]{1,0:T(8,128)(2,1)S(1)}, bf16[256,512]{1,0:T(8,128)(2,1)S(1)}, u32[]{:S(2)}, u32[]{:S(2)}) %collective-permute-start.8) | collective-permute-done | bytes 262176 | tf_op jit(solution)/shard_map/ppermute | solution.py:260
  191.5 1.4 collective-permute-start.1
  192.9 1.5 collective-permute-start.12
  195.0 46.7 %collective-permute-done.12.refs_8_ = bf16[256,4096]{1,0:T(8,128)(2,1)S(1)} collective-permute-done((bf16[256,4096]{1,0:T(8,128)(2,1)}, bf16[256,4096]{1,0:T(8,128)(2,1)S(1)}, u32[]{:S(2)}, u32[]{:S(2)}) %collective-permute-start.12) | collective-permute-done | bytes 2097184 | tf_op jit(solution)/shard_map/ppermute | solution.py:260
  241.7 1.5 collective-permute-start.4
  243.2 43.4 %collective-permute-done.13.refs_9_ = bf16[256,4096]{1,0:T(8,128)(2,1)S(1)} collective-permute-done((bf16[256,4096]{1,0:T(8,128)(2,1)}, bf16[256,4096]{1,0:T(8,128)(2,1)S(1)}, u32[]{:S(2)}, u32[]{:S(2)}) %collective-permute-start.13) | collective-permute-done | bytes 2097184 | tf_op jit(solution)/shard_map/ppermute | solution.py:260
  286.6 1.5 collective-permute-start.5
  288.6 6.7 %collective-permute-done.1.refs_2_ = bf16[1536,768]{1,0:T(8,128)(2,1)S(1)} collective-permute-done((bf16[1536,768]{1,0:T(8,128)(2,1)S(1)}, bf16[1536,768]{1,0:T(8,128)(2,1)S(1)}, u32[]{:S(2)}, u32[]{:S(2)}) %collective-permute-start.1) | collective-permute-done | bytes 2359328 | tf_op jit(solution)/shard_map/ppermute | solution.py:272
  295.3 1.7 collective-permute-start.7
  297.8 1.4 copy-done.8
  299.3 2.6 collective-permute-start.18
  301.9 31.1 %shard_map.32 = (bf16[1536,8192]{1,0:T(8,128)(2,1)}, f32[256,4096]{1,0:T(8,128)}, bf16[256,256]{1,0:T(8,128)(2,1)}) custom-call(bf16[1536,768]{1,0:T(8,128)(2,1)} %refs_0_.3, bf16[1536,768]{1,0:T(8,128)(2,1)} %copy-done.8, bf16[1536,768]{1,0:T(8,128)(2,1)} %copy-done.7, bf16[1536,768]{1,0:T(8,128)(2,1)} %copy-done.6, bf16[1536,8192]{1,0:T(8,128)(2,1)} %refs_4_.3, ...), custom_call_target="tpu_custom_call" | custom-call | flops 19327352832 | bytes 37748736 | tf_op jit(solution)/shard_map/pallas_call | solution.py:71
  332.9 2.1 collective-permute-start.15
  335.1 41.5 %collective-permute-done.5.refs_7_ = bf16[256,4096]{1,0:T(8,128)(2,1)} collective-permute-done((bf16[256,4096]{1,0:T(8,128)(2,1)}, bf16[256,4096]{1,0:T(8,128)(2,1)}, u32[]{:S(2)}, u32[]{:S(2)}) %collective-permute-start.5) | collective-permute-done | bytes 2097184 | tf_op jit(solution)/shard_map/ppermute | solution.py:260
  376.6 3.4 collective-permute-start.16
  380.0 41.5 %collective-permute-done.6.refs_8_ = bf16[256,4096]{1,0:T(8,128)(2,1)} collective-permute-done((bf16[256,4096]{1,0:T(8,128)(2,1)}, bf16[256,4096]{1,0:T(8,128)(2,1)}, u32[]{:S(2)}, u32[]{:S(2)}) %collective-permute-start.6) | collective-permute-done | bytes 2097184 | tf_op jit(solution)/shard_map/ppermute | solution.py:260
  421.5 3.5 collective-permute-start.17
  425.0 40.6 %collective-permute-done.7.refs_9_ = bf16[256,4096]{1,0:T(8,128)(2,1)} collective-permute-done((bf16[256,4096]{1,0:T(8,128)(2,1)}, bf16[256,4096]{1,0:T(8,128)(2,1)}, u32[]{:S(2)}, u32[]{:S(2)}) %collective-permute-start.7) | collective-permute-done | bytes 2097184 | tf_op jit(solution)/shard_map/ppermute | solution.py:260
  465.6 31.4 %shard_map.33 = (bf16[1536,8192]{1,0:T(8,128)(2,1)}, f32[256,4096]{1,0:T(8,128)}, bf16[256,256]{1,0:T(8,128)(2,1)}) custom-call(bf16[1536,768]{1,0:T(8,128)(2,1)} %refs_0_.3, bf16[1536,768]{1,0:T(8,128)(2,1)} %copy-done.8, bf16[1536,768]{1,0:T(8,128)(2,1)} %copy-done.7, bf16[1536,768]{1,0:T(8,128)(2,1)} %copy-done.6, ...), custom_call_target="tpu_custom_call", output_to_operand_aliasing={{0}: (11, {})} | custom-call | flops 19327352832 | bytes 37748736 | tf_op jit(solution)/shard_map/pallas_call | solution.py:71
  498.0 4.5 collective-permute-start.14
  502.5 1.0 slice.7.acc_ref
  503.5 7.0 %collective-permute-done.18.b_ref = bf16[256,4096]{1,0:T(8,128)(2,1)S(1)} collective-permute-done((bf16[256,4096]{1,0:T(8,128)(2,1)}, bf16[256,4096]{1,0:T(8,128)(2,1)S(1)}, u32[]{:S(2)}, u32[]{:S(2)}) %collective-permute-start.18) | collective-permute-done | bytes 2097184 | tf_op jit(solution)/shard_map/ppermute | solution.py:260
  510.5 2.2 copy-done.1
  513.6 33.4 %collective-permute-done.17.b_ref = bf16[256,2048]{1,0:T(8,128)(2,1)S(1)} collective-permute-done((bf16[256,2048]{1,0:T(8,128)(2,1)}, bf16[256,2048]{1,0:T(8,128)(2,1)S(1)}, u32[]{:S(2)}, u32[]{:S(2)}) %collective-permute-start.17) | collective-permute-done | bytes 1048608 | tf_op jit(solution)/shard_map/ppermute | solution.py:260
  547.2 1.9 collective-permute-done.14.b_ref
  (47 shorter events, 4.2 us)
Async XLA Ops:
  1.8 189.7 %collective-permute-start.9 = (bf16[256,4096]{1,0:T(8,128)(2,1)S(1)}, bf16[256,4096]{1,0:T(8,128)(2,1)S(1)}, u32[]{:S(2)}, u32[]{:S(2)}) collective-permute-start(bf16[256,4096]{1,0:T(8,128)(2,1)S(1)} %shard_map.31), channel_id=1, source_target_pairs={{0,4},{4,0},{1,5},{5,1},{2,6},{6,2},{3,7},{7,3}} | collective-permute-start | bytes 6291464 | tf_op jit(solution)/shard_map/ppermute | solution.py:260
  18.8 1.0 copy-start.4
  19.9 173.1 %collective-permute-start.3 = (bf16[256,4096]{1,0:T(8,128)(2,1)S(1)}, bf16[256,4096]{1,0:T(8,128)(2,1)S(1)}, u32[]{:S(2)}, u32[]{:S(2)}) collective-permute-start(bf16[256,4096]{1,0:T(8,128)(2,1)S(1)} %get-tuple-element.25), channel_id=1, source_target_pairs={{0,4},{4,0},{1,5},{5,1},{2,6},{6,2},{3,7},{7,3}} | collective-permute-start | bytes 6291464 | tf_op jit(solution)/shard_map/ppermute | solution.py:260
  19.9 174.6 %collective-permute-start.10 = (bf16[256,4096]{1,0:T(8,128)(2,1)S(1)}, bf16[256,4096]{1,0:T(8,128)(2,1)S(1)}, u32[]{:S(2)}, u32[]{:S(2)}) collective-permute-start(bf16[256,4096]{1,0:T(8,128)(2,1)S(1)} %get-tuple-element.30), channel_id=1, source_target_pairs={{0,4},{4,0},{1,5},{5,1},{2,6},{6,2},{3,7},{7,3}} | collective-permute-start | bytes 6291464 | tf_op jit(solution)/shard_map/ppermute | solution.py:260
  21.9 169.3 %copy-start.5 = (bf16[1536,768]{1,0:T(8,128)(2,1)S(1)}, bf16[1536,768]{1,0:T(8,128)(2,1)}, u32[]{:S(2)}) copy-start(bf16[1536,768]{1,0:T(8,128)(2,1)} %refs_0_.3) | copy-start | bytes 7077892
  21.9 173.1 %collective-permute-start.11 = (bf16[256,4096]{1,0:T(8,128)(2,1)}, bf16[256,4096]{1,0:T(8,128)(2,1)}, u32[]{:S(2)}, u32[]{:S(2)}) collective-permute-start(bf16[256,4096]{1,0:T(8,128)(2,1)} %get-tuple-element.31), channel_id=1, source_target_pairs={{0,4},{4,0},{1,5},{5,1},{2,6},{6,2},{3,7},{7,3}} | collective-permute-start | bytes 6291464 | tf_op jit(solution)/shard_map/ppermute | solution.py:260
  23.0 168.1 %collective-permute-start.8 = (bf16[256,512]{1,0:T(8,128)(2,1)S(1)}, bf16[256,512]{1,0:T(8,128)(2,1)S(1)}, u32[]{:S(2)}, u32[]{:S(2)}) collective-permute-start(bf16[256,512]{1,0:T(8,128)(2,1)S(1)} %shard_map.29), channel_id=1, source_target_pairs={{0,4},{4,0},{1,5},{5,1},{2,6},{6,2},{3,7},{7,3}} | collective-permute-start | bytes 786440 | tf_op jit(solution)/shard_map/ppermute | solution.py:260
  191.2 96.9 %collective-permute-start.2 = (bf16[1536,768]{1,0:T(8,128)(2,1)S(1)}, bf16[1536,768]{1,0:T(8,128)(2,1)S(1)}, u32[]{:S(2)}, u32[]{:S(2)}) collective-permute-start(bf16[1536,768]{1,0:T(8,128)(2,1)S(1)} %copy-done.5), channel_id=1, source_target_pairs={{0,3},{1,2},{2,1},{3,0},{4,7},{5,6},{6,5},{7,4}} | collective-permute-start | bytes 7077896 | tf_op jit(solution)/shard_map/ppermute | solution.py:272
  191.5 106.3 %copy-start.10 = (bf16[256,4096]{1,0:T(8,128)(2,1)}, bf16[256,4096]{1,0:T(8,128)(2,1)S(1)}, u32[]{:S(2)}) copy-start(bf16[256,4096]{1,0:T(8,128)(2,1)S(1)} %collective-permute-done.9.refs_5_) | copy-start | bytes 6291460
  191.5 103.8 %collective-permute-start.1 = (bf16[1536,768]{1,0:T(8,128)(2,1)S(1)}, bf16[1536,768]{1,0:T(8,128)(2,1)S(1)}, u32[]{:S(2)}, u32[]{:S(2)}) collective-permute-start(bf16[1536,768]{1,0:T(8,128)(2,1)S(1)} %copy-done.5), channel_id=1, source_target_pairs={{0,2},{1,3},{2,0},{3,1},{4,6},{5,7},{6,4},{7,5}} | collective-permute-start | bytes 7077896 | tf_op jit(solution)/shard_map/ppermute | solution.py:272
  192.9 104.9 %copy-start.9 = (bf16[256,4096]{1,0:T(8,128)(2,1)}, bf16[256,4096]{1,0:T(8,128)(2,1)S(1)}, u32[]{:S(2)}) copy-start(bf16[256,4096]{1,0:T(8,128)(2,1)S(1)} %collective-permute-done.3.refs_5_) | copy-start | bytes 6291460
  192.9 48.7 %collective-permute-start.12 = (bf16[256,4096]{1,0:T(8,128)(2,1)}, bf16[256,4096]{1,0:T(8,128)(2,1)S(1)}, u32[]{:S(2)}, u32[]{:S(2)}) collective-permute-start(bf16[256,4096]{1,0:T(8,128)(2,1)} %get-tuple-element.32), channel_id=1, source_target_pairs={{0,4},{4,0},{1,5},{5,1},{2,6},{6,2},{3,7},{7,3}} | collective-permute-start | bytes 6291464 | tf_op jit(solution)/shard_map/ppermute | solution.py:260
  194.5 103.3 %copy-start.11 = (bf16[256,4096]{1,0:T(8,128)(2,1)}, bf16[256,4096]{1,0:T(8,128)(2,1)S(1)}, u32[]{:S(2)}) copy-start(bf16[256,4096]{1,0:T(8,128)(2,1)S(1)} %collective-permute-done.10.refs_6_) | copy-start | bytes 6291460
  194.5 92.1 %collective-permute-start.13 = (bf16[256,4096]{1,0:T(8,128)(2,1)}, bf16[256,4096]{1,0:T(8,128)(2,1)S(1)}, u32[]{:S(2)}, u32[]{:S(2)}) collective-permute-start(bf16[256,4096]{1,0:T(8,128)(2,1)} %get-tuple-element.33), channel_id=1, source_target_pairs={{0,4},{4,0},{1,5},{5,1},{2,6},{6,2},{3,7},{7,3}} | collective-permute-start | bytes 6291464 | tf_op jit(solution)/shard_map/ppermute | solution.py:260
  195.0 102.8 %collective-permute-start = (bf16[1536,768]{1,0:T(8,128)(2,1)S(1)}, bf16[1536,768]{1,0:T(8,128)(2,1)S(1)}, u32[]{:S(2)}, u32[]{:S(2)}) collective-permute-start(bf16[1536,768]{1,0:T(8,128)(2,1)S(1)} %copy-done.5), channel_id=1, source_target_pairs={{0,1},{1,0},{2,3},{3,2},{4,5},{5,4},{6,7},{7,6}} | collective-permute-start | bytes 7077896 | tf_op jit(solution)/shard_map/ppermute | solution.py:272
  241.7 56.2 %copy-start.12 = (bf16[256,4096]{1,0:T(8,128)(2,1)}, bf16[256,4096]{1,0:T(8,128)(2,1)S(1)}, u32[]{:S(2)}) copy-start(bf16[256,4096]{1,0:T(8,128)(2,1)S(1)} %collective-permute-done.12.refs_8_) | copy-start | bytes 6291460
  241.7 91.3 %collective-permute-start.4 = (bf16[256,4096]{1,0:T(8,128)(2,1)}, bf16[256,4096]{1,0:T(8,128)(2,1)}, u32[]{:S(2)}, u32[]{:S(2)}) collective-permute-start(bf16[256,4096]{1,0:T(8,128)(2,1)} %get-tuple-element.26), channel_id=1, source_target_pairs={{0,4},{4,0},{1,5},{5,1},{2,6},{6,2},{3,7},{7,3}} | collective-permute-start | bytes 6291464 | tf_op jit(solution)/shard_map/ppermute | solution.py:260
  286.6 11.2 %copy-start.13 = (bf16[256,4096]{1,0:T(8,128)(2,1)}, bf16[256,4096]{1,0:T(8,128)(2,1)S(1)}, u32[]{:S(2)}) copy-start(bf16[256,4096]{1,0:T(8,128)(2,1)S(1)} %collective-permute-done.13.refs_9_) | copy-start | bytes 6291460
  286.6 90.0 %collective-permute-start.5 = (bf16[256,4096]{1,0:T(8,128)(2,1)}, bf16[256,4096]{1,0:T(8,128)(2,1)}, u32[]{:S(2)}, u32[]{:S(2)}) collective-permute-start(bf16[256,4096]{1,0:T(8,128)(2,1)} %get-tuple-element.27), channel_id=1, source_target_pairs={{0,4},{4,0},{1,5},{5,1},{2,6},{6,2},{3,7},{7,3}} | collective-permute-start | bytes 6291464 | tf_op jit(solution)/shard_map/ppermute | solution.py:260
  288.1 9.7 %copy-start.6 = (bf16[1536,768]{1,0:T(8,128)(2,1)}, bf16[1536,768]{1,0:T(8,128)(2,1)S(1)}, u32[]{:S(2)}) copy-start(bf16[1536,768]{1,0:T(8,128)(2,1)S(1)} %collective-permute-done.2.refs_3_) | copy-start | bytes 7077892
  288.1 133.4 %collective-permute-start.6 = (bf16[256,4096]{1,0:T(8,128)(2,1)}, bf16[256,4096]{1,0:T(8,128)(2,1)}, u32[]{:S(2)}, u32[]{:S(2)}) collective-permute-start(bf16[256,4096]{1,0:T(8,128)(2,1)} %get-tuple-element.28), channel_id=1, source_target_pairs={{0,4},{4,0},{1,5},{5,1},{2,6},{6,2},{3,7},{7,3}} | collective-permute-start | bytes 6291464 | tf_op jit(solution)/shard_map/ppermute | solution.py:260
  295.3 2.5 copy-start.7
  295.3 170.3 %collective-permute-start.7 = (bf16[256,4096]{1,0:T(8,128)(2,1)}, bf16[256,4096]{1,0:T(8,128)(2,1)}, u32[]{:S(2)}, u32[]{:S(2)}) collective-permute-start(bf16[256,4096]{1,0:T(8,128)(2,1)} %get-tuple-element.29), channel_id=1, source_target_pairs={{0,4},{4,0},{1,5},{5,1},{2,6},{6,2},{3,7},{7,3}} | collective-permute-start | bytes 6291464 | tf_op jit(solution)/shard_map/ppermute | solution.py:260
  297.8 1.5 copy-start.8
  299.3 211.2 %collective-permute-start.18 = (bf16[256,4096]{1,0:T(8,128)(2,1)}, bf16[256,4096]{1,0:T(8,128)(2,1)S(1)}, u32[]{:S(2)}, u32[]{:S(2)}) collective-permute-start(bf16[256,4096]{1,0:T(8,128)(2,1)} %get-tuple-element.42), channel_id=1, source_target_pairs={{0,4},{1,5},{2,6},{3,7}} | collective-permute-start | bytes 6291464 | tf_op jit(solution)/shard_map/ppermute | solution.py:260
  332.9 214.1 %collective-permute-start.15 = (bf16[256,512]{1,0:T(8,128)(2,1)S(1)}, bf16[256,512]{1,0:T(8,128)(2,1)S(1)}, u32[]{:S(2)}, u32[]{:S(2)}) collective-permute-start(bf16[256,512]{1,0:T(8,128)(2,1)S(1)} %get-tuple-element.38), channel_id=1, source_target_pairs={{0,4},{1,5},{2,6},{3,7}} | collective-permute-start | bytes 786440 | tf_op jit(solution)/shard_map/ppermute | solution.py:260
  376.6 170.4 %collective-permute-start.16 = (bf16[256,768]{1,0:T(8,128)(2,1)}, bf16[256,768]{1,0:T(8,128)(2,1)S(1)}, u32[]{:S(2)}, u32[]{:S(2)}) collective-permute-start(bf16[256,768]{1,0:T(8,128)(2,1)} %get-tuple-element.40), channel_id=1, source_target_pairs={{0,4},{1,5},{2,6},{3,7}} | collective-permute-start | bytes 1179656 | tf_op jit(solution)/shard_map/ppermute | solution.py:260
  421.5 125.4 %collective-permute-start.17 = (bf16[256,2048]{1,0:T(8,128)(2,1)}, bf16[256,2048]{1,0:T(8,128)(2,1)S(1)}, u32[]{:S(2)}, u32[]{:S(2)}) collective-permute-start(bf16[256,2048]{1,0:T(8,128)(2,1)} %copy-done.4), channel_id=1, source_target_pairs={{0,4},{1,5},{2,6},{3,7}} | collective-permute-start | bytes 3145736 | tf_op jit(solution)/shard_map/ppermute | solution.py:260
  498.0 51.0 %collective-permute-start.14 = (bf16[256,256]{1,0:T(8,128)(2,1)S(1)}, bf16[256,256]{1,0:T(8,128)(2,1)S(1)}, u32[]{:S(2)}, u32[]{:S(2)}) collective-permute-start(bf16[256,256]{1,0:T(8,128)(2,1)S(1)} %slice.6), channel_id=1, source_target_pairs={{0,4},{1,5},{2,6},{3,7}} | collective-permute-start | bytes 393224 | tf_op jit(solution)/shard_map/ppermute | solution.py:260
  510.5 2.2 copy-start.1
  512.6 0.9 copy-start.2
  513.5 33.4 %copy-start = (f32[256,4096]{1,0:T(8,128)S(1)}, f32[256,4096]{1,0:T(8,128)}, u32[]{:S(2)}) copy-start(f32[256,4096]{1,0:T(8,128)} %get-tuple-element.39.acc_ref) | copy-start | bytes 12582916
  (1 other events, 0.7 us)
